TPU v7x, 32 devices: a whole 2x2x4 slice. The times are simulated.
32 devices in a mesh: dp: 8 (over z, x), tensor: 4 (over y, core).
Axes of the slice: x: 2, y: 2, z: 4, core: 2. Of those that a mesh axis runs over, the one named last changes fastest.
Arguments:
- hidden_in: float32 [1024, 1536], P('dp'), may hold values from -6 to 6
- cotangent: float32 [1024, 1536], P('dp'), may hold values from -6 to 6
- segment_ids: int32 [8, 128], P('dp'), may hold values from 0 to 4, as said below
- positions: int32 [8, 128], P('dp'), may hold values from 0 to 2174, as said below
- w_query: bfloat16 [2, 1536, 1536], P(None, None, 'tensor'), may hold values from -0.15625 to 0.15625
- w_key: bfloat16 [2, 1536, 768], P(None, None, 'tensor'), may hold values from -0.15625 to 0.15625
- w_value: bfloat16 [2, 1536, 768], P(None, None, 'tensor'), may hold values from -0.15625 to 0.15625
- w_output: bfloat16 [2, 1536, 1536], P(None, 'tensor'), may hold values from -0.625 to 0.625
- w_gate: bfloat16 [2, 1536, 4096], P(None, None, 'tensor'), may hold values from -0.15625 to 0.15625
- w_up: bfloat16 [2, 1536, 4096], P(None, None, 'tensor'), may hold values from -0.15625 to 0.15625
- w_down: bfloat16 [2, 4096, 1536], P(None, 'tensor'), may hold values from -0.09375 to 0.09375
- attn_gain: float32 [2, 1536], replicated, may hold values from 0.1 to 1.9
- mlp_gain: float32 [2, 1536], replicated, may hold values from 0.1 to 1.9
Outputs:
- hidden_out: float32 [1024, 1536], P('dp')
- grad_input: float32 [1024, 1536], P('dp')
- grad_query: float32 [2, 1536, 1536], P(None, 'dp', 'tensor')
- grad_key: float32 [2, 1536, 768], P(None, 'dp', 'tensor')
- grad_value: float32 [2, 1536, 768], P(None, 'dp', 'tensor')
- grad_output: float32 [2, 1536, 1536], P(None, 'tensor', 'dp')
- grad_gate: float32 [2, 1536, 4096], P(None, 'dp', 'tensor')
- grad_up: float32 [2, 1536, 4096], P(None, 'dp', 'tensor')
- grad_down: float32 [2, 4096, 1536], P(None, 'tensor', 'dp')
- grad_attn_gain: float32 [2, 1536], P(None, 'dp')
- grad_mlp_gain: float32 [2, 1536], P(None, 'dp')
Inputs may be any that keep to these rules, and one draw needn't show every extreme that they name: `segment_ids`: segment ids start at 0 in every packed sequence, never fall along it, and every packed sequence holds exactly 5 documents. Within one document, positions rise by one from token to token; the first document of every packed sequence starts at 0 and the last one ends at 2174.
All inputs are finite; a program needn't handle non-finite values.
Results may differ from a plain program's by a relative error of at most 0.025.
Values sent between devices are 32-bit elements; how exact they have to be, the bound alone decides.
A program may use at most 256 MiB of HBM per device.

v0:
```python
import jax
import jax.numpy as jnp
from jax import lax
from jax.sharding import PartitionSpec as P

HD = 96
LAYERS = 2


epsilon = 1e-05
rope_base = 100000.0
masked_score = -1e30


def inverse_rms(values):
    return lax.rsqrt(jnp.mean(values * values, axis=-1, keepdims=True) + epsilon)


def rotary_tables(places):
    half_dim = HD // 2
    frequencies = rope_base ** (-(jnp.arange(half_dim).astype(jnp.float32) * 2.0 / HD))
    angles = places.astype(jnp.float32)[:, None] * frequencies[None, :]
    return (jnp.cos(angles), jnp.sin(angles))


def rotate(tensor, cosine, sine, direction):
    half_dim = tensor.shape[-1] // 2
    first_half = tensor[..., :half_dim]
    second_half = tensor[..., half_dim:]
    cos_part = cosine[:, None, :]
    sin_part = sine[:, None, :]
    return jnp.concatenate(
        [
            first_half * cos_part - direction * second_half * sin_part,
            second_half * cos_part + direction * first_half * sin_part,
        ],
        axis=-1,
    )


def attention_scores(queries, key_rows, allowed):
    scores = jnp.einsum(
        "qkgd,skd->kgqs", queries, key_rows, preferred_element_type=jnp.float32
    ) * HD ** (-0.5)
    return jnp.where(allowed[None, None], scores, masked_score)


def attention_forward(queries, key_rows, value_rows, allowed):
    scores = attention_scores(queries, key_rows, allowed)
    row_max = jnp.max(scores, axis=-1, keepdims=True)
    exponent = jnp.exp(scores - row_max)
    row_total = jnp.sum(exponent, axis=-1, keepdims=True)
    probabilities = (exponent / row_total).astype(jnp.bfloat16)
    logsum = row_max + jnp.log(row_total)
    mixed_rows = jnp.einsum(
        "kgqs,skd->qkgd", probabilities, value_rows, preferred_element_type=jnp.float32
    )
    return (mixed_rows.astype(jnp.bfloat16), logsum)


def attention_backward(queries, key_rows, value_rows, mixed_rows, logsum, grad_mixed, allowed):
    scores = attention_scores(queries, key_rows, allowed)
    again_probs = jnp.exp(scores - logsum)
    probs_low = again_probs.astype(jnp.bfloat16)
    grad_values = jnp.einsum(
        "kgqs,qkgd->skd", probs_low, grad_mixed, preferred_element_type=jnp.float32
    )
    grad_probs = jnp.einsum(
        "qkgd,skd->kgqs", grad_mixed, value_rows, preferred_element_type=jnp.float32
    )
    row_dot = jnp.sum(grad_mixed.astype(jnp.float32) * mixed_rows.astype(jnp.float32), axis=-1)
    row_dot = jnp.transpose(row_dot, (1, 2, 0))[..., None]
    grad_scores = (again_probs * (grad_probs - row_dot) * HD ** (-0.5)).astype(jnp.bfloat16)
    grad_queries = jnp.einsum(
        "kgqs,skd->qkgd", grad_scores, key_rows, preferred_element_type=jnp.float32
    )
    grad_keys = jnp.einsum(
        "kgqs,qkgd->skd", grad_scores, queries, preferred_element_type=jnp.float32
    )
    return (grad_queries, grad_keys, grad_values)


def norm_backward(grad_normed, values, inverse, gain_row):
    normalized = values * inverse
    grad_gain = jnp.sum(grad_normed * normalized, axis=0)
    scaled = grad_normed * gain_row
    grad_values = inverse * (
        scaled - normalized * jnp.mean(scaled * normalized, axis=-1, keepdims=True)
    )
    return (grad_gain, grad_values)


def layer_forward(hidden, allowed, cosine, sine, weights):
    w_query, w_key, w_value, w_output, w_gate, w_up, w_down, attn_gain, mlp_gain = weights
    length = hidden.shape[0]
    query_heads = w_query.shape[1] // HD
    kv_heads = w_key.shape[1] // HD
    group_size = query_heads // kv_heads
    inverse_one = inverse_rms(hidden)
    normed = (hidden * inverse_one * attn_gain).astype(jnp.bfloat16)
    queries = jnp.dot(normed, w_query, preferred_element_type=jnp.float32).reshape(
        length, query_heads, HD
    )
    queries = (
        rotate(queries, cosine, sine, 1.0)
        .astype(jnp.bfloat16)
        .reshape(length, kv_heads, group_size, HD)
    )
    key_rows = jnp.dot(normed, w_key, preferred_element_type=jnp.float32).reshape(
        length, kv_heads, HD
    )
    key_rows = rotate(key_rows, cosine, sine, 1.0).astype(jnp.bfloat16)
    value_rows = (
        jnp.dot(normed, w_value, preferred_element_type=jnp.float32)
        .astype(jnp.bfloat16)
        .reshape(length, kv_heads, HD)
    )
    mixed_rows, logsum = attention_forward(queries, key_rows, value_rows, allowed)
    mixed_flat = mixed_rows.reshape(length, query_heads * HD)
    attn_part = jnp.dot(mixed_flat, w_output, preferred_element_type=jnp.float32)
    attended = hidden + lax.psum(attn_part, "tensor")
    inverse_two = inverse_rms(attended)
    normed_two = (attended * inverse_two * mlp_gain).astype(jnp.bfloat16)
    gate_pre = jnp.dot(normed_two, w_gate, preferred_element_type=jnp.float32)
    up_pre = jnp.dot(normed_two, w_up, preferred_element_type=jnp.float32)
    activated = (jax.nn.silu(gate_pre) * up_pre).astype(jnp.bfloat16)
    mlp_part = jnp.dot(activated, w_down, preferred_element_type=jnp.float32)
    output = attended + lax.psum(mlp_part, "tensor")
    kept_state = (
        hidden,
        inverse_one,
        normed,
        queries,
        key_rows,
        value_rows,
        mixed_rows,
        logsum,
        attended,
        inverse_two,
        normed_two,
        gate_pre,
        up_pre,
        activated,
    )
    return (output, kept_state)


def layer_backward(upstream, kept_state, allowed, cosine, sine, weights):
    w_query, w_key, w_value, w_output, w_gate, w_up, w_down, attn_gain, mlp_gain = weights
    (
        hidden,
        inverse_one,
        normed,
        queries,
        key_rows,
        value_rows,
        mixed_rows,
        logsum,
        attended,
        inverse_two,
        normed_two,
        gate_pre,
        up_pre,
        activated,
    ) = kept_state
    length = hidden.shape[0]
    query_heads = w_query.shape[1] // HD
    kv_heads = w_key.shape[1] // HD
    group_size = query_heads // kv_heads
    g_low = upstream.astype(jnp.bfloat16)
    grad_down = jnp.dot(activated.T, g_low, preferred_element_type=jnp.float32)
    grad_act = jnp.dot(g_low, w_down.T, preferred_element_type=jnp.float32)
    sigmoid_gate = jax.nn.sigmoid(gate_pre)
    grad_gate_low = (
        grad_act * up_pre * sigmoid_gate * (1.0 + gate_pre * (1.0 - sigmoid_gate))
    ).astype(jnp.bfloat16)
    grad_up_low = (grad_act * gate_pre * sigmoid_gate).astype(jnp.bfloat16)
    grad_gate = jnp.dot(normed_two.T, grad_gate_low, preferred_element_type=jnp.float32)
    grad_up = jnp.dot(normed_two.T, grad_up_low, preferred_element_type=jnp.float32)
    mlp_input_part = jnp.dot(grad_gate_low, w_gate.T, preferred_element_type=jnp.float32) + jnp.dot(
        grad_up_low, w_up.T, preferred_element_type=jnp.float32
    )
    grad_normed_two = lax.psum(mlp_input_part, "tensor")
    grad_mlp_gain, grad_norm_two = norm_backward(grad_normed_two, attended, inverse_two, mlp_gain)
    grad_attended = upstream + grad_norm_two
    grad_att_low = grad_attended.astype(jnp.bfloat16)
    mixed_flat = mixed_rows.reshape(length, query_heads * HD)
    grad_output = jnp.dot(mixed_flat.T, grad_att_low, preferred_element_type=jnp.float32)
    grad_mixed = jnp.dot(grad_att_low, w_output.T, preferred_element_type=jnp.float32).astype(
        jnp.bfloat16
    )
    grad_mixed = grad_mixed.reshape(length, kv_heads, group_size, HD)
    grad_queries, grad_keys, grad_values = attention_backward(
        queries, key_rows, value_rows, mixed_rows, logsum, grad_mixed, allowed
    )
    grad_query_low = (
        rotate(grad_queries.reshape(length, query_heads, HD), cosine, sine, -1.0)
        .astype(jnp.bfloat16)
        .reshape(length, query_heads * HD)
    )
    grad_key_low = (
        rotate(grad_keys, cosine, sine, -1.0).astype(jnp.bfloat16).reshape(length, kv_heads * HD)
    )
    grad_value_low = grad_values.astype(jnp.bfloat16).reshape(length, kv_heads * HD)
    grad_query = jnp.dot(normed.T, grad_query_low, preferred_element_type=jnp.float32)
    grad_key = jnp.dot(normed.T, grad_key_low, preferred_element_type=jnp.float32)
    grad_value = jnp.dot(normed.T, grad_value_low, preferred_element_type=jnp.float32)
    attn_input_part = (
        jnp.dot(grad_query_low, w_query.T, preferred_element_type=jnp.float32)
        + jnp.dot(grad_key_low, w_key.T, preferred_element_type=jnp.float32)
        + jnp.dot(grad_value_low, w_value.T, preferred_element_type=jnp.float32)
    )
    grad_normed = lax.psum(attn_input_part, "tensor")
    grad_attn_gain, grad_norm_one = norm_backward(grad_normed, hidden, inverse_one, attn_gain)
    grad_hidden = grad_attended + grad_norm_one
    return (
        grad_hidden,
        (
            grad_query,
            grad_key,
            grad_value,
            grad_output,
            grad_gate,
            grad_up,
            grad_down,
            grad_attn_gain,
            grad_mlp_gain,
        ),
    )


def shards(
    hidden_in,
    cotangent,
    segment_ids,
    positions,
    w_query,
    w_key,
    w_value,
    w_output,
    w_gate,
    w_up,
    w_down,
    attn_gain,
    mlp_gain,
):
    weights_all = (w_query, w_key, w_value, w_output, w_gate, w_up, w_down, attn_gain, mlp_gain)
    length = hidden_in.shape[0]
    cosine, sine = rotary_tables(positions[0])
    segments = segment_ids[0]
    token_order = jnp.arange(length)
    allowed = (segments[:, None] == segments[None, :]) & (
        token_order[None, :] <= token_order[:, None]
    )
    layer_weights = [
        tuple((weight[which_layer] for weight in weights_all)) for which_layer in range(LAYERS)
    ]
    inputs_list = []
    kept_list = []
    hidden = hidden_in
    for which_layer in range(LAYERS):
        inputs_list.append(hidden)
        hidden, kept_state = layer_forward(
            hidden, allowed, cosine, sine, layer_weights[which_layer]
        )
        kept_list.append(kept_state)
    upstream = cotangent
    grad_layers = [None] * LAYERS
    for which_layer in reversed(range(LAYERS)):
        kept_state = kept_list[which_layer]
        upstream, layer_grads = layer_backward(
            upstream, kept_state, allowed, cosine, sine, layer_weights[which_layer]
        )
        grad_layers[which_layer] = layer_grads
    stacked = tuple(
        (
            jnp.stack([grad_layers[which_layer][member] for which_layer in range(LAYERS)])
            for member in range(9)
        )
    )
    stacked = (
        lax.psum_scatter(stacked[0], "dp", scatter_dimension=1, tiled=True),
        lax.psum_scatter(stacked[1], "dp", scatter_dimension=1, tiled=True),
        lax.psum_scatter(stacked[2], "dp", scatter_dimension=1, tiled=True),
        lax.psum_scatter(stacked[3], "dp", scatter_dimension=2, tiled=True),
        lax.psum_scatter(stacked[4], "dp", scatter_dimension=1, tiled=True),
        lax.psum_scatter(stacked[5], "dp", scatter_dimension=1, tiled=True),
        lax.psum_scatter(stacked[6], "dp", scatter_dimension=2, tiled=True),
        lax.psum_scatter(stacked[7], "dp", scatter_dimension=1, tiled=True),
        lax.psum_scatter(stacked[8], "dp", scatter_dimension=1, tiled=True),
    )
    return (
        hidden,
        upstream,
        stacked[0],
        stacked[1],
        stacked[2],
        stacked[3],
        stacked[4],
        stacked[5],
        stacked[6],
        stacked[7],
        stacked[8],
    )


def solution(mesh):
    return jax.shard_map(
        shards,
        mesh=mesh,
        in_specs=(
            P("dp", None),
            P("dp", None),
            P("dp", None),
            P("dp", None),
            P(None, None, "tensor"),
            P(None, None, "tensor"),
            P(None, None, "tensor"),
            P(None, "tensor", None),
            P(None, None, "tensor"),
            P(None, None, "tensor"),
            P(None, "tensor", None),
            P(),
            P(),
        ),
        out_specs=(
            P("dp", None),
            P("dp", None),
            P(None, "dp", "tensor"),
            P(None, "dp", "tensor"),
            P(None, "dp", "tensor"),
            P(None, "tensor", "dp"),
            P(None, "dp", "tensor"),
            P(None, "dp", "tensor"),
            P(None, "tensor", "dp"),
            P(None, "dp"),
            P(None, "dp"),
        ),
        check_vma=False,
    )
```

profile of v0, /device:TPU:0, one launch (start us, length us, event | category | flops | bytes accessed | tf_op | source)
XLA Modules:
  0.0 1677.9 jit_solution(9042979256004189845)
XLA Ops:
  9.4 3.4 slice_bitcast_fusion
  12.7 1.6 copy.40
  20.2 37.2 %all-reduce.13.cloned.1.call-done = f32[128,1536]{1,0:T(8,128)} async-done(((f32[128,1536]{1,0:T(8,128)}), f32[128,1536]{1,0:T(8,128)}) %all-reduce.13.cloned.1.call-update) | async-done | bytes 786448 | tf_op jit(solution)/shard_map/psum | solution.py:121
  57.4 1.5 multiply_reduce_fusion.10
  59.5 2.7 fusion.22
  62.2 3.5 multiply_convert_fusion.9
  65.7 1.5 fusion.14
  67.3 2.4 copy.42
  69.6 32.8 %all-reduce.15.cloned.1.call-done = f32[128,1536]{1,0:T(8,128)} async-done(((f32[128,1536]{1,0:T(8,128)}), f32[128,1536]{1,0:T(8,128)}) %all-reduce.15.cloned.1.call-update) | async-done | bytes 786448 | tf_op jit(solution)/shard_map/psum | solution.py:128
  104.1 1.5 convolution_convert_fusion.2
  108.7 4.1 fusion
  112.8 31.0 %all-reduce.17.cloned.1.call-done = f32[128,1536]{1,0:T(8,128)} async-done(((f32[128,1536]{1,0:T(8,128)}), f32[128,1536]{1,0:T(8,128)}) %all-reduce.17.cloned.1.call-update) | async-done | bytes 786448 | tf_op jit(solution)/shard_map/psum | solution.py:121
  143.9 1.5 multiply_reduce_fusion.8
  146.8 2.7 fusion.6
  149.5 3.7 multiply_convert_fusion.7
  155.1 2.1 fusion.39
  158.6 33.8 %all-reduce.19.cloned.1.call-done = f32[128,1536]{1,0:T(8,128)} async-done(((f32[128,1536]{1,0:T(8,128)}), f32[128,1536]{1,0:T(8,128)}) %all-reduce.19.cloned.1.call-update) | async-done | bytes 786448 | tf_op jit(solution)/shard_map/psum | solution.py:183
  192.4 2.2 multiply_reduce_fusion
  194.6 1.6 multiply_add_fusion.3
  201.8 1.8 fusion.46
  205.7 34.9 %all-reduce.21.cloned.1.call-done = f32[128,1536]{1,0:T(8,128)} async-done(((f32[128,1536]{1,0:T(8,128)}), f32[128,1536]{1,0:T(8,128)}) %all-reduce.21.cloned.1.call-update) | async-done | bytes 786448 | tf_op jit(solution)/shard_map/psum | solution.py:213
  240.6 2.1 multiply_reduce_fusion.2
  242.7 1.5 multiply_add_fusion.2
  244.3 3.4 multiply_convert_fusion.5
  248.4 3.1 fusion.16
  251.5 2.1 fusion.36
  254.3 3.4 fusion.2
  257.7 31.1 %all-reduce.23.cloned.1.call-done = f32[128,1536]{1,0:T(8,128)} async-done(((f32[128,1536]{1,0:T(8,128)}), f32[128,1536]{1,0:T(8,128)}) %all-reduce.23.cloned.1.call-update) | async-done | bytes 786448 | tf_op jit(solution)/shard_map/psum | solution.py:183
  288.8 2.2 multiply_reduce_fusion.1
  297.6 1.8 fusion.52
  306.2 38.9 %all-reduce.27.cloned.1.call-done = (f32[128,1536]{1,0:T(8,128)}, f32[128,1536]{1,0:T(8,128)}) async-done(((f32[128,1536]{1,0:T(8,128)}, f32[128,1536]{1,0:T(8,128)}), (f32[128,1536]{1,0:T(8,128)}, f32[128,1536]{1,0:T(8,128)})) %all-reduce.27.cloned.1.call-update) | async-done | bytes 1572880 | tf_op jit(solution)/shard_map/psum | solution.py:128
  347.8 1.8 pad_maximum_fusion.6
  349.6 3.4 copy.76
  353.0 5.0 reshape.307
  358.7 1.5 pad_maximum_fusion.5
  360.2 4.0 copy.74
  364.3 3.6 reshape.305
  368.2 2.3 convolution_bitcast_fusion
  370.5 1.8 convolution_bitcast_fusion.6
  372.4 3.6 convolution_bitcast_fusion.1
  376.0 8.7 pad_maximum_fusion.2
  384.7 19.5 %copy.53 = f32[2,1024,1536]{1,0,2:T(2,128)} copy(f32[2,1024,1536]{2,1,0:T(8,128)} %pad_maximum_fusion.2) | data formatting | bytes 25165824 | tf_op jit(solution)/shard_map/stack | solution.py:277
  404.2 1.5 convolution_bitcast_fusion.7
  406.0 2.4 pad_maximum_fusion.4
  408.4 8.2 copy.52
  418.6 2.4 pad_maximum_fusion.3
  421.1 2.1 convolution_bitcast_fusion.4
  423.3 3.6 convolution_bitcast_fusion.5
  426.9 9.5 pad_maximum_fusion
  436.7 2.1 convolution_bitcast_fusion.2
  438.8 3.6 convolution_bitcast_fusion.3
  442.4 9.5 pad_maximum_fusion.1
  453.8 1.6 copy.81
  455.3 2.1 add.176
  458.6 18.7 %reduce-scatter.26.cloned.1.call-done = f32[192,2]{1,0:T(8,128)} async-done(((f32[1536,2]{1,0:T(8,128)}), f32[192,2]{1,0:T(8,128)}) %reduce-scatter.26.cloned.1.call-update) | async-done | bytes 1552
  477.3 1.5 copy.79
  478.8 70.6 %reduce-scatter.24.cloned.1.call-done = f32[192,384]{1,0:T(8,128)} async-done(((f32[1536,384]{1,0:T(8,128)}), f32[192,384]{1,0:T(8,128)}) %reduce-scatter.24.cloned.1.call-update) | async-done | bytes 294928
  551.5 70.2 %reduce-scatter.22.cloned.1.call-done = f32[192,384]{1,0:T(8,128)} async-done(((f32[1536,384]{1,0:T(8,128)}), f32[192,384]{1,0:T(8,128)}) %reduce-scatter.22.cloned.1.call-update) | async-done | bytes 294928
  623.7 526.5 %all-reduce.25.cloned.1.call-done = (f32[2,384,1536]{1,0,2:T(2,128)}, f32[2,1024,1536]{1,0,2:T(2,128)}) async-done(((f32[2,384,1536]{1,0,2:T(2,128)}, f32[2,1024,1536]{1,0,2:T(2,128)}), (f32[2,384,1536]{1,0,2:T(2,128)}, f32[2,1024,1536]{1,0,2:T(2,128)})) %all-reduce.25.cloned.1.call-update) | async-done | bytes 17301520
  1150.2 1.9 constant_dynamic-slice_fusion
  1152.2 1.6 copy.57
  1155.9 93.3 %reduce-scatter.16.cloned.1.call-done = f32[2,192,384]{2,1,0:T(8,128)} async-done(((f32[2,1536,384]{2,1,0:T(8,128)}), f32[2,192,384]{2,1,0:T(8,128)}) %reduce-scatter.16.cloned.1.call-update) | async-done | bytes 589840 | tf_op jit(solution)/shard_map/reduce_scatter | solution.py:282
  1249.2 211.1 %reduce-scatter.18.cloned.1.call-done = f32[2,192,1024]{2,1,0:T(8,128)} async-done(((f32[2,1536,1024]{2,1,0:T(8,128)}), f32[2,192,1024]{2,1,0:T(8,128)}) %reduce-scatter.18.cloned.1.call-update) | async-done | bytes 1572880 | tf_op jit(solution)/shard_map/reduce_scatter | solution.py:286
  1460.3 210.6 %reduce-scatter.20.cloned.1.call-done = f32[2,192,1024]{2,1,0:T(8,128)} async-done(((f32[2,1536,1024]{2,1,0:T(8,128)}), f32[2,192,1024]{2,1,0:T(8,128)}) %reduce-scatter.20.cloned.1.call-update) | async-done | bytes 1572880 | tf_op jit(solution)/shard_map/reduce_scatter | solution.py:287
  (350 shorter events, 54.1 us)
Async XLA Ops:
  7.2 50.2 %all-reduce.13.cloned.1.call-start = ((), (), s32[]{:S(2)}) async-start(), calls=%async_computation.7 | async-start | bytes 1572864 | tf_op jit(solution)/shard_map/psum | solution.py:121
  9.3 6.0 copy-start.92
  9.3 5.0 copy-start.99
  9.4 5.0 copy-start.25
  17.0 89.4 %copy-start.31 = (f32[128,48]{0,1:T(8,128)}, f32[128,48]{0,1:T(8,128)S(1)}, u32[]{:S(2)}) copy-start(f32[128,48]{0,1:T(8,128)S(1)} %get-tuple-element.82) | copy-start | bytes 73732
  17.1 41.8 %copy-start.60 = (bf16[128,4,48]{0,2,1:T(8,128)(2,1)}, bf16[128,4,48]{0,2,1:T(8,128)(2,1)S(1)}, u32[]{:S(2)}) copy-start(bf16[128,4,48]{0,2,1:T(8,128)(2,1)S(1)} %get-tuple-element.70) | copy-start | bytes 147460
  17.1 41.8 %copy-start.62 = (bf16[128,4,48]{0,2,1:T(8,128)(2,1)}, bf16[128,4,48]{0,2,1:T(8,128)(2,1)S(1)}, u32[]{:S(2)}) copy-start(bf16[128,4,48]{0,2,1:T(8,128)(2,1)S(1)} %get-tuple-element.71) | copy-start | bytes 147460
  17.1 41.7 %copy-start.70 = (bf16[128,2,48]{0,2,1:T(8,128)(2,1)}, bf16[128,2,48]{0,2,1:T(8,128)(2,1)S(1)}, u32[]{:S(2)}) copy-start(bf16[128,2,48]{0,2,1:T(8,128)(2,1)S(1)} %get-tuple-element.78) | copy-start | bytes 73732
  17.6 41.3 %copy-start.78 = (bf16[128,192]{0,1:T(8,128)(2,1)}, bf16[128,192]{0,1:T(8,128)(2,1)S(1)}, u32[]{:S(2)}) copy-start(bf16[128,192]{0,1:T(8,128)(2,1)S(1)} %convolution_convert_fusion.3) | copy-start | bytes 147460
  17.9 41.0 %copy-start.28 = (f32[2,2,128,128]{2,3,1,0:T(8,128)}, f32[2,2,128,128]{2,3,1,0:T(8,128)S(1)}, u32[]{:S(2)}) copy-start(f32[2,2,128,128]{2,3,1,0:T(8,128)S(1)} %get-tuple-element.84) | copy-start | bytes 786436
  17.9 41.0 %copy-start.86 = (f32[2,2,128]{2,1,0:T(2,128)}, f32[2,2,128]{2,1,0:T(2,128)S(1)}, u32[]{:S(2)}) copy-start(f32[2,2,128]{2,1,0:T(2,128)S(1)} %get-tuple-element.83) | copy-start | bytes 6148
  17.9 41.0 %copy-start.88 = (f32[2,2,128]{2,1,0:T(2,128)}, f32[2,2,128]{2,1,0:T(2,128)S(1)}, u32[]{:S(2)}) copy-start(f32[2,2,128]{2,1,0:T(2,128)S(1)} %fusion.98) | copy-start | bytes 6148
  18.2 40.9 %copy-start.40 = (bf16[2,96,2,128]{3,1,2,0:T(8,128)(2,1)}, bf16[2,96,2,128]{3,1,2,0:T(8,128)(2,1)S(1)}, u32[]{:S(2)}) copy-start(bf16[2,96,2,128]{3,1,2,0:T(8,128)(2,1)S(1)} %convolution_convert_fusion.1) | copy-start | bytes 294916
  19.5 82.9 %all-reduce.15.cloned.1.call-start = ((), (), s32[]{:S(2)}) async-start(), calls=%async_computation.8 | async-start | bytes 1572864 | tf_op jit(solution)/shard_map/psum | solution.py:128
  20.2 38.9 %copy-start.68 = (f32[1536]{0:T(1024)}, f32[1536]{0:T(1024)S(1)}, u32[]{:S(2)}) copy-start(f32[1536]{0:T(1024)S(1)} %get-tuple-element.42) | copy-start | bytes 18436
  57.4 8.3 slice-start.4
  59.5 6.2 copy-start.18
  59.5 6.2 slice-start.5
  67.2 76.7 %all-reduce.17.cloned.1.call-start = ((), (), s32[]{:S(2)}) async-start(), calls=%async_computation.9 | async-start | bytes 1572864 | tf_op jit(solution)/shard_map/psum | solution.py:121
  106.5 6.3 copy-start.76
  106.8 6.0 copy-start.29
  106.8 6.0 copy-start.90
  107.1 5.7 copy-start.91
  107.3 5.5 copy-start.41
  108.7 83.7 %all-reduce.19.cloned.1.call-start = ((), (), s32[]{:S(2)}) async-start(), calls=%async_computation.10 | async-start | bytes 1572864 | tf_op jit(solution)/shard_map/psum | solution.py:183
  143.9 10.0 slice-start.6
  145.3 49.2 %copy-start.2 = (f32[128,1536]{1,0:T(8,128)}, f32[128,1536]{1,0:T(8,128)S(1)}, u32[]{:S(2)}) copy-start(f32[128,1536]{1,0:T(8,128)S(1)} %get-tuple-element.50) | copy-start | bytes 2359300
  146.8 6.5 copy-start.20
  146.8 7.2 slice-start.7
  146.8 8.3 slice-start
  149.5 5.6 slice-start.1
  157.2 83.4 %all-reduce.21.cloned.1.call-start = ((), (), s32[]{:S(2)}) async-start(), calls=%async_computation.11 | async-start | bytes 1572864 | tf_op jit(solution)/shard_map/psum | solution.py:213
  192.4 4.7 copy-start.15
  197.1 4.4 copy-start.77
  197.1 4.5 copy-start.32
  197.1 4.5 copy-start.50
  197.8 5.9 copy-start.26
  203.6 39.1 %copy-start.11 = (f32[128,1536]{1,0:T(8,128)S(1)}, f32[128,1536]{1,0:T(8,128)}, u32[]{:S(2)}) copy-start(f32[128,1536]{1,0:T(8,128)} %copy-done.10) | copy-start | bytes 2359300
  205.4 83.4 %all-reduce.23.cloned.1.call-start = ((), (), s32[]{:S(2)}) async-start(), calls=%async_computation.12 | async-start | bytes 1572864 | tf_op jit(solution)/shard_map/psum | solution.py:183
  242.7 8.8 slice-start.2
  244.3 7.3 slice-start.3
  247.7 5.9 copy-start.38
  253.6 35.2 %copy-start.69 = (f32[1536]{0:T(1024)S(1)}, f32[1536]{0:T(1024)}, u32[]{:S(2)}) copy-start(f32[1536]{0:T(1024)} %copy-done.68) | copy-start | bytes 18436
  253.6 35.2 %copy-start.95 = (f32[128]{0:T(128)S(1)}, f32[128]{0:T(128)}, u32[]{:S(2)}) copy-start(f32[128]{0:T(128)} %copy-done.94) | copy-start | bytes 1540
  253.6 37.3 %copy-start.22 = (f32[128,1536]{1,0:T(8,128)S(1)}, f32[128,1536]{1,0:T(8,128)}, u32[]{:S(2)}) copy-start(f32[128,1536]{1,0:T(8,128)} %copy-done.21) | copy-start | bytes 2359300
  253.6 91.5 %all-reduce.27.cloned.1.call-start = ((), (), s32[]{:S(2)}) async-start(), calls=%async_computation.21 | async-start | bytes 3145728 | tf_op jit(solution)/shard_map/psum | solution.py:128
  292.4 7.0 copy-start.7
  292.4 4.4 copy-start.33
  292.4 4.4 copy-start.51
  295.2 5.7 copy-start.36
  302.0 43.1 %copy-start.93 = (f32[128]{0:T(128)S(1)}, f32[128]{0:T(128)}, u32[]{:S(2)}) copy-start(f32[128]{0:T(128)} %copy-done.92) | copy-start | bytes 1540
  302.1 151.7 %reduce-scatter.28.cloned.1.call-start = ((), (), s32[]{:S(2)}) async-start(), calls=%async_computation.19 | async-start | bytes 884736
  306.1 171.1 %reduce-scatter.26.cloned.1.call-start = ((), (), s32[]{:S(2)}) async-start(), calls=%async_computation.18 | async-start | bytes 884736
  347.8 201.7 %reduce-scatter.24.cloned.1.call-start = ((), (), s32[]{:S(2)}) async-start(), calls=%async_computation.17 | async-start | bytes 2654208
  353.0 5.1 copy-start.54
  358.0 263.7 %reduce-scatter.22.cloned.1.call-start = ((), (), s32[]{:S(2)}) async-start(), calls=%async_computation.16 | async-start | bytes 2654208
  367.9 782.3 %all-reduce.25.cloned.1.call-start = ((), (), s32[]{:S(2)}) async-start(), calls=%async_computation.20 | async-start | bytes 34603008
  384.7 19.5 %copy-start.8 = (f32[128,1536]{1,0:T(8,128)S(1)}, f32[128,1536]{1,0:T(8,128)}, u32[]{:S(2)}) copy-start(f32[128,1536]{1,0:T(8,128)} %copy-done.7) | copy-start | bytes 2359300
  416.6 832.6 %reduce-scatter.16.cloned.1.call-start = ((), (), s32[]{:S(2)}) async-start(), calls=%async_computation.13 | async-start | bytes 5308416 | tf_op jit(solution)/shard_map/reduce_scatter | solution.py:282
  421.1 1039.3 %reduce-scatter.18.cloned.1.call-start = ((), (), s32[]{:S(2)}) async-start(), calls=%async_computation.14 | async-start | bytes 14155776 | tf_op jit(solution)/shard_map/reduce_scatter | solution.py:286
  436.4 1234.6 %reduce-scatter.20.cloned.1.call-start = ((), (), s32[]{:S(2)}) async-start(), calls=%async_computation.15 | async-start | bytes 14155776 | tf_op jit(solution)/shard_map/reduce_scatter | solution.py:287
  451.9 5.6 copy-start.1
  451.9 5.6 copy-start.9
  451.9 5.6 copy-start.27
  (63 other events, 156.0 us)
Sparse Core Ops, SparseCore 0:
  19.6 37.7 all-reduce.12
  67.3 35.0 all-reduce.14
  108.8 35.0 all-reduce.16
  157.3 35.0 all-reduce.18
  205.6 34.9 all-reduce.20
  253.8 34.9 all-reduce.22
  302.2 42.8 all-reduce.26
  348.4 63.1 reduce-scatter.27
  414.9 62.3 reduce-scatter.25
  480.6 68.7 reduce-scatter.23
  553.0 68.7 reduce-scatter.21
  625.9 524.3 all-reduce.24
  1154.5 94.6 reduce-scatter.15
  1253.2 207.0 reduce-scatter.17
  1464.3 206.5 reduce-scatter.19
where the time goes:
time: 1690 us; the launch traced here: 1680 us
  waiting for transfers between devices  1440 us (85%)
  matrix products  79.1 us (5%)
  local copies, waits for them, and re-layouts  76.1 us (5%)
  other arithmetic  63.4 us (4%)
    unnamed x20, waiting for transfers between devices  686 us
    reduce_scatter x1, waiting for transfers between devices, shards(): lax.psum_scatter(stacked[4], 'dp', scatter_dimension=1, tiled=True)  211 us
    reduce_scatter x1, waiting for transfers between devices, shards(): lax.psum_scatter(stacked[5], 'dp', scatter_dimension=1, tiled=True)  211 us
    reduce_scatter x1, waiting for transfers between devices, shards(): lax.psum_scatter(stacked[0], 'dp', scatter_dimension=1, tiled=True)  93.3 us
    psum x2, waiting for transfers between devices, layer_forward(): output = attended + lax.psum(mlp_part, 'tensor')  71.7 us
    psum x2, waiting for transfers between devices, layer_forward(): attended = hidden + lax.psum(attn_part, 'tensor')  68.3 us
    psum x2, waiting for transfers between devices, layer_backward(): grad_normed_two = lax.psum(mlp_input_part, 'tensor')  65 us
    unnamed x241, local copies, waits for them, and re-layouts  38.5 us
  transfers between devices with their start and end apart: 15, of which 14 were waited for; matrix products, arithmetic and copies ran while one was open for 8% of the time, Pallas kernels for 0%

commit v1 on v0

--- a/solution.py
+++ b/solution.py
@@ -1,15 +1,256 @@
+import functools
+
 import jax
 import jax.numpy as jnp
 from jax import lax
+from jax.experimental import pallas as pl
+from jax.experimental.pallas import tpu as pltpu
 from jax.sharding import PartitionSpec as P
 
 HD = 96
 LAYERS = 2
+CHUNKS = 4
+MESH = pl.DeviceIdType.MESH
 
 
 epsilon = 1e-05
 rope_base = 100000.0
 masked_score = -1e30
+
+
+def reduce_kernel(part, base, out, from_core, half, from_y, send, recv):
+    dp = lax.axis_index("dp")
+    tensor = lax.axis_index("tensor")
+    core = tensor % 2
+    core_peer = (dp, tensor + 1 - 2 * core)
+    y_peer = (dp, lax.rem(tensor + 2, 4))
+    rows = part.shape[0] // CHUNKS
+    width = part.shape[1] // 2
+    mine = pl.ds(pl.multiple_of(core * width, 128), width)
+    other = pl.ds(pl.multiple_of((1 - core) * width, 128), width)
+
+    barrier = pltpu.get_barrier_semaphore()
+    for peer in (core_peer, y_peer):
+        pl.semaphore_signal(barrier, inc=1, device_id=peer, device_id_type=MESH)
+    pl.semaphore_wait(barrier, 2)
+
+    def copy(stage, k, src, dst, peer):
+        return pltpu.make_async_remote_copy(
+            src_ref=src,
+            dst_ref=dst,
+            send_sem=send.at[stage, k],
+            recv_sem=recv.at[stage, k],
+            device_id=peer,
+            device_id_type=MESH,
+        )
+
+    rows_of = [pl.ds(k * rows, rows) for k in range(CHUNKS)]
+    first = [
+        copy(0, k, part.at[rows_of[k], other], from_core.at[rows_of[k]], core_peer)
+        for k in range(CHUNKS)
+    ]
+    second = [
+        copy(1, k, half.at[rows_of[k]], from_y.at[rows_of[k]], y_peer) for k in range(CHUNKS)
+    ]
+    third = [
+        copy(2, k, out.at[rows_of[k], mine], out.at[rows_of[k], mine], core_peer)
+        for k in range(CHUNKS)
+    ]
+    for k in range(CHUNKS):
+        first[k].start()
+    for k in range(CHUNKS):
+        first[k].wait_recv()
+        half[rows_of[k], :] = part[rows_of[k], mine] + from_core[rows_of[k], :]
+        second[k].start()
+    for k in range(CHUNKS):
+        second[k].wait_recv()
+        out[rows_of[k], mine] = base[rows_of[k], mine] + (
+            half[rows_of[k], :] + from_y[rows_of[k], :]
+        )
+        third[k].start()
+    for k in range(CHUNKS):
+        third[k].wait_recv()
+    for k in range(CHUNKS):
+        first[k].wait_send()
+        second[k].wait_send()
+        third[k].wait_send()
+
+
+def tensor_sum(part, base):
+    length, width = part.shape
+    vmem = pl.BlockSpec(memory_space=pltpu.VMEM)
+    return pl.pallas_call(
+        reduce_kernel,
+        out_shape=jax.ShapeDtypeStruct((length, width), jnp.float32),
+        in_specs=[vmem, vmem],
+        out_specs=vmem,
+        scratch_shapes=[
+            pltpu.VMEM((length, width // 2), jnp.float32),
+            pltpu.VMEM((length, width // 2), jnp.float32),
+            pltpu.VMEM((length, width // 2), jnp.float32),
+            pltpu.SemaphoreType.DMA((3, CHUNKS)),
+            pltpu.SemaphoreType.DMA((3, CHUNKS)),
+        ],
+        compiler_params=pltpu.CompilerParams(collective_id=0, has_side_effects=True),
+        name="tensor_sum",
+    )(part, base)
+
+
+def gather_kernel(n, own_full, shared_full, sliced_full, *refs):
+    own_n, shared_n, sliced_n = len(own_full), len(shared_full), len(sliced_full)
+    ins = refs[: own_n + shared_n + sliced_n]
+    outs = refs[own_n + shared_n + sliced_n : 2 * (own_n + shared_n + sliced_n)]
+    send, recv, send_x, recv_x, send_c, recv_c, send_a, recv_a, local = refs[
+        2 * (own_n + shared_n + sliced_n) :
+    ]
+    dp = lax.axis_index("dp")
+    tensor = lax.axis_index("tensor")
+    core = tensor % 2
+    side = dp % 2
+    group = dp // 2
+    groups = n // 2
+    core_peer = (dp, tensor + 1 - 2 * core)
+    x_peer = (dp + 1 - 2 * side, tensor)
+
+    barrier = pltpu.get_barrier_semaphore()
+    for peer in [core_peer] + [(lax.rem(dp + k, n), tensor) for k in range(1, n)]:
+        pl.semaphore_signal(barrier, inc=1, device_id=peer, device_id_type=MESH)
+    pl.semaphore_wait(barrier, n)
+
+    def remote(src, dst, s, r, peer):
+        return pltpu.make_async_remote_copy(
+            src_ref=src, dst_ref=dst, send_sem=s, recv_sem=r, device_id=peer, device_id_type=MESH
+        )
+
+    locals_ = []
+    for a, (src, dst) in enumerate(zip(ins, outs)):
+        if a < own_n + shared_n:
+            length = src.shape[0]
+            there = dst.at[pl.ds(pl.multiple_of(dp * length, 8), length)]
+            locals_.append(pltpu.make_async_copy(src, there, local.at[a]))
+        else:
+            locals_.append(pltpu.make_async_copy(src.at[dp], dst.at[dp], local.at[a]))
+        locals_[-1].start()
+
+    def block(a, ref, index, whole):
+        length = ins[a].shape[0]
+        rows = pl.ds(pl.multiple_of(index * length, 8), length)
+        if a < own_n:
+            return ref.at[:, :] if whole else ref.at[rows]
+        width = ins[a].shape[1] // 2
+        columns = pl.ds(pl.multiple_of(core * width, 128), width)
+        return ref.at[:, columns] if whole else ref.at[rows, columns]
+
+    pending = []
+    arrays = range(own_n + shared_n)
+    direct = {}
+    for a in arrays:
+        for k in range(1, groups):
+            peer = (lax.rem(group + k, groups) * 2 + side, tensor)
+            c = remote(
+                block(a, ins[a], 0, True),
+                block(a, outs[a], dp, False),
+                send.at[a, k],
+                recv.at[a, k],
+                peer,
+            )
+            c.start()
+            direct[a, k] = c
+        c = remote(
+            block(a, ins[a], 0, True),
+            block(a, outs[a], dp, False),
+            send_x.at[a, 0],
+            recv_x.at[a, 0],
+            x_peer,
+        )
+        c.start()
+        direct[a, 0] = c
+    exchange = []
+    for b in range(sliced_n):
+        a = own_n + shared_n + b
+        for k in range(1, n):
+            to = lax.rem(dp + k, n)
+            c = remote(
+                ins[a].at[to], outs[a].at[dp], send_a.at[b, k], recv_a.at[b, k], (to, tensor)
+            )
+            c.start()
+            exchange.append(c)
+    crossed = {}
+    for a in arrays:
+        for k in range(1, groups):
+            direct[a, k].wait_recv()
+            source = lax.rem(group + groups - k, groups) * 2 + side
+            c = remote(
+                block(a, outs[a], source, False),
+                block(a, outs[a], source, False),
+                send_x.at[a, k],
+                recv_x.at[a, k],
+                x_peer,
+            )
+            c.start()
+            crossed[a, k] = c
+            if a >= own_n:
+                c = remote(
+                    block(a, outs[a], source, False),
+                    block(a, outs[a], source, False),
+                    send_c.at[a - own_n, k],
+                    recv_c.at[a - own_n, k],
+                    core_peer,
+                )
+                c.start()
+                pending.append(c)
+    for a in arrays:
+        for k in range(groups):
+            (direct[a, 0] if k == 0 else crossed[a, k]).wait_recv()
+            if a >= own_n:
+                source = lax.rem(group + groups - k, groups) * 2 + 1 - side
+                c = remote(
+                    block(a, outs[a], source, False),
+                    block(a, outs[a], source, False),
+                    send_c.at[a - own_n, groups + k],
+                    recv_c.at[a - own_n, groups + k],
+                    core_peer,
+                )
+                c.start()
+                pending.append(c)
+    for c in exchange:
+        c.wait()
+    for c in pending:
+        c.wait()
+    for c in list(direct.values()) + list(crossed.values()):
+        c.wait_send()
+    for c in locals_:
+        c.wait()
+
+
+def gather(n, own, shared, sliced):
+    arrays = list(own) + list(shared) + list(sliced)
+    out_shape = [
+        jax.ShapeDtypeStruct((n * a.shape[0], a.shape[1]), jnp.float32)
+        for a in list(own) + list(shared)
+    ] + [jax.ShapeDtypeStruct(a.shape, jnp.float32) for a in sliced]
+    anywhere = pl.BlockSpec(memory_space=pl.ANY)
+    whole = len(own) + len(shared)
+    dma = pltpu.SemaphoreType.DMA
+    return pl.pallas_call(
+        functools.partial(gather_kernel, n, tuple(own), tuple(shared), tuple(sliced)),
+        out_shape=out_shape,
+        in_specs=[anywhere] * len(arrays),
+        out_specs=[anywhere] * len(arrays),
+        scratch_shapes=[
+            dma((whole, n // 2)),
+            dma((whole, n // 2)),
+            dma((whole, n // 2)),
+            dma((whole, n // 2)),
+            dma((len(shared), n)),
+            dma((len(shared), n)),
+            dma((len(sliced), n)),
+            dma((len(sliced), n)),
+            dma((len(arrays),)),
+        ],
+        compiler_params=pltpu.CompilerParams(collective_id=1, has_side_effects=True),
+        name="gather_tokens",
+    )(*arrays)
 
 
 def inverse_rms(values):
@@ -118,14 +359,14 @@
     mixed_rows, logsum = attention_forward(queries, key_rows, value_rows, allowed)
     mixed_flat = mixed_rows.reshape(length, query_heads * HD)
     attn_part = jnp.dot(mixed_flat, w_output, preferred_element_type=jnp.float32)
-    attended = hidden + lax.psum(attn_part, "tensor")
+    attended = tensor_sum(attn_part, hidden)
     inverse_two = inverse_rms(attended)
     normed_two = (attended * inverse_two * mlp_gain).astype(jnp.bfloat16)
     gate_pre = jnp.dot(normed_two, w_gate, preferred_element_type=jnp.float32)
     up_pre = jnp.dot(normed_two, w_up, preferred_element_type=jnp.float32)
     activated = (jax.nn.silu(gate_pre) * up_pre).astype(jnp.bfloat16)
     mlp_part = jnp.dot(activated, w_down, preferred_element_type=jnp.float32)
-    output = attended + lax.psum(mlp_part, "tensor")
+    output = tensor_sum(mlp_part, attended)
     kept_state = (
         hidden,
         inverse_one,
@@ -140,7 +381,6 @@
         normed_two,
         gate_pre,
         up_pre,
-        activated,
     )
     return (output, kept_state)
 
@@ -161,71 +401,74 @@
         normed_two,
         gate_pre,
         up_pre,
-        activated,
     ) = kept_state
     length = hidden.shape[0]
     query_heads = w_query.shape[1] // HD
     kv_heads = w_key.shape[1] // HD
     group_size = query_heads // kv_heads
+    zeros = jnp.zeros_like(hidden)
     g_low = upstream.astype(jnp.bfloat16)
-    grad_down = jnp.dot(activated.T, g_low, preferred_element_type=jnp.float32)
     grad_act = jnp.dot(g_low, w_down.T, preferred_element_type=jnp.float32)
+    grad_gate_low, grad_up_low, _ = mlp_grads(gate_pre, up_pre, grad_act)
+    mlp_input_part = jnp.dot(grad_gate_low, w_gate.T, preferred_element_type=jnp.float32) + jnp.dot(
+        grad_up_low, w_up.T, preferred_element_type=jnp.float32
+    )
+    grad_normed_two = tensor_sum(mlp_input_part, zeros)
+    grad_mlp_gain, grad_norm_two = norm_backward(grad_normed_two, attended, inverse_two, mlp_gain)
+    grad_attended = upstream + grad_norm_two
+    grad_att_low = grad_attended.astype(jnp.bfloat16)
+    grad_mixed = jnp.dot(grad_att_low, w_output.T, preferred_element_type=jnp.float32).astype(
+        jnp.bfloat16
+    )
+    grad_mixed = grad_mixed.reshape(length, kv_heads, group_size, HD)
+    grad_queries, grad_keys, grad_values = attention_backward(
+        queries, key_rows, value_rows, mixed_rows, logsum, grad_mixed, allowed
+    )
+    grad_query_low = (
+        rotate(grad_queries.reshape(length, query_heads, HD), cosine, sine, -1.0)
+        .astype(jnp.bfloat16)
+        .reshape(length, query_heads * HD)
+    )
+    grad_key_low = (
+        rotate(grad_keys, cosine, sine, -1.0).astype(jnp.bfloat16).reshape(length, kv_heads * HD)
+    )
+    grad_value_low = grad_values.astype(jnp.bfloat16).reshape(length, kv_heads * HD)
+    attn_input_part = (
+        jnp.dot(grad_query_low, w_query.T, preferred_element_type=jnp.float32)
+        + jnp.dot(grad_key_low, w_key.T, preferred_element_type=jnp.float32)
+        + jnp.dot(grad_value_low, w_value.T, preferred_element_type=jnp.float32)
+    )
+    grad_normed = tensor_sum(attn_input_part, zeros)
+    grad_attn_gain, grad_norm_one = norm_backward(grad_normed, hidden, inverse_one, attn_gain)
+    grad_hidden = grad_attended + grad_norm_one
+    sent = (
+        jnp.concatenate(
+            [mixed_rows.reshape(length, query_heads * HD), grad_query_low, grad_key_low, grad_value_low],
+            axis=1,
+        ).astype(jnp.float32),
+        normed_two.astype(jnp.float32),
+        g_low.astype(jnp.float32),
+        normed.astype(jnp.float32),
+        grad_att_low.astype(jnp.float32),
+        grad_attn_gain,
+        grad_mlp_gain,
+    )
+    return grad_hidden, sent
+
+
+def mlp_grads(gate_pre, up_pre, grad_act):
     sigmoid_gate = jax.nn.sigmoid(gate_pre)
     grad_gate_low = (
         grad_act * up_pre * sigmoid_gate * (1.0 + gate_pre * (1.0 - sigmoid_gate))
     ).astype(jnp.bfloat16)
     grad_up_low = (grad_act * gate_pre * sigmoid_gate).astype(jnp.bfloat16)
-    grad_gate = jnp.dot(normed_two.T, grad_gate_low, preferred_element_type=jnp.float32)
-    grad_up = jnp.dot(normed_two.T, grad_up_low, preferred_element_type=jnp.float32)
-    mlp_input_part = jnp.dot(grad_gate_low, w_gate.T, preferred_element_type=jnp.float32) + jnp.dot(
-        grad_up_low, w_up.T, preferred_element_type=jnp.float32
-    )
-    grad_normed_two = lax.psum(mlp_input_part, "tensor")
-    grad_mlp_gain, grad_norm_two = norm_backward(grad_normed_two, attended, inverse_two, mlp_gain)
-    grad_attended = upstream + grad_norm_two
-    grad_att_low = grad_attended.astype(jnp.bfloat16)
-    mixed_flat = mixed_rows.reshape(length, query_heads * HD)
-    grad_output = jnp.dot(mixed_flat.T, grad_att_low, preferred_element_type=jnp.float32)
-    grad_mixed = jnp.dot(grad_att_low, w_output.T, preferred_element_type=jnp.float32).astype(
-        jnp.bfloat16
-    )
-    grad_mixed = grad_mixed.reshape(length, kv_heads, group_size, HD)
-    grad_queries, grad_keys, grad_values = attention_backward(
-        queries, key_rows, value_rows, mixed_rows, logsum, grad_mixed, allowed
-    )
-    grad_query_low = (
-        rotate(grad_queries.reshape(length, query_heads, HD), cosine, sine, -1.0)
-        .astype(jnp.bfloat16)
-        .reshape(length, query_heads * HD)
-    )
-    grad_key_low = (
-        rotate(grad_keys, cosine, sine, -1.0).astype(jnp.bfloat16).reshape(length, kv_heads * HD)
-    )
-    grad_value_low = grad_values.astype(jnp.bfloat16).reshape(length, kv_heads * HD)
-    grad_query = jnp.dot(normed.T, grad_query_low, preferred_element_type=jnp.float32)
-    grad_key = jnp.dot(normed.T, grad_key_low, preferred_element_type=jnp.float32)
-    grad_value = jnp.dot(normed.T, grad_value_low, preferred_element_type=jnp.float32)
-    attn_input_part = (
-        jnp.dot(grad_query_low, w_query.T, preferred_element_type=jnp.float32)
-        + jnp.dot(grad_key_low, w_key.T, preferred_element_type=jnp.float32)
-        + jnp.dot(grad_value_low, w_value.T, preferred_element_type=jnp.float32)
-    )
-    grad_normed = lax.psum(attn_input_part, "tensor")
-    grad_attn_gain, grad_norm_one = norm_backward(grad_normed, hidden, inverse_one, attn_gain)
-    grad_hidden = grad_attended + grad_norm_one
-    return (
-        grad_hidden,
-        (
-            grad_query,
-            grad_key,
-            grad_value,
-            grad_output,
-            grad_gate,
-            grad_up,
-            grad_down,
-            grad_attn_gain,
-            grad_mlp_gain,
-        ),
+    activated = (gate_pre * sigmoid_gate * up_pre).astype(jnp.bfloat16)
+    return grad_gate_low, grad_up_low, activated
+
+
+def over_tokens(left, right):
+    return lax.dot_general(
+        left, right, (((0,), (0,)), ((), ())), preferred_element_type=jnp.float32
     )
 
 
@@ -244,8 +487,11 @@
     attn_gain,
     mlp_gain,
 ):
+    n = lax.axis_size("dp")
+    dp = lax.axis_index("dp")
     weights_all = (w_query, w_key, w_value, w_output, w_gate, w_up, w_down, attn_gain, mlp_gain)
-    length = hidden_in.shape[0]
+    length, width = hidden_in.shape
+    piece = width // n
     cosine, sine = rotary_tables(positions[0])
     segments = segment_ids[0]
     token_order = jnp.arange(length)
@@ -255,52 +501,64 @@
     layer_weights = [
         tuple((weight[which_layer] for weight in weights_all)) for which_layer in range(LAYERS)
     ]
-    inputs_list = []
     kept_list = []
     hidden = hidden_in
     for which_layer in range(LAYERS):
-        inputs_list.append(hidden)
         hidden, kept_state = layer_forward(
             hidden, allowed, cosine, sine, layer_weights[which_layer]
         )
         kept_list.append(kept_state)
     upstream = cotangent
-    grad_layers = [None] * LAYERS
+    sent_layers = [None] * LAYERS
     for which_layer in reversed(range(LAYERS)):
-        kept_state = kept_list[which_layer]
-        upstream, layer_grads = layer_backward(
-            upstream, kept_state, allowed, cosine, sine, layer_weights[which_layer]
+        upstream, sent_layers[which_layer] = layer_backward(
+            upstream, kept_list[which_layer], allowed, cosine, sine, layer_weights[which_layer]
         )
-        grad_layers[which_layer] = layer_grads
-    stacked = tuple(
-        (
-            jnp.stack([grad_layers[which_layer][member] for which_layer in range(LAYERS)])
-            for member in range(9)
-        )
-    )
-    stacked = (
-        lax.psum_scatter(stacked[0], "dp", scatter_dimension=1, tiled=True),
-        lax.psum_scatter(stacked[1], "dp", scatter_dimension=1, tiled=True),
-        lax.psum_scatter(stacked[2], "dp", scatter_dimension=1, tiled=True),
-        lax.psum_scatter(stacked[3], "dp", scatter_dimension=2, tiled=True),
-        lax.psum_scatter(stacked[4], "dp", scatter_dimension=1, tiled=True),
-        lax.psum_scatter(stacked[5], "dp", scatter_dimension=1, tiled=True),
-        lax.psum_scatter(stacked[6], "dp", scatter_dimension=2, tiled=True),
-        lax.psum_scatter(stacked[7], "dp", scatter_dimension=1, tiled=True),
-        lax.psum_scatter(stacked[8], "dp", scatter_dimension=1, tiled=True),
-    )
+
+    def by_piece(rows):
+        return jnp.transpose(rows.reshape(rows.shape[0], n, piece), (1, 0, 2))
+
+    own, shared, sliced = [], [], []
+    for sent in sent_layers:
+        own.append(sent[0])
+        shared.extend(sent[1:3])
+        sliced.extend([by_piece(sent[3]), by_piece(sent[4])])
+    gains = jnp.stack([sent[5] for sent in sent_layers] + [sent[6] for sent in sent_layers])
+    gains = jnp.concatenate([gains, jnp.zeros_like(gains)], axis=0)
+    sliced.append(by_piece(gains))
+    gathered = gather(n, own, shared, sliced)
+    whole = len(own) + len(shared)
+    heads = w_query.shape[2]
+    kv = w_key.shape[2]
+    grads = [[] for _ in range(7)]
+    for l in range(LAYERS):
+        state = gathered[l].astype(jnp.bfloat16)
+        normed_two = gathered[LAYERS + 2 * l].astype(jnp.bfloat16)
+        g_low = gathered[LAYERS + 2 * l + 1].astype(jnp.bfloat16)
+        normed = gathered[whole + 2 * l].reshape(n * length, piece).astype(jnp.bfloat16)
+        grad_att = gathered[whole + 2 * l + 1].reshape(n * length, piece).astype(jnp.bfloat16)
+        gate_pre = jnp.dot(normed_two, w_gate[l], preferred_element_type=jnp.float32)
+        up_pre = jnp.dot(normed_two, w_up[l], preferred_element_type=jnp.float32)
+        grad_act = jnp.dot(g_low, w_down[l].T, preferred_element_type=jnp.float32)
+        grad_gate_low, grad_up_low, activated = mlp_grads(gate_pre, up_pre, grad_act)
+        my_normed_two = lax.dynamic_slice_in_dim(normed_two, dp * piece, piece, 1)
+        my_g = lax.dynamic_slice_in_dim(g_low, dp * piece, piece, 1)
+        mixed = state[:, :heads]
+        grad_qkv = over_tokens(normed, state[:, heads:])
+        grads[0].append(grad_qkv[:, :heads])
+        grads[1].append(grad_qkv[:, heads : heads + kv])
+        grads[2].append(grad_qkv[:, heads + kv :])
+        grads[3].append(over_tokens(mixed, grad_att))
+        grads[4].append(over_tokens(my_normed_two, grad_gate_low))
+        grads[5].append(over_tokens(my_normed_two, grad_up_low))
+        grads[6].append(over_tokens(activated, my_g))
+    gain_sums = jnp.sum(gathered[-1], axis=0)
     return (
         hidden,
         upstream,
-        stacked[0],
-        stacked[1],
-        stacked[2],
-        stacked[3],
-        stacked[4],
-        stacked[5],
-        stacked[6],
-        stacked[7],
-        stacked[8],
+        *[jnp.stack(g) for g in grads],
+        gain_sums[:LAYERS],
+        gain_sums[LAYERS : 2 * LAYERS],
     )
 
 

time: 1690 us -> 665 us (0.39)
  waiting for transfers between devices: 1440 us -> 0 us
  Pallas kernels: 0 us -> 466 us
  local copies, waits for them, and re-layouts: 76.1 us -> 33.8 us
  matrix products: 79.1 us -> 107 us
    unnamed x20 -> x0, waiting for transfers between devices: 686 us -> none
    reduce_scatter x3 -> x0, waiting for transfers between devices: 515 us -> none  [the longest x1 211 us: shards(): lax.psum_scatter(stacked[4], 'dp', scatter_dimension=1, tiled=True)]
    pallas_call x0 -> x9, Pallas kernels: none -> 466 us  [the longest x1 336 us: gather(): pl.pallas_call(functools.partial(gather_kernel, n, tuple(own), tuple(shar...]
    psum x7 -> x0, waiting for transfers between devices: 240 us -> none  [the longest x2 71.7 us: layer_forward(): output = attended + lax.psum(mlp_part, 'tensor')]
    another operation x13 -> x9, other arithmetic: 36 us -> 5.88 us  [the longest x5 5.77 us: shards(): jnp.stack(g)]
    unnamed x241 -> x243, local copies, waits for them, and re-layouts: 38.5 us -> 11.8 us
    another operation x6 -> x4, local copies, waits for them, and re-layouts: 27.7 us -> 1.24 us  [shards(): jnp.stack([grad_layers[which_layer][member] for which_layer in range(LAYE...]
    dot_general x14 -> x16, matrix products: 24.9 us -> 49 us  [the longest x10 19.5 us: over_tokens(): lax.dot_general(left, right, (((0,), (0,)), ((), ())), preferred_element_...]
  transfers between devices with their start and end apart: 15 -> 0, of which waited for: 14 -> 0; matrix products, arithmetic and copies ran while one was open for 8% -> 0% of each run, Pallas kernels for 0% -> 0%
where the time goes in v1:
time: 665 us; the launch traced here: 659 us
  Pallas kernels  466 us (70%)
  matrix products  107 us (16%)
  other arithmetic  49.6 us (7%)
  local copies, waits for them, and re-layouts  33.8 us (5%)
    pallas_call x1, Pallas kernels, gather(): pl.pallas_call(functools.partial(gather_kernel, n, tuple(own), tuple(shar...  336 us
    pallas_call x8, Pallas kernels, tensor_sum(): pl.pallas_call(reduce_kernel, out_shape=jax.ShapeDtypeStruct((length, wid...  129 us
    dot_general x10, matrix products, over_tokens(): lax.dot_general(left, right, (((0,), (0,)), ((), ())), preferred_element_...  19.5 us

profile of v1, /device:TPU:0, one launch (start us, length us, event | category | flops | bytes accessed | tf_op | source)
XLA Modules:
  0.0 659.2 jit_solution(1616036846338941452)
XLA Ops:
  0.7 1.5 slice_reduce_fusion
  2.2 1.4 slice_reduce_fusion.1
  6.1 2.0 convolution_convert_fusion.3
  8.1 1.6 slice_bitcast_fusion
  9.8 2.4 copy.44
  12.2 1.7 fusion.136
  14.8 2.2 fusion.189
  18.4 1.3 fusion.84.part
  19.6 17.0 %tensor_sum.8.base = f32[128,1536]{1,0:T(8,128)} custom-call(f32[128,1536]{1,0:T(8,128)} %fusion.84.part, f32[128,1536]{1,0:T(8,128)} %base.1), custom_call_target="tpu_custom_call" | custom-call | tf_op jit(solution)/shard_map/tensor_sum/pallas_call | solution.py:82
  36.7 1.4 multiply_reduce_fusion.10
  38.1 2.2 fusion.188
  40.3 2.6 fusion.28
  43.0 2.7 fusion.34
  46.4 1.5 fusion.22.part
  48.0 16.1 %tensor_sum.9.base = f32[128,1536]{1,0:T(8,128)} custom-call(f32[128,1536]{1,0:T(8,128)} %fusion.22.part, f32[128,1536]{1,0:T(8,128)} %tensor_sum.8.base), custom_call_target="tpu_custom_call" | custom-call | tf_op jit(solution)/shard_map/tensor_sum/pallas_call | solution.py:82
  66.6 2.1 convolution_convert_fusion.2
  68.8 2.5 copy.46
  71.3 1.9 fusion.132
  73.3 1.4 fusion.134
  77.3 16.1 %tensor_sum.10.base = f32[128,1536]{1,0:T(8,128)} custom-call(f32[128,1536]{1,0:T(8,128)} %fusion.78.part, f32[128,1536]{1,0:T(8,128)} %tensor_sum.9.base), custom_call_target="tpu_custom_call" | custom-call | tf_op jit(solution)/shard_map/tensor_sum/pallas_call | solution.py:82
  93.4 1.4 multiply_reduce_fusion.8
  94.9 2.2 fusion.187
  97.1 2.6 fusion.10
  99.8 2.7 fusion.16
  103.2 1.5 fusion.4.part
  104.8 16.1 %tensor_sum.11 = f32[128,1536]{1,0:T(8,128)} custom-call(f32[128,1536]{1,0:T(8,128)} %fusion.4.part, f32[128,1536]{1,0:T(8,128)} %tensor_sum.10.base), custom_call_target="tpu_custom_call" | custom-call | tf_op jit(solution)/shard_map/tensor_sum/pallas_call | solution.py:82
  120.9 3.1 fusion.2
  124.0 3.1 fusion.8
  127.2 4.0 fusion.39.part
  132.1 16.0 %tensor_sum.12 = f32[128,1536]{1,0:T(8,128)} custom-call(f32[128,1536]{1,0:T(8,128)} %fusion.39.part, f32[128,1536]{1,0:T(8,128)} %broadcast_14_base.2.base), custom_call_target="tpu_custom_call" | custom-call | tf_op jit(solution)/shard_map/tensor_sum/pallas_call | solution.py:82
  148.2 2.2 multiply_reduce_fusion
  150.4 3.1 convert_convert_fusion.2
  163.7 16.0 %tensor_sum.13 = f32[128,1536]{1,0:T(8,128)} custom-call(f32[128,1536]{1,0:T(8,128)} %convolution_add_fusion.2.part, f32[128,1536]{1,0:T(8,128)} %broadcast_14_base.2.base), custom_call_target="tpu_custom_call" | custom-call | tf_op jit(solution)/shard_map/tensor_sum/pallas_call | solution.py:82
  179.8 2.0 multiply_reduce_fusion.2
  181.8 2.7 convert_convert_fusion.1
  184.5 3.4 fusion.20
  187.9 3.1 fusion.26
  191.1 2.1 fusion.36.part
  193.2 16.0 %tensor_sum.14 = f32[128,1536]{1,0:T(8,128)} custom-call(f32[128,1536]{1,0:T(8,128)} %fusion.36.part, f32[128,1536]{1,0:T(8,128)} %broadcast_14_base.2.base), custom_call_target="tpu_custom_call" | custom-call | tf_op jit(solution)/shard_map/tensor_sum/pallas_call | solution.py:82
  209.2 2.2 multiply_reduce_fusion.1
  211.4 2.5 convert_convert_fusion
  223.9 16.1 %tensor_sum.15 = f32[128,1536]{1,0:T(8,128)} custom-call(f32[128,1536]{1,0:T(8,128)} %convolution_add_fusion.part, f32[128,1536]{1,0:T(8,128)} %broadcast_14_base.2.base), custom_call_target="tpu_custom_call" | custom-call | tf_op jit(solution)/shard_map/tensor_sum/pallas_call | solution.py:82
  240.0 1.5 multiply_reduce_fusion.3
  241.5 2.3 multiply_add_fusion
  247.0 1.3 copy.65
  248.5 1.3 copy.67
  250.0 1.3 copy.69
  251.6 1.3 copy.71
  254.0 336.3 %gather_tokens.1 = (f32[1024,1152]{1,0:T(8,128)}, f32[1024,1152]{1,0:T(8,128)}, f32[1024,1536]{1,0:T(8,128)}, f32[1024,1536]{1,0:T(8,128)}, f32[1024,1536]{1,0:T...) custom-call(f32[128,1152]{1,0:T(8,128)} %convert_element_type.316.re, ...), custom_call_target="tpu_custom_call" | custom-call | tf_op jit(solution)/shard_map/gather_tokens/pallas_call | solution.py:235
  591.7 2.7 convert_element_type.327
  601.9 5.0 fusion.12
  608.4 5.4 fusion
  613.8 5.0 fusion.6
  618.8 7.0 %fusion.70 = f32[1,192,1024]{2,1,0:T(8,128)S(1)} fusion(f32[1024,1024]{1,0:T(8,128)} %fusion.12, f32[1024,1024]{1,0:T(8,128)} %fusion, f32[1024,1024]{1,0:T(8,128)} %fusion.6, bf16[1024,1536]{1,0:T(8,128)(2,1)} %copy-done.20, s32[]{:T(128)S(6)} %select_n.17), kind=kOutput, calls=%fused_computation.81 | convolution fusion | flops 413138944 | bytes 13893636 | tf_op jit(solution)/shard_map/dot_general | solution.py:470
  626.3 5.5 fusion.30
  632.3 5.3 fusion.18
  637.6 3.4 fusion.24
  641.0 2.2 fusion.71
  644.5 2.6 fusion.74
  647.1 1.6 fusion.75
  648.7 1.9 pad_maximum_fusion
  650.6 1.4 copy-done.92
  652.0 2.7 fusion.72
  654.7 1.6 fusion.73
  (358 shorter events, 52.1 us)
Async XLA Ops:
  0.6 7.5 %copy-start.4 = (bf16[2,1536,384]{2,1,0:T(8,128)(2,1)S(1)}, bf16[2,1536,384]{2,1,0:T(8,128)(2,1)}, u32[]{:S(2)}) copy-start(bf16[2,1536,384]{2,1,0:T(8,128)(2,1)} %param.17) | copy-start | bytes 7077892
  12.2 5.2 copy-start.81
  12.2 5.9 copy-start.66
  14.8 59.9 %copy-start.27 = (f32[128,48]{0,1:T(8,128)}, f32[128,48]{0,1:T(8,128)S(1)}, u32[]{:S(2)}) copy-start(f32[128,48]{0,1:T(8,128)S(1)} %get-tuple-element.84) | copy-start | bytes 73732
  17.3 20.8 %copy-start.61 = (bf16[128,2,48]{0,2,1:T(8,128)(2,1)}, bf16[128,2,48]{0,2,1:T(8,128)(2,1)S(1)}, u32[]{:S(2)}) copy-start(bf16[128,2,48]{0,2,1:T(8,128)(2,1)S(1)} %get-tuple-element.78) | copy-start | bytes 73732
  17.3 20.8 %copy-start.62 = (bf16[128,2,48]{0,2,1:T(8,128)(2,1)}, bf16[128,2,48]{0,2,1:T(8,128)(2,1)S(1)}, u32[]{:S(2)}) copy-start(bf16[128,2,48]{0,2,1:T(8,128)(2,1)S(1)} %get-tuple-element.79) | copy-start | bytes 73732
  17.7 20.4 %copy-start.23 = (f32[2,2,128,128]{2,3,1,0:T(8,128)}, f32[2,2,128,128]{2,3,1,0:T(8,128)S(1)}, u32[]{:S(2)}) copy-start(f32[2,2,128,128]{2,3,1,0:T(8,128)S(1)} %get-tuple-element.86) | copy-start | bytes 786436
  17.7 20.4 %copy-start.72 = (f32[2,2,128]{2,1,0:T(2,128)}, f32[2,2,128]{2,1,0:T(2,128)S(1)}, u32[]{:S(2)}) copy-start(f32[2,2,128]{2,1,0:T(2,128)S(1)} %get-tuple-element.85) | copy-start | bytes 6148
  18.1 20.0 %copy-start.73 = (f32[2,2,128]{2,1,0:T(2,128)}, f32[2,2,128]{2,1,0:T(2,128)S(1)}, u32[]{:S(2)}) copy-start(f32[2,2,128]{2,1,0:T(2,128)S(1)} %fusion.146) | copy-start | bytes 6148
  18.3 22.0 %copy-start.38 = (bf16[2,96,2,128]{3,1,2,0:T(8,128)(2,1)}, bf16[2,96,2,128]{3,1,2,0:T(8,128)(2,1)S(1)}, u32[]{:S(2)}) copy-start(bf16[2,96,2,128]{3,1,2,0:T(8,128)(2,1)S(1)} %convolution_convert_fusion.1) | copy-start | bytes 294916
  36.7 9.8 %slice-start.8 = ((s8[6291456]{0:T(1024)(128)(4,1)}), s8[4194304]{0:T(1024)(128)(4,1)S(1)}, s32[]{:S(2)}) async-start(s8[6291456]{0:T(1024)(128)(4,1)} %bitcast.306), calls=%async_computation.8 | async-start | bytes 8388608
  40.3 6.1 slice-start.9
  48.0 17.3 %copy-start.60 = (f32[1536]{0:T(1024)S(1)}, f32[1536]{0:T(1024)}, u32[]{:S(2)}) copy-start(f32[1536]{0:T(1024)} %get-tuple-element.43) | copy-start | bytes 18436
  65.3 6.0 copy-start.79
  66.6 8.1 %copy-start.13 = (bf16[128,1536]{1,0:T(8,128)(2,1)}, bf16[128,1536]{1,0:T(8,128)(2,1)S(1)}, u32[]{:S(2)}) copy-start(bf16[128,1536]{1,0:T(8,128)(2,1)S(1)} %multiply_convert_fusion.25) | copy-start | bytes 1179652
  73.2 20.1 %copy-start.56 = (bf16[128,4,48]{0,2,1:T(8,128)(2,1)}, bf16[128,4,48]{0,2,1:T(8,128)(2,1)S(1)}, u32[]{:S(2)}) copy-start(bf16[128,4,48]{0,2,1:T(8,128)(2,1)S(1)} %get-tuple-element.68) | copy-start | bytes 147460
  74.7 20.1 %copy-start.63 = (bf16[128,2,48]{0,2,1:T(8,128)(2,1)}, bf16[128,2,48]{0,2,1:T(8,128)(2,1)S(1)}, u32[]{:S(2)}) copy-start(bf16[128,2,48]{0,2,1:T(8,128)(2,1)S(1)} %get-tuple-element.76) | copy-start | bytes 73732
  74.7 20.1 %copy-start.64 = (bf16[128,2,48]{0,2,1:T(8,128)(2,1)}, bf16[128,2,48]{0,2,1:T(8,128)(2,1)S(1)}, u32[]{:S(2)}) copy-start(bf16[128,2,48]{0,2,1:T(8,128)(2,1)S(1)} %get-tuple-element.77) | copy-start | bytes 73732
  75.7 19.2 %copy-start.25 = (f32[2,2,128,128]{2,3,1,0:T(8,128)}, f32[2,2,128,128]{2,3,1,0:T(8,128)S(1)}, u32[]{:S(2)}) copy-start(f32[2,2,128,128]{2,3,1,0:T(8,128)S(1)} %get-tuple-element.88) | copy-start | bytes 786436
  75.7 19.1 %copy-start.74 = (f32[2,2,128]{2,1,0:T(2,128)}, f32[2,2,128]{2,1,0:T(2,128)S(1)}, u32[]{:S(2)}) copy-start(f32[2,2,128]{2,1,0:T(2,128)S(1)} %get-tuple-element.87) | copy-start | bytes 6148
  75.8 19.1 %copy-start.75 = (f32[2,2,128]{2,1,0:T(2,128)}, f32[2,2,128]{2,1,0:T(2,128)S(1)}, u32[]{:S(2)}) copy-start(f32[2,2,128]{2,1,0:T(2,128)S(1)} %fusion.147) | copy-start | bytes 6148
  76.0 21.1 %copy-start.40 = (bf16[2,96,2,128]{3,1,2,0:T(8,128)(2,1)}, bf16[2,96,2,128]{3,1,2,0:T(8,128)(2,1)S(1)}, u32[]{:S(2)}) copy-start(bf16[2,96,2,128]{3,1,2,0:T(8,128)(2,1)S(1)} %convolution_convert_fusion) | copy-start | bytes 294916
  93.4 9.8 %slice-start.10 = ((s8[6291456]{0:T(1024)(128)(4,1)}), s8[4194304]{0:T(1024)(128)(4,1)S(1)}, s32[]{:S(2)}) async-start(s8[6291456]{0:T(1024)(128)(4,1)} %bitcast.308), calls=%async_computation.10 | async-start | bytes 8388608
  97.1 6.1 slice-start.11
  103.2 17.6 %copy-start.22 = (f32[128,1536]{1,0:T(8,128)S(1)}, f32[128,1536]{1,0:T(8,128)}, u32[]{:S(2)}) copy-start(f32[128,1536]{1,0:T(8,128)} %param.14) | copy-start | bytes 2359300
  131.2 17.0 %copy-start.2 = (f32[128,1536]{1,0:T(8,128)S(1)}, f32[128,1536]{1,0:T(8,128)}, u32[]{:S(2)}) copy-start(f32[128,1536]{1,0:T(8,128)} %tensor_sum.10.base) | copy-start | bytes 2359300
  148.2 6.2 copy-start.7
  153.5 5.6 copy-start.28
  153.5 5.6 copy-start.46
  153.5 6.2 copy-start.57
  153.5 6.2 copy-start.59
  155.0 5.6 copy-start.15
  160.6 19.2 %copy-start.1 = (f32[128,1536]{1,0:T(8,128)S(1)}, f32[128,1536]{1,0:T(8,128)}, u32[]{:S(2)}) copy-start(f32[128,1536]{1,0:T(8,128)} %tensor_sum.9.base) | copy-start | bytes 2359300
  181.8 9.2 %slice-start.18 = ((s8[6291456]{0:T(1024)(128)(4,1)}), s8[4194304]{0:T(1024)(128)(4,1)S(1)}, s32[]{:S(2)}) async-start(s8[6291456]{0:T(1024)(128)(4,1)} %bitcast.372), calls=%async_computation.18 | async-start | bytes 8388608
  184.5 6.6 slice-start.19
  191.1 18.1 %copy-start = (f32[128,1536]{1,0:T(8,128)S(1)}, f32[128,1536]{1,0:T(8,128)}, u32[]{:S(2)}) copy-start(f32[128,1536]{1,0:T(8,128)} %tensor_sum.8.base) | copy-start | bytes 2359300
  209.2 5.6 copy-start.8
  213.9 5.8 copy-start.29
  213.9 5.8 copy-start.47
  215.6 6.5 copy-start.16
  217.4 5.1 copy-start.24
  222.1 17.9 %copy-start.3 = (f32[128,1536]{1,0:T(8,128)S(1)}, f32[128,1536]{1,0:T(8,128)}, u32[]{:S(2)}) copy-start(f32[128,1536]{1,0:T(8,128)} %base.1) | copy-start | bytes 2359300
  222.1 17.9 %copy-start.77 = (f32[128]{0:T(128)S(1)}, f32[128]{0:T(128)}, u32[]{:S(2)}) copy-start(f32[128]{0:T(128)} %copy-done.76) | copy-start | bytes 1540
  222.7 18.9 %copy-start.10 = (f32[128,1536]{1,0:T(8,128)S(1)}, f32[128,1536]{1,0:T(8,128)}, u32[]{:S(2)}) copy-start(f32[128,1536]{1,0:T(8,128)} %copy-done.9) | copy-start | bytes 2359300
  223.9 19.9 %copy-start.39 = (bf16[2,96,2,128]{3,1,2,0:T(8,128)(2,1)S(1)}, bf16[2,96,2,128]{3,1,2,0:T(8,128)(2,1)}, u32[]{:S(2)}) copy-start(bf16[2,96,2,128]{3,1,2,0:T(8,128)(2,1)} %copy-done.38) | copy-start | bytes 294916
  223.9 20.0 %copy-start.45 = (bf16[128,4,96]{0,2,1:T(8,128)(2,1)S(1)}, bf16[128,4,96]{0,2,1:T(8,128)(2,1)}, u32[]{:S(2)}) copy-start(bf16[128,4,96]{0,2,1:T(8,128)(2,1)} %copy-done.44) | copy-start | bytes 294916
  240.0 5.3 copy-start.41
  240.0 5.4 copy-start.43
  595.8 5.7 slice-start.20
  601.1 5.7 slice-start.4
  601.1 6.1 slice-start.12
  601.9 11.9 %copy-start.20 = (bf16[1024,1536]{1,0:T(8,128)(2,1)}, bf16[1024,1536]{1,0:T(8,128)(2,1)S(1)}, u32[]{:S(2)}) copy-start(bf16[1024,1536]{1,0:T(8,128)(2,1)S(1)} %convert_element_type.335) | copy-start | bytes 9437188
  601.9 6.5 slice-start.13
  606.9 6.9 %slice-start.22 = ((s8[6291456]{0:T(1024)(128)(4,1)}), s8[4194304]{0:T(1024)(128)(4,1)S(1)}, s32[]{:S(2)}) async-start(s8[6291456]{0:T(1024)(128)(4,1)} %bitcast.376), calls=%async_computation.22 | async-start | bytes 8388608
  608.3 5.4 copy-start.19
  608.3 5.4 slice-start.23
  613.8 12.0 %slice-start.2 = ((s8[6291456]{0:T(1024)(128)(4,1)}), s8[2097152]{0:T(1024)(128)(4,1)S(1)}, s32[]{:S(2)}) async-start(s8[6291456]{0:T(1024)(128)(4,1)} %bitcast.300), calls=%async_computation.2 | async-start | bytes 4194304
  618.8 7.1 %slice-start.3 = ((s8[6291456]{0:T(1024)(128)(4,1)}), s8[4194304]{0:T(1024)(128)(4,1)S(1)}, s32[]{:S(2)}) async-start(s8[6291456]{0:T(1024)(128)(4,1)} %bitcast.300), calls=%async_computation.3 | async-start | bytes 8388608
  625.9 6.0 slice-start
  625.9 6.4 slice-start.14
  626.3 5.6 slice-start.1
  626.3 6.0 slice-start.15
  631.8 5.7 slice-start.24
  632.3 5.3 slice-start.25
  (57 other events, 175.0 us)

commit v2 on v0

v2 whole, which is shorter than its diff:
```python
import functools

import jax
import jax.numpy as jnp
from jax import lax
from jax.experimental import pallas as pl
from jax.experimental.pallas import tpu as pltpu
from jax.sharding import PartitionSpec as P

HD = 96
LAYERS = 2
TILE = 256
ROWS = 16
MESH = pl.DeviceIdType.MESH


epsilon = 1e-05
rope_base = 100000.0
masked_score = -1e30
low = jnp.bfloat16
full = jnp.float32


def nn(a, b):
    return lax.dot_general(a, b, (((1,), (0,)), ((), ())), preferred_element_type=full)


def nt(a, b):
    return lax.dot_general(a, b, (((1,), (1,)), ((), ())), preferred_element_type=full)


def tn(a, b):
    return lax.dot_general(a, b, (((0,), (0,)), ((), ())), preferred_element_type=full)


def mlp_grads(gate_pre, up_pre, grad_act):
    sigmoid_gate = jax.nn.sigmoid(gate_pre)
    grad_gate_low = (
        grad_act * up_pre * sigmoid_gate * (1.0 + gate_pre * (1.0 - sigmoid_gate))
    ).astype(low)
    grad_up_low = (grad_act * gate_pre * sigmoid_gate).astype(low)
    activated = (gate_pre * sigmoid_gate * up_pre).astype(low)
    return grad_gate_low, grad_up_low, activated


def each(count, body):
    def step(i, carry):
        body(i)
        return carry

    lax.fori_loop(0, count, step, 0)


def columns(start, size):
    return pl.ds(pl.multiple_of(start, 128), size)


def layers_kernel(n, *refs):
    (
        hidden_in,
        cotangent,
        cosine,
        sine,
        allowed,
        attn_gain,
        mlp_gain,
        w_query,
        w_key,
        w_value,
        w_output,
        w_gate,
        w_up,
        w_down,
        hidden_out,
        grad_input,
        mixed_all,
        qkv_all,
        normed_two_all,
        g_all,
        normed_all,
        grad_att_all,
        gains_all,
        v_query,
        v_key,
        v_value,
        v_output,
        v_gate,
        v_up,
        v_down,
        stream,
        grads,
        upstream,
        normed_low,
        left_low,
        right_low,
        gate_pre,
        up_pre,
        query_t,
        key_t,
        value_t,
        mixed_t,
        logsum,
        mixed_out,
        qkv_out,
        normed_two_out,
        g_out,
        normed_out,
        grad_att_out,
        gains_out,
        gain_rows,
        wide,
        part,
        from_core,
        half,
        from_y,
        w_sem,
        sum_send,
        sum_recv,
        z_send,
        z_recv,
        x_send,
        x_recv,
        c_send,
        c_recv,
        a_send,
        a_recv,
        b_send,
        b_recv,
        local,
    ) = refs
    length, width = hidden_in.shape
    heads = w_query.shape[2] // HD
    kv_heads = w_key.shape[2] // HD
    share = heads // kv_heads
    hidden_units = w_gate.shape[2]
    piece = width // n
    side_width = width // 2
    chunks = side_width // TILE
    turn = HD // 2
    scale = HD ** (-0.5)

    dp = lax.axis_index("dp")
    tensor = lax.axis_index("tensor")
    core = tensor % 2
    side = dp % 2
    group = dp // 2
    groups = n // 2
    core_peer = (dp, tensor + 1 - 2 * core)
    y_peer = (dp, lax.rem(tensor + 2, 4))
    x_peer = (dp + 1 - 2 * side, tensor)

    stored = (w_query, w_key, w_value, w_output, w_gate, w_up, w_down)
    held = (v_query, v_key, v_value, v_output, v_gate, v_up, v_down)
    loads = {}
    for l in range(LAYERS):
        for i, (src, dst) in enumerate(zip(stored, held)):
            loads[l, i] = pltpu.make_async_copy(src.at[l], dst.at[l], w_sem.at[l, i])
            loads[l, i].start()

    barrier = pltpu.get_barrier_semaphore()
    greeted = [core_peer, y_peer] + [(lax.rem(dp + k, n), tensor) for k in range(1, n)]
    for peer in greeted:
        pl.semaphore_signal(barrier, inc=1, device_id=peer, device_id_type=MESH)
    pl.semaphore_wait(barrier, len(greeted))

    def remote(src, dst, s, r, peer):
        return pltpu.make_async_remote_copy(
            src_ref=src, dst_ref=dst, send_sem=s, recv_sem=r, device_id=peer, device_id_type=MESH
        )

    unsent = []
    unreceived = []

    ways = {}
    kinds = {
        "mixed": (0, mixed_out, mixed_all, False),
        "qkv": (1, qkv_out, qkv_all, False),
        "normed_two": (2, normed_two_out, normed_two_all, True),
        "g": (3, g_out, g_all, True),
    }

    def block(kind, l, index):
        _, _, everywhere, shared = kinds[kind]
        rows = pl.ds(pl.multiple_of(index * length, 8), length)
        if shared:
            return everywhere.at[l, rows, columns(core * side_width, side_width)]
        return everywhere.at[l, rows]

    def send_own(kind, l):
        a, own, everywhere, shared = kinds[kind]
        slot = a * LAYERS + l
        mine = own.at[l, :, columns(core * side_width, side_width)] if shared else own.at[l]
        for k in range(groups):
            if k == 0:
                c = remote(
                    mine, block(kind, l, dp), x_send.at[slot, 0], x_recv.at[slot, 0], x_peer
                )
            else:
                peer = (lax.rem(group + k, groups) * 2 + side, tensor)
                c = remote(
                    mine, block(kind, l, dp), z_send.at[slot, k], z_recv.at[slot, k], peer
                )
            c.start()
            ways[kind, l, "own", k] = c
            unsent.append(c)
        rows = pl.ds(pl.multiple_of(dp * length, 8), length)
        c = pltpu.make_async_copy(own.at[l], everywhere.at[l, rows], local.at[slot])
        c.start()
        unreceived.append(c.wait)

    def to_core(kind, l, index, k):
        a = kinds[kind][0]
        if kinds[kind][3]:
            slot = (a - 2) * LAYERS + l
            here = block(kind, l, index)
            c = remote(here, here, c_send.at[slot, k], c_recv.at[slot, k], core_peer)
            c.start()
            unsent.append(c)
            unreceived.append(c.wait_recv)

    def pass_on(kind, l):
        slot = kinds[kind][0] * LAYERS + l
        for k in range(1, groups):
            ways[kind, l, "own", k].wait_recv()
            source = lax.rem(group + groups - k, groups) * 2 + side
            here = block(kind, l, source)
            c = remote(here, here, x_send.at[slot, k], x_recv.at[slot, k], x_peer)
            c.start()
            ways[kind, l, "x", k] = c
            unsent.append(c)
            to_core(kind, l, source, k)

    def take_across(kind, l):
        for k in range(groups):
            ways[kind, l, "own" if k == 0 else "x", k].wait_recv()
            source = lax.rem(group + groups - k, groups) * 2 + 1 - side
            to_core(kind, l, source, groups + k)

    slices = {
        "normed": (0, normed_out, normed_all, True),
        "grad_att": (1, grad_att_out, grad_att_all, True),
        "gains": (2, gains_out, gains_all, False),
    }

    def sliced(kind, ref, l, index):
        if slices[kind][3]:
            rows = pl.ds(pl.multiple_of(core * (length // 2), 8), length // 2)
            return ref.at[l, index, rows]
        return ref.at[l, index]

    def send_slices(kind, l):
        b, own, everywhere, halves = slices[kind]
        slot = b * LAYERS + l
        for k in range(1, n):
            to = lax.rem(dp + k, n)
            c = remote(
                sliced(kind, own, l, to),
                sliced(kind, everywhere, l, dp),
                a_send.at[slot, k],
                a_recv.at[slot, k],
                (to, tensor),
            )
            c.start()
            ways[kind, l, k] = c
            unsent.append(c)
        c = pltpu.make_async_copy(
            own.at[l, dp], everywhere.at[l, dp], local.at[4 * LAYERS + slot]
        )
        c.start()
        unreceived.append(c.wait)

    def take_slices(kind, l):
        b, _, everywhere, halves = slices[kind]
        slot = b * LAYERS + l
        for k in range(1, n):
            ways[kind, l, k].wait_recv()
            if halves:
                source = lax.rem(dp + n - k, n)
                here = sliced(kind, everywhere, l, source)
                c = remote(here, here, b_send.at[slot, k], b_recv.at[slot, k], core_peer)
                c.start()
                unsent.append(c)
                unreceived.append(c.wait_recv)

    def cut(dst, l, src):
        for t in range(n):
            dst[l, t] = src[:, t * piece : (t + 1) * piece]

    def tensor_sum(j, tile, base, dest, meanwhile):
        def copy(stage, k, src, dst, peer):
            return remote(src, dst, sum_send.at[j, stage, k], sum_recv.at[j, stage, k], peer)

        def at(k):
            return pl.ds(pl.multiple_of(k * TILE, 128), TILE)

        def mine(k):
            return columns(core * side_width + k * TILE, TILE)

        def other(k):
            return columns((1 - core) * side_width + k * TILE, TILE)

        def first(k):
            return copy(0, k, part.at[:, at(k)], from_core.at[j, :, at(k)], core_peer)

        def second(k):
            return copy(1, k, half.at[:, at(k)], from_y.at[j, :, at(k)], y_peer)

        def third(k):
            return copy(2, k, dest.at[:, mine(k)], dest.at[:, mine(k)], core_peer)

        def begin(k):
            part[:, at(k)] = tile(other(k))
            first(k).start()

        def middle(k):
            own = tile(mine(k))
            first(k).wait_recv()
            half[:, at(k)] = own + from_core[j, :, at(k)]
            second(k).start()

        def finish(k):
            second(k).wait_recv()
            total = half[:, at(k)] + from_y[j, :, at(k)]
            if base is not None:
                total = base[:, mine(k)] + total
            dest[:, mine(k)] = total
            third(k).start()

        def settle(k):
            third(k).wait_recv()
            first(k).wait_send()
            second(k).wait_send()
            third(k).wait_send()

        each(chunks, begin)
        each(chunks, middle)
        meanwhile()
        each(chunks, finish)
        each(chunks, settle)

    def inverse_rms(values):
        return lax.rsqrt(jnp.mean(values * values, axis=-1, keepdims=True) + epsilon)

    def normalize(src, gain, l, out, out_wide):
        def rows_of(i):
            rows = pl.ds(pl.multiple_of(i * ROWS, ROWS), ROWS)
            values = src[rows, :]
            normed = (values * inverse_rms(values) * gain[l : l + 1, :]).astype(low)
            out[rows, :] = normed
            out_wide[rows, :] = normed.astype(full)

        each(length // ROWS, rows_of)

    def norm_backward(grad, values_ref, gain, l, row, before, out, out_low, out_wide):
        def rows_of(i, total):
            rows = pl.ds(pl.multiple_of(i * ROWS, ROWS), ROWS)
            values = values_ref[rows, :]
            grad_normed = grad[rows, :]
            inverse = inverse_rms(values)
            normalized = values * inverse
            term = grad_normed * normalized
            total = total + term[:8] + term[8:]
            scaled = grad_normed * gain[l : l + 1, :]
            back = inverse * (
                scaled - normalized * jnp.mean(scaled * normalized, axis=-1, keepdims=True)
            )
            after = before[rows, :] + back
            out[rows, :] = after
            if out_low is not None:
                after_low = after.astype(low)
                out_low[rows, :] = after_low
                out_wide[rows, :] = after_low.astype(full)
            return total

        total = lax.fori_loop(0, length // ROWS, rows_of, jnp.zeros((8, width), full))
        gain_rows[row : row + 1, :] = jnp.sum(total, axis=0, keepdims=True)

    def turned(values, direction):
        u, w = values[:turn], values[turn:]
        c, s = cosine[...], sine[...]
        return jnp.concatenate([u * c - direction * w * s, w * c + direction * u * s], axis=0)

    def head(ref, l, h):
        return ref[l, h * HD : (h + 1) * HD, :]

    def scores_t(l, h):
        raw = tn(head(key_t, l, h // share), head(query_t, l, h)) * scale
        return jnp.where(allowed[...] > 0.5, raw, masked_score)

    def attend(l):
        for i in range(3):
            loads[l, i].wait()
        source = normed_low[...]
        for ref, dst, count, rope in (
            (v_query, query_t, heads, True),
            (v_key, key_t, kv_heads, True),
            (v_value, value_t, kv_heads, False),
        ):
            projected = jnp.transpose(nn(source, ref[l]))
            for h in range(count):
                values = projected[h * HD : (h + 1) * HD]
                values = turned(values, 1.0) if rope else values
                dst[l, h * HD : (h + 1) * HD, :] = values.astype(low)
        for h in range(heads):
            scores = scores_t(l, h)
            row_max = jnp.max(scores, axis=0, keepdims=True)
            exponent = jnp.exp(scores - row_max)
            row_total = jnp.sum(exponent, axis=0, keepdims=True)
            probabilities = (exponent / row_total).astype(low)
            logsum[l, h : h + 1, :] = row_max + jnp.log(row_total)
            mixed = nn(head(value_t, l, h // share), probabilities)
            mixed_t[l, h * HD : (h + 1) * HD, :] = mixed.astype(low).astype(full)
        mixed = jnp.transpose(mixed_t[l])
        mixed_out[l] = mixed
        left_low[:, : heads * HD] = mixed.astype(low)

    def attention_back(l):
        grad_mixed_t = jnp.transpose(nt(normed_low[...], v_output[l]).astype(low).astype(full))
        for g in range(kv_heads):
            grad_value = jnp.zeros((HD, length), full)
            grad_key = jnp.zeros((HD, length), full)
            for h in range(g * share, (g + 1) * share):
                grad_mixed = grad_mixed_t[h * HD : (h + 1) * HD]
                grad_mixed_low = grad_mixed.astype(low)
                again = jnp.exp(scores_t(l, h) - logsum[l, h : h + 1, :])
                grad_value += nt(grad_mixed_low, again.astype(low))
                grad_probs = tn(head(value_t, l, g), grad_mixed_low)
                row_dot = jnp.sum(grad_mixed * head(mixed_t, l, h), axis=0, keepdims=True)
                grad_scores = (again * (grad_probs - row_dot) * scale).astype(low)
                grad_query = nn(head(key_t, l, g), grad_scores)
                grad_key += nt(head(query_t, l, h), grad_scores)
                wide[h * HD : (h + 1) * HD, :] = turned(grad_query, -1.0).astype(low).astype(full)
            at = (heads + g) * HD
            wide[at : at + HD, :] = turned(grad_key, -1.0).astype(low).astype(full)
            at = (heads + kv_heads + g) * HD
            wide[at : at + HD, :] = grad_value.astype(low).astype(full)
        rows = jnp.transpose(wide[...])
        qkv_out[l] = rows
        left_low[:, : rows.shape[1]] = rows.astype(low)

    step = hidden_units // 2
    nothing = lambda: None

    def attention_layer(l, meanwhile):
        normalize(stream.at[2 * l], attn_gain, l, normed_low, normed_two_out.at[l])
        cut(normed_out, l, normed_two_out.at[l])
        send_slices("normed", l)
        attend(l)
        send_own("mixed", l)
        loads[l, 3].wait()
        tensor_sum(
            2 * l,
            lambda at: nn(left_low[:, : heads * HD], v_output[l, :, at]),
            stream.at[2 * l],
            stream.at[2 * l + 1],
            meanwhile,
        )

    def mlp_layer(l, meanwhile):
        normalize(stream.at[2 * l + 1], mlp_gain, l, normed_low, normed_two_out.at[l])
        send_own("normed_two", l)
        loads[l, 4].wait()
        loads[l, 5].wait()

        def units(i):
            at = columns(i * TILE, TILE)
            source = normed_low[...]
            gate = nn(source, v_gate[l, :, at])
            up = nn(source, v_up[l, :, at])
            gate_pre[l, :, at] = gate
            up_pre[l, :, at] = up
            left_low[:, at] = (gate * jax.nn.sigmoid(gate) * up).astype(low)

        each(hidden_units // TILE, units)
        loads[l, 6].wait()
        tensor_sum(
            2 * l + 1,
            lambda at: nn(left_low[...], v_down[l, :, at]),
            stream.at[2 * l + 1],
            stream.at[2 * l + 2],
            meanwhile,
        )

    def mlp_back(l, meanwhile):
        def units(i):
            at = columns(i * TILE, TILE)
            grad_act = nt(normed_low[...], v_down[l, at, :])
            left, right, _ = mlp_grads(gate_pre[l, :, at], up_pre[l, :, at], grad_act)
            left_low[:, at] = left
            right_low[:, at] = right

        each(hidden_units // TILE, units)
        j = 2 * LAYERS + 2 * (LAYERS - 1 - l)
        tensor_sum(
            j,
            lambda at: nt(left_low[...], v_gate[l, at, :]) + nt(right_low[...], v_up[l, at, :]),
            None,
            grads.at[j - 2 * LAYERS],
            meanwhile,
        )
        norm_backward(
            grads.at[j - 2 * LAYERS],
            stream.at[2 * l + 1],
            mlp_gain,
            l,
            LAYERS + l,
            upstream,
            upstream,
            normed_low,
            part_wide,
        )
        cut(grad_att_out, l, part_wide)
        send_slices("grad_att", l)

    part_wide = grads.at[2 * LAYERS]

    def attention_layer_back(l, meanwhile):
        attention_back(l)
        send_own("qkv", l)
        j = 2 * LAYERS + 2 * (LAYERS - 1 - l) + 1
        q_end, k_end = heads * HD, (heads + kv_heads) * HD
        v_end = (heads + 2 * kv_heads) * HD
        tensor_sum(
            j,
            lambda at: nt(left_low[:, :q_end], v_query[l, at, :])
            + nt(left_low[:, q_end:k_end], v_key[l, at, :])
            + nt(left_low[:, k_end:v_end], v_value[l, at, :]),
            None,
            grads.at[j - 2 * LAYERS],
            meanwhile,
        )
        last = l == 0
        norm_backward(
            grads.at[j - 2 * LAYERS],
            stream.at[2 * l],
            attn_gain,
            l,
            l,
            upstream,
            grad_input if last else upstream,
            None if last else normed_low,
            None if last else g_out.at[l - 1],
        )
        if not last:
            send_own("g", l - 1)

    stream[0] = hidden_in[...]
    upstream[...] = cotangent[...]
    g_out[LAYERS - 1] = cotangent[...].astype(low).astype(full)
    send_own("g", LAYERS - 1)
    gain_rows[...] = jnp.zeros_like(gain_rows)

    def steps(*calls):
        def run():
            for call, kind, l in calls:
                call(kind, l)

        return run

    attention_layer(0, nothing)
    mlp_layer(0, steps((pass_on, "g", 1), (take_slices, "normed", 0)))
    attention_layer(1, steps((pass_on, "mixed", 0), (take_across, "g", 1)))
    mlp_layer(1, steps((take_across, "mixed", 0)))
    hidden_out[...] = stream[2 * LAYERS]
    normed_low[...] = g_out[LAYERS - 1].astype(low)
    mlp_back(1, steps((pass_on, "normed_two", 0), (take_slices, "normed", 1)))
    attention_layer_back(1, steps((pass_on, "mixed", 1), (take_across, "normed_two", 0)))
    mlp_back(0, steps((pass_on, "normed_two", 1), (take_across, "mixed", 1)))
    attention_layer_back(0, steps((pass_on, "qkv", 1), (take_slices, "grad_att", 1)))
    cut(gains_out, 0, gain_rows)
    send_slices("gains", 0)
    for call, kind, l in (
        (take_across, "normed_two", 1),
        (pass_on, "g", 0),
        (take_across, "qkv", 1),
        (pass_on, "qkv", 0),
        (take_across, "g", 0),
        (take_slices, "grad_att", 0),
        (take_across, "qkv", 0),
        (take_slices, "gains", 0),
    ):
        call(kind, l)
    for wait in unreceived:
        wait()
    for c in unsent:
        c.wait_send()


def layers(n, hidden_in, cotangent, cosine, sine, allowed, attn_gain, mlp_gain, weights):
    length, width = hidden_in.shape
    w_query, w_key, w_value, w_output, w_gate, w_up, w_down = weights
    q_width, kv_width, hidden_units = w_query.shape[2], w_key.shape[2], w_gate.shape[2]
    qkv_width = q_width + 2 * kv_width
    piece = width // n
    f32 = lambda *shape: jax.ShapeDtypeStruct(shape, full)
    out_shape = [
        f32(length, width),
        f32(length, width),
        f32(LAYERS, n * length, q_width),
        f32(LAYERS, n * length, qkv_width),
        f32(LAYERS, n * length, width),
        f32(LAYERS, n * length, width),
        f32(LAYERS, n, length, piece),
        f32(LAYERS, n, length, piece),
        f32(1, n, 8, piece),
    ]
    vmem = pl.BlockSpec(memory_space=pltpu.VMEM)
    anywhere = pl.BlockSpec(memory_space=pl.ANY)
    dma = pltpu.SemaphoreType.DMA
    keep = lambda dtype, *shape: pltpu.VMEM(shape, dtype)
    sums = 4 * LAYERS
    chunks = width // 2 // TILE
    return pl.pallas_call(
        functools.partial(layers_kernel, n),
        out_shape=out_shape,
        in_specs=[vmem] * 7 + [anywhere] * 7,
        out_specs=[vmem] * 2 + [anywhere] * 7,
        scratch_shapes=[keep(low, *w.shape) for w in weights]
        + [
            keep(full, 2 * LAYERS + 1, length, width),
            keep(full, 2 * LAYERS + 1, length, width),
            keep(full, length, width),
            keep(low, length, width),
            keep(low, length, hidden_units),
            keep(low, length, hidden_units),
            keep(full, LAYERS, length, hidden_units),
            keep(full, LAYERS, length, hidden_units),
            keep(low, LAYERS, q_width, length),
            keep(low, LAYERS, kv_width, length),
            keep(low, LAYERS, kv_width, length),
            keep(full, LAYERS, q_width, length),
            keep(full, LAYERS, 8, length),
            keep(full, LAYERS, length, q_width),
            keep(full, LAYERS, length, qkv_width),
            keep(full, LAYERS, length, width),
            keep(full, LAYERS, length, width),
            keep(full, LAYERS, n, length, piece),
            keep(full, LAYERS, n, length, piece),
            keep(full, 1, n, 8, piece),
            keep(full, 8, width),
            keep(full, qkv_width, length),
            keep(full, length, width // 2),
            keep(full, sums, length, width // 2),
            keep(full, length, width // 2),
            keep(full, sums, length, width // 2),
            dma((LAYERS, 7)),
            dma((sums, 3, chunks)),
            dma((sums, 3, chunks)),
            dma((4 * LAYERS, n // 2)),
            dma((4 * LAYERS, n // 2)),
            dma((4 * LAYERS, n // 2)),
            dma((4 * LAYERS, n // 2)),
            dma((2 * LAYERS, n)),
            dma((2 * LAYERS, n)),
            dma((3 * LAYERS, n)),
            dma((3 * LAYERS, n)),
            dma((2 * LAYERS, n)),
            dma((2 * LAYERS, n)),
            dma((7 * LAYERS,)),
        ],
        compiler_params=pltpu.CompilerParams(
            collective_id=0, has_side_effects=True, vmem_limit_bytes=66_000_000
        ),
        name="layers",
    )(hidden_in, cotangent, cosine, sine, allowed, attn_gain, mlp_gain, *weights)


def shards(
    hidden_in,
    cotangent,
    segment_ids,
    positions,
    w_query,
    w_key,
    w_value,
    w_output,
    w_gate,
    w_up,
    w_down,
    attn_gain,
    mlp_gain,
):
    n = lax.axis_size("dp")
    dp = lax.axis_index("dp")
    weights = (w_query, w_key, w_value, w_output, w_gate, w_up, w_down)
    length, width = hidden_in.shape
    piece = width // n
    half_dim = HD // 2
    frequencies = rope_base ** (-(jnp.arange(half_dim).astype(jnp.float32) * 2.0 / HD))
    angles = frequencies[:, None] * positions[0].astype(jnp.float32)[None, :]
    segments = segment_ids[0]
    token_order = jnp.arange(length)
    allowed = (segments[:, None] == segments[None, :]) & (
        token_order[:, None] <= token_order[None, :]
    )
    hidden, grad_input, mixed_all, qkv_all, normed_two_all, g_all, normed_all, grad_att_all, gains = (
        layers(
            n,
            hidden_in,
            cotangent,
            jnp.cos(angles),
            jnp.sin(angles),
            allowed.astype(jnp.float32),
            attn_gain,
            mlp_gain,
            weights,
        )
    )
    heads = w_query.shape[2]
    kv = w_key.shape[2]
    grads = [[] for _ in range(7)]
    for l in range(LAYERS):
        mixed = mixed_all[l].astype(low)
        qkv = qkv_all[l].astype(low)
        normed_two = normed_two_all[l].astype(low)
        g_low = g_all[l].astype(low)
        normed = normed_all[l].reshape(n * length, piece).astype(low)
        grad_att = grad_att_all[l].reshape(n * length, piece).astype(low)
        gate_pre = nn(normed_two, w_gate[l])
        up_pre = nn(normed_two, w_up[l])
        grad_act = nt(g_low, w_down[l])
        grad_gate_low, grad_up_low, activated = mlp_grads(gate_pre, up_pre, grad_act)
        my_normed_two = lax.dynamic_slice_in_dim(normed_two, dp * piece, piece, 1)
        my_g = lax.dynamic_slice_in_dim(g_low, dp * piece, piece, 1)
        grad_qkv = tn(normed, qkv)
        grads[0].append(grad_qkv[:, :heads])
        grads[1].append(grad_qkv[:, heads : heads + kv])
        grads[2].append(grad_qkv[:, heads + kv :])
        grads[3].append(tn(mixed, grad_att))
        grads[4].append(tn(my_normed_two, grad_gate_low))
        grads[5].append(tn(my_normed_two, grad_up_low))
        grads[6].append(tn(activated, my_g))
    gain_sums = jnp.sum(gains[0], axis=0)
    return (
        hidden,
        grad_input,
        *[jnp.stack(g) for g in grads],
        gain_sums[:LAYERS],
        gain_sums[LAYERS : 2 * LAYERS],
    )


def solution(mesh):
    return jax.shard_map(
        shards,
        mesh=mesh,
        in_specs=(
            P("dp", None),
            P("dp", None),
            P("dp", None),
            P("dp", None),
            P(None, None, "tensor"),
            P(None, None, "tensor"),
            P(None, None, "tensor"),
            P(None, "tensor", None),
            P(None, None, "tensor"),
            P(None, None, "tensor"),
            P(None, "tensor", None),
            P(),
            P(),
        ),
        out_specs=(
            P("dp", None),
            P("dp", None),
            P(None, "dp", "tensor"),
            P(None, "dp", "tensor"),
            P(None, "dp", "tensor"),
            P(None, "tensor", "dp"),
            P(None, "dp", "tensor"),
            P(None, "dp", "tensor"),
            P(None, "tensor", "dp"),
            P(None, "dp"),
            P(None, "dp"),
        ),
        check_vma=False,
    )
```

time: 1690 us -> 408 us (0.24)
  waiting for transfers between devices: 1440 us -> 0 us
  Pallas kernels: 0 us -> 319 us
  local copies, waits for them, and re-layouts: 76.1 us -> 20.9 us
  other arithmetic: 63.4 us -> 12.7 us
  matrix products: 79.1 us -> 48.9 us
    unnamed x20 -> x0, waiting for transfers between devices: 686 us -> none
    reduce_scatter x3 -> x0, waiting for transfers between devices: 515 us -> none  [the longest x1 211 us: shards(): lax.psum_scatter(stacked[4], 'dp', scatter_dimension=1, tiled=True)]
    pallas_call x0 -> x1, Pallas kernels: none -> 319 us  [layers(): pl.pallas_call(functools.partial(layers_kernel, n), out_shape=out_shape,...]
    psum x7 -> x0, waiting for transfers between devices: 240 us -> none  [the longest x2 71.7 us: layer_forward(): output = attended + lax.psum(mlp_part, 'tensor')]
    dot_general x54 -> x16, matrix products: 79.1 us -> 48.9 us  [the longest x10 21.3 us: tn(): lax.dot_general(a, b, (((0,), (0,)), ((), ())), preferred_element_type=full)]
    unnamed x241 -> x32, local copies, waits for them, and re-layouts: 38.5 us -> 8.56 us
    another operation x6 -> x3, local copies, waits for them, and re-layouts: 27.7 us -> 0.26 us  [shards(): jnp.stack(g)]
    another operation x13 -> x10, other arithmetic: 36 us -> 8.77 us  [the longest x6 6.45 us: shards(): jnp.stack(g)]
  transfers between devices with their start and end apart: 15 -> 0, of which waited for: 14 -> 0; matrix products, arithmetic and copies ran while one was open for 8% -> 0% of each run, Pallas kernels for 0% -> 0%
where the time goes in v2:
time: 408 us; the launch traced here: 402 us
  Pallas kernels  319 us (78%)
  matrix products  48.9 us (12%)
  local copies, waits for them, and re-layouts  20.9 us (5%)
  other arithmetic  12.7 us (3%)
    pallas_call x1, Pallas kernels, layers(): pl.pallas_call(functools.partial(layers_kernel, n), out_shape=out_shape,...  319 us
    dot_general x10, matrix products, tn(): lax.dot_general(a, b, (((0,), (0,)), ((), ())), preferred_element_type=full)  21.3 us
    dot_general x4, matrix products, nn(): lax.dot_general(a, b, (((1,), (0,)), ((), ())), preferred_element_type=full)  18.9 us
    slice x1, local copies, waits for them, and re-layouts, shards(): g_low = g_all[l].astype(low)  11.3 us
    dot_general x2, matrix products, nt(): lax.dot_general(a, b, (((1,), (1,)), ((), ())), preferred_element_type=full)  8.71 us
    unnamed x32, local copies, waits for them, and re-layouts  8.56 us

profile of v2, /device:TPU:0, one launch (start us, length us, event | category | flops | bytes accessed | tf_op | source)
XLA Modules:
  0.0 402.1 jit_solution(9543044758668235267)
XLA Ops:
  0.6 0.7 convert_bitcast_fusion
  1.3 0.8 multiply_sine_fusion
  2.1 1.4 fusion.51.refs_4_
  3.6 2.5 copy.24.refs_8_
  6.1 2.5 copy.25.refs_9_
  8.6 318.8 %layers.1 = (f32[128,1536]{1,0:T(8,128)}, f32[128,1536]{1,0:T(8,128)}, f32[2,1024,384]{2,1,0:T(8,128)}, f32[2,1024,768]{2,1,0:T(8,128)}, f32[2,1024,1536]{2,1,0:...) custom-call(f32[128,1536]{1,0:T(8,128)} %refs_0_.1, ...), custom_call_target="tpu_custom_call" | custom-call | tf_op jit(solution)/shard_map/layers/pallas_call | solution.py:613
  327.3 0.0 copy-start.2
  327.3 1.0 reduce_sum.9
  328.4 0.6 fusion.68
  328.9 1.7 convert.16
  330.7 0.0 copy-start.1
  330.7 0.1 fusion.67
  330.7 0.0 copy-done.2
  330.8 0.1 convert.19
  330.9 0.0 slice-start
  330.9 0.1 fusion.66
  331.0 1.6 copy-done.1
  332.6 0.2 convert.18
  332.7 0.4 convolution_bitcast_fusion
  333.1 0.4 convolution_bitcast_fusion.1
  333.6 0.9 pad_maximum_fusion.4
  334.4 0.0 slice-done
  334.4 0.2 slice-done.1
  334.6 0.3 convert.17
  334.9 0.5 fusion.30
  335.4 0.5 fusion.31
  335.9 0.1 slice_bitcast_fusion.11
  336.1 0.1 slice_bitcast_fusion.10
  336.2 0.9 pad_maximum_fusion.3
  337.1 0.9 pad_maximum_fusion.5
  338.0 11.3 %fusion.64 = (bf16[1,1024,1536]{2,1,0:T(8,128)(2,1)S(1)}, bf16[1,1024,1536]{2,1,0:T(8,128)(2,1)S(1)}, bf16[1,1024,1536]{2,1,0:T(8,128)(2,1)}, bf16[1,1024,1536]{2,1,0:T(8,128)(2,1)S(1)}) fusion(f32[2,1024,1536]{2,1,0:T(8,128)} %get-tuple-element.27, f32[2,1024,1536]{2,1,0:T(8,128)} %get-tuple-element.26), kind=kLoop, calls=%fused_computation.100 | loop fusion | bytes 25165824 | tf_op jit(solution)/shard_map/slice | solution.py:716
  349.3 0.0 slice-done.2
  349.3 0.0 slice-done.3
  349.4 0.0 slice-start.4
  349.4 7.1 %fusion = f32[1024,1024]{1,0:T(8,128)} fusion(bf16[1,1024,1536]{2,1,0:T(8,128)(2,1)} %get-tuple-element.45, bf16[2,1536,1024]{2,1,0:T(8,128)(2,1)S(1)} %bitcast.104), kind=kOutput, calls=%fused_computation.12 | convolution fusion | flops 3221225472 | bytes 10485760 | tf_op jit(solution)/shard_map/dot_general | solution.py:25
  356.4 3.4 fusion.9
  359.8 0.0 slice-done.4
  359.9 0.0 slice-done.5
  359.9 3.4 fusion.15
  363.3 0.0 slice-start.6
  363.3 1.6 fusion.37
  364.9 0.0 copy-start
  364.9 0.0 slice-start.7
  364.9 5.3 %fusion.6 = f32[1024,1024]{1,0:T(8,128)} fusion(bf16[1,1024,1536]{2,1,0:T(8,128)(2,1)S(1)} %get-tuple-element.30, bf16[2,1024,1536]{2,1,0:T(8,128)(2,1)S(1)} %bitcast.106), kind=kOutput, calls=%fused_computation.18 | convolution fusion | flops 3221225472 | bytes 10485760 | tf_op jit(solution)/shard_map/dot_general | solution.py:29
  370.2 0.0 copy-done
  370.2 5.0 %fusion.36 = f32[1,192,1024]{2,1,0:T(8,128)S(1)} fusion(f32[1024,1024]{1,0:T(8,128)} %fusion.6, f32[1024,1024]{1,0:T(8,128)} %fusion, bf16[1,1024,1536]{2,1,0:T(8,128)(2,1)S(1)} %copy-done, s32[]{:T(128)S(6)} %select_n.2), kind=kOutput, calls=%fused_computation.53 | convolution fusion | flops 408944640 | bytes 9699332 | tf_op jit(solution)/shard_map/dot_general | solution.py:33
  375.2 1.3 pad_maximum_fusion.1
  376.5 0.0 slice-done.6
  376.5 0.0 slice-done.7
  376.5 5.0 %fusion.2 = f32[1024,1024]{1,0:T(8,128)} fusion(bf16[1,1024,1536]{2,1,0:T(8,128)(2,1)S(1)} %copy-done, bf16[2,1536,1024]{2,1,0:T(8,128)(2,1)S(1)} %bitcast.108), kind=kOutput, calls=%fused_computation.14 | convolution fusion | flops 3221225472 | bytes 10485760 | tf_op jit(solution)/shard_map/dot_general | solution.py:25
  381.5 0.0 copy-done.5
  381.5 5.5 %fusion.32 = f32[1,192,1024]{2,1,0:T(8,128)S(1)} fusion(f32[1024,1024]{1,0:T(8,128)S(1)} %copy-done.5, f32[1024,1024]{1,0:T(8,128)} %fusion.6, f32[1024,1024]{1,0:T(8,128)} %fusion.2, bf16[1,1024,1536]{2,1,0:T(8,128)(2,1)S(1)} %copy-done, s32[]{:T(128)S(6)} %select_n.2), kind=kOutput, calls=%fused_computation.49 | convolution fusion | flops 413138944 | bytes 13893636 | tf_op jit(solution)/shard_map/dot_general | solution.py:33
  387.0 3.7 fusion.34
  390.7 3.4 fusion.11
  394.1 2.2 fusion.33
  396.3 1.6 fusion.35
  397.9 0.0 copy-start.4
  397.9 0.0 copy-start.3
  397.9 1.2 pad_maximum_fusion.2
  399.1 1.2 pad_maximum_fusion
  400.4 0.0 copy-done.4
  400.4 0.9 copy.28
  401.3 0.0 copy-done.3
  401.3 0.9 copy.29
  (11 shorter events, 0.1 us)
Async XLA Ops:
  327.3 3.4 copy-start.2
  330.7 1.9 copy-start.1
  330.9 3.5 slice-start
  332.5 2.1 slice-start.1
  337.1 12.3 %slice-start.2 = ((s8[6291456]{0:T(1024)(128)(4,1)}), s8[4194304]{0:T(1024)(128)(4,1)S(1)}, s32[]{:S(2)}) async-start(s8[6291456]{0:T(1024)(128)(4,1)} %bitcast.103), calls=%async_computation.2 | async-start | bytes 8388608
  338.0 11.3 %slice-start.3 = ((s8[6291456]{0:T(1024)(128)(4,1)}), s8[2097152]{0:T(1024)(128)(4,1)S(1)}, s32[]{:S(2)}) async-start(s8[6291456]{0:T(1024)(128)(4,1)} %bitcast.103), calls=%async_computation.3 | async-start | bytes 4194304
  349.4 10.5 %slice-start.4 = ((s8[6291456]{0:T(1024)(128)(4,1)}), s8[4194304]{0:T(1024)(128)(4,1)S(1)}, s32[]{:S(2)}) async-start(s8[6291456]{0:T(1024)(128)(4,1)} %bitcast.105), calls=%async_computation.4 | async-start | bytes 8388608
  356.4 3.4 slice-start.5
  363.3 13.2 %slice-start.6 = ((s8[6291456]{0:T(1024)(128)(4,1)}), s8[4194304]{0:T(1024)(128)(4,1)S(1)}, s32[]{:S(2)}) async-start(s8[6291456]{0:T(1024)(128)(4,1)} %bitcast.107), calls=%async_computation.6 | async-start | bytes 8388608
  364.9 5.3 %copy-start = (bf16[1,1024,1536]{2,1,0:T(8,128)(2,1)S(1)}, bf16[1,1024,1536]{2,1,0:T(8,128)(2,1)}, u32[]{:S(2)}) copy-start(bf16[1,1024,1536]{2,1,0:T(8,128)(2,1)} %get-tuple-element.45) | copy-start | bytes 9437188
  364.9 11.6 %slice-start.7 = ((s8[6291456]{0:T(1024)(128)(4,1)}), s8[2097152]{0:T(1024)(128)(4,1)S(1)}, s32[]{:S(2)}) async-start(s8[6291456]{0:T(1024)(128)(4,1)} %bitcast.107), calls=%async_computation.7 | async-start | bytes 4194304
  376.5 5.0 %copy-start.5 = (f32[1024,1024]{1,0:T(8,128)S(1)}, f32[1024,1024]{1,0:T(8,128)}, u32[]{:S(2)}) copy-start(f32[1024,1024]{1,0:T(8,128)} %fusion) | copy-start | bytes 12582916
  397.9 2.5 copy-start.4
  397.9 3.4 copy-start.3

commit v3 on v2

--- a/solution.py
+++ b/solution.py
@@ -1,4 +1,5 @@
 import functools
+import math
 
 import jax
 import jax.numpy as jnp
@@ -11,6 +12,8 @@
 LAYERS = 2
 TILE = 256
 ROWS = 16
+TOKENS = 256
+SHARED_Y = (("normed_two", 0), ("g", 0))
 MESH = pl.DeviceIdType.MESH
 
 
@@ -73,6 +76,13 @@
         w_down,
         hidden_out,
         grad_input,
+        grad_q,
+        grad_k,
+        grad_v,
+        grad_o,
+        grad_g,
+        grad_u,
+        grad_d,
         mixed_all,
         qkv_all,
         normed_two_all,
@@ -104,8 +114,7 @@
         qkv_out,
         normed_two_out,
         g_out,
-        normed_out,
-        grad_att_out,
+        slices_out,
         gains_out,
         gain_rows,
         wide,
@@ -113,6 +122,23 @@
         from_core,
         half,
         from_y,
+        token_a,
+        token_b,
+        low_a,
+        low_b,
+        cut_a,
+        cut_b,
+        sum_g,
+        sum_u,
+        sum_d,
+        state_qkv,
+        state_mixed,
+        state_a,
+        state_b,
+        sum_q,
+        sum_k,
+        sum_v,
+        sum_o,
         w_sem,
         sum_send,
         sum_recv,
@@ -126,11 +152,17 @@
         a_recv,
         b_send,
         b_recv,
+        y_send,
+        y_recv,
+        d_send,
+        d_recv,
         local,
+        edge,
+        fetch,
     ) = refs
     length, width = hidden_in.shape
     heads = w_query.shape[2] // HD
-    kv_heads = w_key.shape[2] // HD
+    kv_heads = w_key.shape[1] // HD
     share = heads // kv_heads
     hidden_units = w_gate.shape[2]
     piece = width // n
@@ -157,6 +189,13 @@
             loads[l, i] = pltpu.make_async_copy(src.at[l], dst.at[l], w_sem.at[l, i])
             loads[l, i].start()
 
+    arriving = [
+        pltpu.make_async_copy(hidden_in, stream.at[0], edge.at[0]),
+        pltpu.make_async_copy(cotangent, upstream, edge.at[1]),
+    ]
+    for c in arriving:
+        c.start()
+
     barrier = pltpu.get_barrier_semaphore()
     greeted = [core_peer, y_peer] + [(lax.rem(dp + k, n), tensor) for k in range(1, n)]
     for peer in greeted:
@@ -169,7 +208,8 @@
         )
 
     unsent = []
-    unreceived = []
+    missing = {}
+    leaving = {}
 
     ways = {}
     kinds = {
@@ -179,9 +219,14 @@
         "g": (3, g_out, g_all, True),
     }
 
-    def block(kind, l, index):
+    quarter_width = width // 4
+
+    def block(kind, l, index, owner=None):
         _, _, everywhere, shared = kinds[kind]
         rows = pl.ds(pl.multiple_of(index * length, 8), length)
+        if (kind, l) in SHARED_Y:
+            at = tensor if owner is None else owner
+            return everywhere.at[l, rows, columns(at * quarter_width, quarter_width)]
         if shared:
             return everywhere.at[l, rows, columns(core * side_width, side_width)]
         return everywhere.at[l, rows]
@@ -189,7 +234,12 @@
     def send_own(kind, l):
         a, own, everywhere, shared = kinds[kind]
         slot = a * LAYERS + l
-        mine = own.at[l, :, columns(core * side_width, side_width)] if shared else own.at[l]
+        if (kind, l) in SHARED_Y:
+            mine = own.at[l, :, columns(tensor * quarter_width, quarter_width)]
+        elif shared:
+            mine = own.at[l, :, columns(core * side_width, side_width)]
+        else:
+            mine = own.at[l]
         for k in range(groups):
             if k == 0:
                 c = remote(
@@ -206,39 +256,78 @@
         rows = pl.ds(pl.multiple_of(dp * length, 8), length)
         c = pltpu.make_async_copy(own.at[l], everywhere.at[l, rows], local.at[slot])
         c.start()
-        unreceived.append(c.wait)
-
-    def to_core(kind, l, index, k):
+        missing.setdefault((kind, l), []).append(c.wait)
+
+    def source_of(i):
+        if i < groups - 1:
+            return lax.rem(group + groups - 1 - i, groups) * 2 + side
+        return lax.rem(group + 2 * groups - 1 - i, groups) * 2 + 1 - side
+
+    def to_core(kind, l, i):
         a = kinds[kind][0]
         if kinds[kind][3]:
             slot = (a - 2) * LAYERS + l
-            here = block(kind, l, index)
-            c = remote(here, here, c_send.at[slot, k], c_recv.at[slot, k], core_peer)
+            here = block(kind, l, source_of(i))
+            c = remote(here, here, c_send.at[slot, i], c_recv.at[slot, i], core_peer)
             c.start()
             unsent.append(c)
-            unreceived.append(c.wait_recv)
+            missing[kind, l].append(c.wait_recv)
+
+    def pass_one(kind, l, k):
+        slot = kinds[kind][0] * LAYERS + l
+        ways[kind, l, "own", k].wait_recv()
+        here = block(kind, l, source_of(k - 1))
+        c = remote(here, here, x_send.at[slot, k], x_recv.at[slot, k], x_peer)
+        c.start()
+        ways[kind, l, "x", k] = c
+        unsent.append(c)
+        to_core(kind, l, k - 1)
 
     def pass_on(kind, l):
-        slot = kinds[kind][0] * LAYERS + l
         for k in range(1, groups):
-            ways[kind, l, "own", k].wait_recv()
-            source = lax.rem(group + groups - k, groups) * 2 + side
-            here = block(kind, l, source)
-            c = remote(here, here, x_send.at[slot, k], x_recv.at[slot, k], x_peer)
-            c.start()
-            ways[kind, l, "x", k] = c
-            unsent.append(c)
-            to_core(kind, l, source, k)
+            pass_one(kind, l, k)
+
+    def take_one(kind, l, k):
+        ways[kind, l, "own" if k == 0 else "x", k].wait_recv()
+        to_core(kind, l, groups - 1 + k)
 
     def take_across(kind, l):
         for k in range(groups):
-            ways[kind, l, "own" if k == 0 else "x", k].wait_recv()
-            source = lax.rem(group + groups - k, groups) * 2 + 1 - side
-            to_core(kind, l, source, groups + k)
+            take_one(kind, l, k)
+
+    def share_one(kind, l, i):
+        slot = (kinds[kind][0] - 2) * LAYERS + l
+        here = block(kind, l, source_of(i))
+        c = remote(here, here, y_send.at[slot, i], y_recv.at[slot, i], y_peer)
+        c.start()
+        ways[kind, l, "y", i] = c
+        unsent.append(c)
+
+    def share_y(kind, l, part=0, parts=1):
+        if (kind, l) in SHARED_Y:
+            for i in range(part * (n - 1) // parts, (part + 1) * (n - 1) // parts):
+                share_one(kind, l, i)
+
+    def take_y(kind, l):
+        if (kind, l) in SHARED_Y:
+            slot = (kinds[kind][0] - 2) * LAYERS + l
+            for i in range(n - 1):
+                ways[kind, l, "y", i].wait_recv()
+                here = block(kind, l, source_of(i), lax.rem(tensor + 2, 4))
+                c = remote(here, here, d_send.at[slot, i], d_recv.at[slot, i], core_peer)
+                c.start()
+                unsent.append(c)
+                missing[kind, l].append(c.wait_recv)
+
+    def complete(kind, l):
+        for wait in missing.pop((kind, l)):
+            wait()
+        if (kind, l) in leaving:
+            settle_slices(kind, l)
 
     slices = {
-        "normed": (0, normed_out, normed_all, True),
-        "grad_att": (1, grad_att_out, grad_att_all, True),
+        "normed": (0, slices_out, normed_all, True),
+        "grad_att": (1, slices_out, grad_att_all, True),
         "gains": (2, gains_out, gains_all, False),
     }
 
@@ -251,10 +340,12 @@
     def send_slices(kind, l):
         b, own, everywhere, halves = slices[kind]
         slot = b * LAYERS + l
+        held_at = LAYERS - 1 - l if kind == "grad_att" else l
+        sent = []
         for k in range(1, n):
             to = lax.rem(dp + k, n)
             c = remote(
-                sliced(kind, own, l, to),
+                sliced(kind, own, held_at, to),
                 sliced(kind, everywhere, l, dp),
                 a_send.at[slot, k],
                 a_recv.at[slot, k],
@@ -262,12 +353,17 @@
             )
             c.start()
             ways[kind, l, k] = c
-            unsent.append(c)
+            sent.append(c.wait_send)
         c = pltpu.make_async_copy(
-            own.at[l, dp], everywhere.at[l, dp], local.at[4 * LAYERS + slot]
+            own.at[held_at, dp], everywhere.at[l, dp], local.at[4 * LAYERS + slot]
         )
         c.start()
-        unreceived.append(c.wait)
+        missing[kind, l] = []
+        leaving[kind, l] = sent + [c.wait]
+
+    def settle_slices(kind, l):
+        for wait in leaving.pop((kind, l)):
+            wait()
 
     def take_slices(kind, l):
         b, _, everywhere, halves = slices[kind]
@@ -280,7 +376,7 @@
                 c = remote(here, here, b_send.at[slot, k], b_recv.at[slot, k], core_peer)
                 c.start()
                 unsent.append(c)
-                unreceived.append(c.wait_recv)
+                missing[kind, l].append(c.wait_recv)
 
     def cut(dst, l, src):
         for t in range(n):
@@ -300,10 +396,10 @@
             return columns((1 - core) * side_width + k * TILE, TILE)
 
         def first(k):
-            return copy(0, k, part.at[:, at(k)], from_core.at[j, :, at(k)], core_peer)
+            return copy(0, k, part.at[:, at(k)], from_core.at[j % 2, :, at(k)], core_peer)
 
         def second(k):
-            return copy(1, k, half.at[:, at(k)], from_y.at[j, :, at(k)], y_peer)
+            return copy(1, k, half.at[:, at(k)], from_y.at[j % 2, :, at(k)], y_peer)
 
         def third(k):
             return copy(2, k, dest.at[:, mine(k)], dest.at[:, mine(k)], core_peer)
@@ -315,12 +411,12 @@
         def middle(k):
             own = tile(mine(k))
             first(k).wait_recv()
-            half[:, at(k)] = own + from_core[j, :, at(k)]
+            half[:, at(k)] = own + from_core[j % 2, :, at(k)]
             second(k).start()
 
         def finish(k):
             second(k).wait_recv()
-            total = half[:, at(k)] + from_y[j, :, at(k)]
+            total = half[:, at(k)] + from_y[j % 2, :, at(k)]
             if base is not None:
                 total = base[:, mine(k)] + total
             dest[:, mine(k)] = total
@@ -396,7 +492,7 @@
             (v_key, key_t, kv_heads, True),
             (v_value, value_t, kv_heads, False),
         ):
-            projected = jnp.transpose(nn(source, ref[l]))
+            projected = jnp.transpose(nn(source, ref[l])) if ref is v_query else nt(ref[l], source)
             for h in range(count):
                 values = projected[h * HD : (h + 1) * HD]
                 values = turned(values, 1.0) if rope else values
@@ -443,7 +539,7 @@
 
     def attention_layer(l, meanwhile):
         normalize(stream.at[2 * l], attn_gain, l, normed_low, normed_two_out.at[l])
-        cut(normed_out, l, normed_two_out.at[l])
+        cut(slices_out, l, normed_two_out.at[l])
         send_slices("normed", l)
         attend(l)
         send_own("mixed", l)
@@ -495,11 +591,11 @@
             j,
             lambda at: nt(left_low[...], v_gate[l, at, :]) + nt(right_low[...], v_up[l, at, :]),
             None,
-            grads.at[j - 2 * LAYERS],
+            grads.at[j % 2],
             meanwhile,
         )
         norm_backward(
-            grads.at[j - 2 * LAYERS],
+            grads.at[j % 2],
             stream.at[2 * l + 1],
             mlp_gain,
             l,
@@ -509,93 +605,242 @@
             normed_low,
             part_wide,
         )
-        cut(grad_att_out, l, part_wide)
+        settle_slices("normed", LAYERS - 1 - l)
+        cut(slices_out, LAYERS - 1 - l, part_wide)
         send_slices("grad_att", l)
 
-    part_wide = grads.at[2 * LAYERS]
+    part_wide = grads.at[2]
 
     def attention_layer_back(l, meanwhile):
         attention_back(l)
-        send_own("qkv", l)
+        if l == 0:
+            send_own("qkv", l)
         j = 2 * LAYERS + 2 * (LAYERS - 1 - l) + 1
         q_end, k_end = heads * HD, (heads + kv_heads) * HD
         v_end = (heads + 2 * kv_heads) * HD
         tensor_sum(
             j,
             lambda at: nt(left_low[:, :q_end], v_query[l, at, :])
-            + nt(left_low[:, q_end:k_end], v_key[l, at, :])
-            + nt(left_low[:, k_end:v_end], v_value[l, at, :]),
+            + nn(left_low[:, q_end:k_end], v_key[l, :, at])
+            + nn(left_low[:, k_end:v_end], v_value[l, :, at]),
             None,
-            grads.at[j - 2 * LAYERS],
+            grads.at[j % 2],
             meanwhile,
         )
         last = l == 0
         norm_backward(
-            grads.at[j - 2 * LAYERS],
+            grads.at[j % 2],
             stream.at[2 * l],
             attn_gain,
             l,
             l,
             upstream,
-            grad_input if last else upstream,
+            upstream,
             None if last else normed_low,
             None if last else g_out.at[l - 1],
         )
-        if not last:
-            send_own("g", l - 1)
-
-    stream[0] = hidden_in[...]
-    upstream[...] = cotangent[...]
-    g_out[LAYERS - 1] = cotangent[...].astype(low).astype(full)
+
+    window = cut_a.shape[0]
+    start = jnp.minimum(dp * piece // 128 * 128, width - window)
+    offset = pl.multiple_of(dp * piece - start, 8)
+
+    def stream_tokens(count, copies, body):
+        def go(i, slot):
+            for c in copies(i, slot):
+                c.start()
+
+        go(0, 0)
+
+        def step(i):
+            slot = lax.rem(i, 2)
+            for c in copies(i, slot):
+                c.wait()
+
+            @pl.when(i + 1 < count)
+            def _():
+                go(i + 1, 1 - slot)
+
+            body(slot)
+
+        each(count, step)
+
+    def mlp_gradients(l):
+        def copies(i, slot):
+            rows = pl.ds(pl.multiple_of(i * TOKENS, 8), TOKENS)
+            return (
+                pltpu.make_async_copy(
+                    normed_two_all.at[l, rows], token_a.at[slot], fetch.at[0, slot]
+                ),
+                pltpu.make_async_copy(g_all.at[l, rows], token_b.at[slot], fetch.at[1, slot]),
+            )
+
+        sum_g[...] = jnp.zeros_like(sum_g)
+        sum_u[...] = jnp.zeros_like(sum_u)
+        sum_d[...] = jnp.zeros_like(sum_d)
+
+        def body(slot):
+            low_a[...] = token_a[slot].astype(low)
+            low_b[...] = token_b[slot].astype(low)
+            cut_a[...] = jnp.transpose(token_a[slot, :, columns(start, window)]).astype(low)
+            cut_b[...] = jnp.transpose(token_b[slot, :, columns(start, window)]).astype(low)
+
+            def units(i):
+                at = columns(i * TILE, TILE)
+                gate = nn(low_a[...], v_gate[l, :, at])
+                up = nn(low_a[...], v_up[l, :, at])
+                grad_act = nt(low_b[...], v_down[l, at, :])
+                left, right, activated = mlp_grads(gate, up, grad_act)
+                sum_g[:, at] += nn(cut_a[...], left)
+                sum_u[:, at] += nn(cut_a[...], right)
+                sum_d[:, at] += nn(cut_b[...], activated)
+
+            each(hidden_units // TILE, units)
+
+        stream_tokens(n * length // TOKENS, copies, body)
+        outs = [
+            pltpu.make_async_copy(src.at[pl.ds(offset, piece)], dst.at[l], edge.at[4 + i])
+            for i, (src, dst) in enumerate(((sum_g, grad_g), (sum_u, grad_u), (sum_d, grad_d)))
+        ]
+        for c in outs:
+            c.start()
+        for c in outs:
+            c.wait()
+
+    def attention_gradients(l):
+        blocks = TOKENS // length
+
+        def copies(i, slot):
+            rows = pl.ds(pl.multiple_of(i * TOKENS, 8), TOKENS)
+            several = pl.ds(i * blocks, blocks)
+            return (
+                pltpu.make_async_copy(qkv_all.at[l, rows], state_qkv.at[slot], fetch.at[2, slot]),
+                pltpu.make_async_copy(
+                    mixed_all.at[l, rows], state_mixed.at[slot], fetch.at[3, slot]
+                ),
+                pltpu.make_async_copy(
+                    normed_all.at[l, several], state_a.at[slot], fetch.at[4, slot]
+                ),
+                pltpu.make_async_copy(
+                    grad_att_all.at[l, several], state_b.at[slot], fetch.at[5, slot]
+                ),
+            )
+
+        for ref in (sum_q, sum_k, sum_v, sum_o):
+            ref[...] = jnp.zeros_like(ref)
+        q_end, k_end = heads * HD, (heads + kv_heads) * HD
+
+        def body(slot):
+            for b in range(blocks):
+                rows = slice(b * length, (b + 1) * length)
+                normed = jnp.transpose(state_a[slot, b]).astype(low)
+                grad_att = jnp.transpose(state_b[slot, b]).astype(low)
+                qkv = state_qkv[slot, rows, :].astype(low)
+                sum_q[...] += nn(normed, qkv[:, :q_end])
+                sum_k[...] += nn(normed, qkv[:, q_end:k_end])
+                sum_v[...] += nn(normed, qkv[:, k_end:])
+                sum_o[...] += nn(grad_att, state_mixed[slot, rows, :].astype(low))
+
+        stream_tokens(n * length // TOKENS, copies, body)
+        outs = [
+            pltpu.make_async_copy(src, dst.at[l], edge.at[7 + i])
+            for i, (src, dst) in enumerate(
+                ((sum_q, grad_q), (sum_k, grad_k), (sum_v, grad_v), (sum_o, grad_o))
+            )
+        ]
+        for c in outs:
+            c.start()
+        for c in outs:
+            c.wait()
+
+    def steps(*calls):
+        def run():
+            for call, *what in calls:
+                call(*what)
+
+        return run
+
+    for c in arriving:
+        c.wait()
+    g_out[LAYERS - 1] = upstream[...].astype(low).astype(full)
     send_own("g", LAYERS - 1)
     gain_rows[...] = jnp.zeros_like(gain_rows)
-
-    def steps(*calls):
-        def run():
-            for call, kind, l in calls:
-                call(kind, l)
-
-        return run
 
     attention_layer(0, nothing)
     mlp_layer(0, steps((pass_on, "g", 1), (take_slices, "normed", 0)))
     attention_layer(1, steps((pass_on, "mixed", 0), (take_across, "g", 1)))
-    mlp_layer(1, steps((take_across, "mixed", 0)))
-    hidden_out[...] = stream[2 * LAYERS]
+    mlp_layer(1, steps((pass_on, "normed_two", 0), (take_across, "mixed", 0)))
+    going = [pltpu.make_async_copy(stream.at[2 * LAYERS], hidden_out, edge.at[2])]
+    going[0].start()
     normed_low[...] = g_out[LAYERS - 1].astype(low)
-    mlp_back(1, steps((pass_on, "normed_two", 0), (take_slices, "normed", 1)))
-    attention_layer_back(1, steps((pass_on, "mixed", 1), (take_across, "normed_two", 0)))
-    mlp_back(0, steps((pass_on, "normed_two", 1), (take_across, "mixed", 1)))
-    attention_layer_back(0, steps((pass_on, "qkv", 1), (take_slices, "grad_att", 1)))
+    mlp_back(1, steps((take_slices, "normed", 1), (take_across, "normed_two", 0)))
+    attention_layer_back(1, steps((pass_on, "mixed", 1), (share_y, "normed_two", 0, 0, 3)))
+    send_own("g", 0)
+    send_own("qkv", 1)
+    mlp_back(0, steps((take_across, "mixed", 1), (share_y, "normed_two", 0, 1, 3)))
+    attention_layer_back(0, steps((pass_on, "normed_two", 1), (share_y, "normed_two", 0, 2, 3)))
+    going.append(pltpu.make_async_copy(upstream, grad_input, edge.at[3]))
+    going[1].start()
     cut(gains_out, 0, gain_rows)
     send_slices("gains", 0)
-    for call, kind, l in (
+    for call, *what in (
+        (take_slices, "grad_att", 1),
+        (pass_on, "g", 0),
         (take_across, "normed_two", 1),
-        (pass_on, "g", 0),
+        (take_y, "normed_two", 0),
+        (take_across, "g", 0),
+        (share_y, "g", 0),
+        (complete, "normed_two", 1),
+        (complete, "g", 1),
+        (pass_on, "qkv", 1),
+        (mlp_gradients, 1),
+        (take_y, "g", 0),
         (take_across, "qkv", 1),
+        (complete, "normed_two", 0),
+        (complete, "g", 0),
+        (mlp_gradients, 0),
+        (take_slices, "grad_att", 0),
         (pass_on, "qkv", 0),
-        (take_across, "g", 0),
-        (take_slices, "grad_att", 0),
+        (complete, "qkv", 1),
+        (complete, "mixed", 1),
+        (complete, "normed", 1),
+        (complete, "grad_att", 1),
+        (attention_gradients, 1),
         (take_across, "qkv", 0),
         (take_slices, "gains", 0),
+        (complete, "gains", 0),
+        (complete, "qkv", 0),
+        (complete, "mixed", 0),
+        (complete, "normed", 0),
+        (complete, "grad_att", 0),
+        (attention_gradients, 0),
     ):
-        call(kind, l)
-    for wait in unreceived:
-        wait()
+        call(*what)
+    assert not missing
     for c in unsent:
         c.wait_send()
+    for key in list(leaving):
+        settle_slices(*key)
+    for c in going:
+        c.wait()
 
 
 def layers(n, hidden_in, cotangent, cosine, sine, allowed, attn_gain, mlp_gain, weights):
     length, width = hidden_in.shape
     w_query, w_key, w_value, w_output, w_gate, w_up, w_down = weights
-    q_width, kv_width, hidden_units = w_query.shape[2], w_key.shape[2], w_gate.shape[2]
+    q_width, kv_width, hidden_units = w_query.shape[2], w_key.shape[1], w_gate.shape[2]
     qkv_width = q_width + 2 * kv_width
     piece = width // n
     f32 = lambda *shape: jax.ShapeDtypeStruct(shape, full)
     out_shape = [
         f32(length, width),
         f32(length, width),
+        f32(LAYERS, piece, q_width),
+        f32(LAYERS, piece, kv_width),
+        f32(LAYERS, piece, kv_width),
+        f32(LAYERS, piece, q_width),
+        f32(LAYERS, piece, hidden_units),
+        f32(LAYERS, piece, hidden_units),
+        f32(LAYERS, piece, hidden_units),
         f32(LAYERS, n * length, q_width),
         f32(LAYERS, n * length, qkv_width),
         f32(LAYERS, n * length, width),
@@ -610,15 +855,16 @@
     keep = lambda dtype, *shape: pltpu.VMEM(shape, dtype)
     sums = 4 * LAYERS
     chunks = width // 2 // TILE
+    window = pl.cdiv(piece + 128 - math.gcd(piece, 128), 128) * 128
     return pl.pallas_call(
         functools.partial(layers_kernel, n),
         out_shape=out_shape,
-        in_specs=[vmem] * 7 + [anywhere] * 7,
-        out_specs=[vmem] * 2 + [anywhere] * 7,
+        in_specs=[anywhere] * 2 + [vmem] * 5 + [anywhere] * 7,
+        out_specs=[anywhere] * 16,
         scratch_shapes=[keep(low, *w.shape) for w in weights]
         + [
             keep(full, 2 * LAYERS + 1, length, width),
-            keep(full, 2 * LAYERS + 1, length, width),
+            keep(full, 3, length, width),
             keep(full, length, width),
             keep(low, length, width),
             keep(low, length, hidden_units),
@@ -635,14 +881,30 @@
             keep(full, LAYERS, length, width),
             keep(full, LAYERS, length, width),
             keep(full, LAYERS, n, length, piece),
-            keep(full, LAYERS, n, length, piece),
             keep(full, 1, n, 8, piece),
             keep(full, 8, width),
             keep(full, qkv_width, length),
             keep(full, length, width // 2),
-            keep(full, sums, length, width // 2),
+            keep(full, 2, length, width // 2),
             keep(full, length, width // 2),
-            keep(full, sums, length, width // 2),
+            keep(full, 2, length, width // 2),
+            keep(full, 2, TOKENS, width),
+            keep(full, 2, TOKENS, width),
+            keep(low, TOKENS, width),
+            keep(low, TOKENS, width),
+            keep(low, window, TOKENS),
+            keep(low, window, TOKENS),
+            keep(full, window, hidden_units),
+            keep(full, window, hidden_units),
+            keep(full, window, hidden_units),
+            keep(full, 2, TOKENS, qkv_width),
+            keep(full, 2, TOKENS, q_width),
+            keep(full, 2, TOKENS // length, length, piece),
+            keep(full, 2, TOKENS // length, length, piece),
+            keep(full, piece, q_width),
+            keep(full, piece, kv_width),
+            keep(full, piece, kv_width),
+            keep(full, piece, q_width),
             dma((LAYERS, 7)),
             dma((sums, 3, chunks)),
             dma((sums, 3, chunks)),
@@ -656,7 +918,13 @@
             dma((3 * LAYERS, n)),
             dma((2 * LAYERS, n)),
             dma((2 * LAYERS, n)),
+            dma((2 * LAYERS, n)),
+            dma((2 * LAYERS, n)),
+            dma((2 * LAYERS, n)),
+            dma((2 * LAYERS, n)),
             dma((7 * LAYERS,)),
+            dma((11,)),
+            dma((6, 2)),
         ],
         compiler_params=pltpu.CompilerParams(
             collective_id=0, has_side_effects=True, vmem_limit_bytes=66_000_000
@@ -681,10 +949,16 @@
     mlp_gain,
 ):
     n = lax.axis_size("dp")
-    dp = lax.axis_index("dp")
-    weights = (w_query, w_key, w_value, w_output, w_gate, w_up, w_down)
-    length, width = hidden_in.shape
-    piece = width // n
+    length = hidden_in.shape[0]
+    weights = (
+        w_query,
+        jnp.swapaxes(w_key, 1, 2),
+        jnp.swapaxes(w_value, 1, 2),
+        w_output,
+        w_gate,
+        w_up,
+        w_down,
+    )
     half_dim = HD // 2
     frequencies = rope_base ** (-(jnp.arange(half_dim).astype(jnp.float32) * 2.0 / HD))
     angles = frequencies[:, None] * positions[0].astype(jnp.float32)[None, :]
@@ -693,48 +967,29 @@
     allowed = (segments[:, None] == segments[None, :]) & (
         token_order[:, None] <= token_order[None, :]
     )
-    hidden, grad_input, mixed_all, qkv_all, normed_two_all, g_all, normed_all, grad_att_all, gains = (
-        layers(
-            n,
-            hidden_in,
-            cotangent,
-            jnp.cos(angles),
-            jnp.sin(angles),
-            allowed.astype(jnp.float32),
-            attn_gain,
-            mlp_gain,
-            weights,
-        )
+    outs = layers(
+        n,
+        hidden_in,
+        cotangent,
+        jnp.cos(angles),
+        jnp.sin(angles),
+        allowed.astype(jnp.float32),
+        attn_gain,
+        mlp_gain,
+        weights,
     )
-    heads = w_query.shape[2]
-    kv = w_key.shape[2]
-    grads = [[] for _ in range(7)]
-    for l in range(LAYERS):
-        mixed = mixed_all[l].astype(low)
-        qkv = qkv_all[l].astype(low)
-        normed_two = normed_two_all[l].astype(low)
-        g_low = g_all[l].astype(low)
-        normed = normed_all[l].reshape(n * length, piece).astype(low)
-        grad_att = grad_att_all[l].reshape(n * length, piece).astype(low)
-        gate_pre = nn(normed_two, w_gate[l])
-        up_pre = nn(normed_two, w_up[l])
-        grad_act = nt(g_low, w_down[l])
-        grad_gate_low, grad_up_low, activated = mlp_grads(gate_pre, up_pre, grad_act)
-        my_normed_two = lax.dynamic_slice_in_dim(normed_two, dp * piece, piece, 1)
-        my_g = lax.dynamic_slice_in_dim(g_low, dp * piece, piece, 1)
-        grad_qkv = tn(normed, qkv)
-        grads[0].append(grad_qkv[:, :heads])
-        grads[1].append(grad_qkv[:, heads : heads + kv])
-        grads[2].append(grad_qkv[:, heads + kv :])
-        grads[3].append(tn(mixed, grad_att))
-        grads[4].append(tn(my_normed_two, grad_gate_low))
-        grads[5].append(tn(my_normed_two, grad_up_low))
-        grads[6].append(tn(activated, my_g))
-    gain_sums = jnp.sum(gains[0], axis=0)
+    hidden, grad_input, grad_q, grad_k, grad_v, grad_o, grad_g, grad_u, grad_d = outs[:9]
+    gain_sums = jnp.sum(outs[-1][0], axis=0)
     return (
         hidden,
         grad_input,
-        *[jnp.stack(g) for g in grads],
+        grad_q,
+        grad_k,
+        grad_v,
+        jnp.swapaxes(grad_o, 1, 2),
+        grad_g,
+        grad_u,
+        jnp.swapaxes(grad_d, 1, 2),
         gain_sums[:LAYERS],
         gain_sums[LAYERS : 2 * LAYERS],
     )

time: 408 us -> 347 us (0.85)
  matrix products: 48.9 us -> 0 us
  local copies, waits for them, and re-layouts: 20.9 us -> 11 us
  other arithmetic: 12.7 us -> 3.86 us
  Pallas kernels: 319 us -> 325 us
    dot_general x16 -> x0, matrix products: 48.9 us -> none  [the longest x10 21.3 us: tn(): lax.dot_general(a, b, (((0,), (0,)), ((), ())), preferred_element_type=full)]
    slice x3 -> x0, local copies, waits for them, and re-layouts: 11.5 us -> none  [the longest x1 11.3 us: shards(): g_low = g_all[l].astype(low)]
    another operation x10 -> x0, other arithmetic: 8.77 us -> none  [the longest x6 6.45 us: shards(): jnp.stack(g)]
    pallas_call x1, Pallas kernels: 319 us -> 325 us  [layers(): pl.pallas_call(functools.partial(layers_kernel, n), out_shape=out_shape,...]
    unnamed x32 -> x25, local copies, waits for them, and re-layouts: 8.56 us -> 10.4 us
where the time goes in v3:
time: 347 us; the launch traced here: 340 us
  Pallas kernels  325 us (94%)
  local copies, waits for them, and re-layouts  11 us (3%)
  other arithmetic  3.86 us (1%)
    pallas_call x1, Pallas kernels, layers(): pl.pallas_call(functools.partial(layers_kernel, n), out_shape=out_shape,...  325 us
    unnamed x25, local copies, waits for them, and re-layouts  10.4 us

profile of v3, /device:TPU:0, one launch (start us, length us, event | category | flops | bytes accessed | tf_op | source)
XLA Modules:
  0.0 340.4 jit_solution(16440432946313348779)
XLA Ops:
  0.6 0.7 convert_bitcast_fusion
  1.3 0.8 multiply_sine_fusion
  2.1 1.4 fusion.1.refs_4_
  3.5 324.9 %layers.1 = (f32[128,1536]{1,0:T(8,128)}, f32[128,1536]{1,0:T(8,128)}, f32[2,192,384]{2,1,0:T(8,128)}, f32[2,192,192]{2,1,0:T(8,128)}, f32[2,192,192]{2,1,0:T(8,...) custom-call(f32[128,1536]{1,0:T(8,128)} %refs_0_.1, ...), custom_call_target="tpu_custom_call" | custom-call | tf_op jit(solution)/shard_map/layers/pallas_call | solution.py:859
  328.4 0.0 copy-start.3
  328.4 0.0 copy-start.5
  328.4 1.0 reduce_sum.9
  329.4 0.6 fusion.2
  330.0 0.0 copy-start.7
  330.0 2.1 copy.33
  332.1 0.0 copy-done.3
  332.1 0.0 copy-start.6
  332.1 0.0 copy-start.4
  332.1 0.9 copy.34
  333.0 0.0 copy-done.5
  333.0 0.0 copy-start.2
  333.0 0.8 copy.35
  333.8 0.0 copy-done.7
  333.8 0.7 copy.36
  334.6 0.0 copy-done.6
  334.6 0.7 copy.37
  335.3 0.0 copy-done.4
  335.3 0.0 copy-start.1
  335.3 0.8 copy.38
  336.1 0.0 copy-done.2
  336.1 1.1 copy.39
  337.3 0.0 copy-done.1
  337.3 0.0 copy-start
  337.3 1.1 copy.40
  338.4 0.8 copy-done
  339.2 1.1 copy.41
  (1 shorter events, 0.0 us)
Async XLA Ops:
  328.4 3.7 %copy-start.3 = (f32[128,1536]{1,0:T(8,128)S(1)}, f32[128,1536]{1,0:T(8,128)}, u32[]{:S(2)}) copy-start(f32[128,1536]{1,0:T(8,128)} %get-tuple-element.47) | copy-start | bytes 2359300
  328.4 4.6 %copy-start.5 = (f32[2,192,384]{2,1,0:T(8,128)S(1)}, f32[2,192,384]{2,1,0:T(8,128)}, u32[]{:S(2)}) copy-start(f32[2,192,384]{2,1,0:T(8,128)} %get-tuple-element.48) | copy-start | bytes 1769476
  330.0 3.8 %copy-start.7 = (f32[2,192,192]{2,1,0:T(8,128)S(1)}, f32[2,192,192]{2,1,0:T(8,128)}, u32[]{:S(2)}) copy-start(f32[2,192,192]{2,1,0:T(8,128)} %get-tuple-element.49) | copy-start | bytes 884740
  332.1 2.5 copy-start.6
  332.1 3.2 copy-start.4
  333.0 3.1 copy-start.2
  335.3 2.0 copy-start.1
  337.3 2.0 copy-start

commit v4 on v3

--- a/solution.py
+++ b/solution.py
@@ -13,7 +13,7 @@
 TILE = 256
 ROWS = 16
 TOKENS = 256
-SHARED_Y = (("normed_two", 0), ("g", 0))
+SHARED_Y = (("g", 1), ("normed_two", 0), ("g", 0))
 MESH = pl.DeviceIdType.MESH
 
 
@@ -156,6 +156,10 @@
         y_recv,
         d_send,
         d_recv,
+        e_send,
+        e_recv,
+        f_send,
+        f_recv,
         local,
         edge,
         fetch,
@@ -283,9 +287,12 @@
         unsent.append(c)
         to_core(kind, l, k - 1)
 
+    def pass_part(kind, l, part, parts):
+        for k in range(1 + part * (groups - 1) // parts, 1 + (part + 1) * (groups - 1) // parts):
+            pass_one(kind, l, k)
+
     def pass_on(kind, l):
-        for k in range(1, groups):
-            pass_one(kind, l, k)
+        pass_part(kind, l, 0, 1)
 
     def take_one(kind, l, k):
         ways[kind, l, "own" if k == 0 else "x", k].wait_recv()
@@ -331,11 +338,26 @@
         "gains": (2, gains_out, gains_all, False),
     }
 
-    def sliced(kind, ref, l, index):
+    slice_parts = 4 if piece % 32 == 0 else 2
+    slice_rows = piece // slice_parts
+    slice_mine = tensor if slice_parts == 4 else core
+
+    def sliced(kind, l, index, owner=None):
+        everywhere = slices[kind][2]
         if slices[kind][3]:
-            rows = pl.ds(pl.multiple_of(core * (length // 2), 8), length // 2)
-            return ref.at[l, index, rows]
-        return ref.at[l, index]
+            at = slice_mine if owner is None else owner
+            rows = pl.ds(pl.multiple_of(at * slice_rows, 8), slice_rows)
+            return everywhere.at[l, index, rows]
+        return everywhere.at[l, index]
+
+    def sliced_own(kind, slot, index, whole=False):
+        own = slices[kind][1]
+        if not slices[kind][3]:
+            return own.at[slot, index]
+        if whole:
+            return own.at[slot, pl.ds(pl.multiple_of(index * piece, 8), piece)]
+        first = pl.multiple_of(index * piece + slice_mine * slice_rows, 8)
+        return own.at[slot, pl.ds(first, slice_rows)]
 
     def send_slices(kind, l):
         b, own, everywhere, halves = slices[kind]
@@ -345,8 +367,8 @@
         for k in range(1, n):
             to = lax.rem(dp + k, n)
             c = remote(
-                sliced(kind, own, held_at, to),
-                sliced(kind, everywhere, l, dp),
+                sliced_own(kind, held_at, to),
+                sliced(kind, l, dp),
                 a_send.at[slot, k],
                 a_recv.at[slot, k],
                 (to, tensor),
@@ -355,7 +377,7 @@
             ways[kind, l, k] = c
             sent.append(c.wait_send)
         c = pltpu.make_async_copy(
-            own.at[held_at, dp], everywhere.at[l, dp], local.at[4 * LAYERS + slot]
+            sliced_own(kind, held_at, dp, True), everywhere.at[l, dp], local.at[4 * LAYERS + slot]
         )
         c.start()
         missing[kind, l] = []
@@ -366,17 +388,37 @@
             wait()
 
     def take_slices(kind, l):
-        b, _, everywhere, halves = slices[kind]
+        b, _, everywhere, divided = slices[kind]
         slot = b * LAYERS + l
         for k in range(1, n):
             ways[kind, l, k].wait_recv()
-            if halves:
-                source = lax.rem(dp + n - k, n)
-                here = sliced(kind, everywhere, l, source)
+            if divided:
+                here = sliced(kind, l, lax.rem(dp + n - k, n))
                 c = remote(here, here, b_send.at[slot, k], b_recv.at[slot, k], core_peer)
                 c.start()
                 unsent.append(c)
                 missing[kind, l].append(c.wait_recv)
+                if slice_parts == 4:
+                    c = remote(here, here, e_send.at[slot, k], e_recv.at[slot, k], y_peer)
+                    c.start()
+                    unsent.append(c)
+                    ways[kind, l, "y", k] = c
+
+    def take_slices_y(kind, l):
+        slot = slices[kind][0] * LAYERS + l
+        if slice_parts == 4:
+            for k in range(1, n):
+                ways[kind, l, "y", k].wait_recv()
+                here = sliced(kind, l, lax.rem(dp + n - k, n), lax.rem(tensor + 2, 4))
+                c = remote(here, here, f_send.at[slot, k], f_recv.at[slot, k], core_peer)
+                c.start()
+                unsent.append(c)
+                missing[kind, l].append(c.wait_recv)
+
+    def turn_over(dst, src):
+        for t in range(width // 128):
+            at = slice(t * 128, (t + 1) * 128)
+            dst[at, :] = jnp.transpose(src[:, at])
 
     def cut(dst, l, src):
         for t in range(n):
@@ -539,7 +581,7 @@
 
     def attention_layer(l, meanwhile):
         normalize(stream.at[2 * l], attn_gain, l, normed_low, normed_two_out.at[l])
-        cut(slices_out, l, normed_two_out.at[l])
+        turn_over(slices_out.at[l], normed_two_out.at[l])
         send_slices("normed", l)
         attend(l)
         send_own("mixed", l)
@@ -606,7 +648,7 @@
             part_wide,
         )
         settle_slices("normed", LAYERS - 1 - l)
-        cut(slices_out, LAYERS - 1 - l, part_wide)
+        turn_over(slices_out.at[LAYERS - 1 - l], part_wide)
         send_slices("grad_att", l)
 
     part_wide = grads.at[2]
@@ -644,27 +686,27 @@
     start = jnp.minimum(dp * piece // 128 * 128, width - window)
     offset = pl.multiple_of(dp * piece - start, 8)
 
-    def stream_tokens(count, copies, body):
+    def stream_tokens(first, count, copies, body):
         def go(i, slot):
             for c in copies(i, slot):
                 c.start()
 
-        go(0, 0)
+        go(first, 0)
 
         def step(i):
             slot = lax.rem(i, 2)
-            for c in copies(i, slot):
+            for c in copies(first + i, slot):
                 c.wait()
 
             @pl.when(i + 1 < count)
             def _():
-                go(i + 1, 1 - slot)
+                go(first + i + 1, 1 - slot)
 
             body(slot)
 
         each(count, step)
 
-    def mlp_gradients(l):
+    def mlp_gradients(l, share=0, shares=1):
         def copies(i, slot):
             rows = pl.ds(pl.multiple_of(i * TOKENS, 8), TOKENS)
             return (
@@ -674,9 +716,10 @@
                 pltpu.make_async_copy(g_all.at[l, rows], token_b.at[slot], fetch.at[1, slot]),
             )
 
-        sum_g[...] = jnp.zeros_like(sum_g)
-        sum_u[...] = jnp.zeros_like(sum_u)
-        sum_d[...] = jnp.zeros_like(sum_d)
+        if share == 0:
+            sum_g[...] = jnp.zeros_like(sum_g)
+            sum_u[...] = jnp.zeros_like(sum_u)
+            sum_d[...] = jnp.zeros_like(sum_d)
 
         def body(slot):
             low_a[...] = token_a[slot].astype(low)
@@ -696,7 +739,10 @@
 
             each(hidden_units // TILE, units)
 
-        stream_tokens(n * length // TOKENS, copies, body)
+        count = n * length // TOKENS // shares
+        stream_tokens(share * count, count, copies, body)
+        if share < shares - 1:
+            return
         outs = [
             pltpu.make_async_copy(src.at[pl.ds(offset, piece)], dst.at[l], edge.at[4 + i])
             for i, (src, dst) in enumerate(((sum_g, grad_g), (sum_u, grad_u), (sum_d, grad_d)))
@@ -732,15 +778,15 @@
         def body(slot):
             for b in range(blocks):
                 rows = slice(b * length, (b + 1) * length)
-                normed = jnp.transpose(state_a[slot, b]).astype(low)
-                grad_att = jnp.transpose(state_b[slot, b]).astype(low)
+                normed = state_a[slot, b].astype(low)
+                grad_att = state_b[slot, b].astype(low)
                 qkv = state_qkv[slot, rows, :].astype(low)
                 sum_q[...] += nn(normed, qkv[:, :q_end])
                 sum_k[...] += nn(normed, qkv[:, q_end:k_end])
                 sum_v[...] += nn(normed, qkv[:, k_end:])
                 sum_o[...] += nn(grad_att, state_mixed[slot, rows, :].astype(low))
 
-        stream_tokens(n * length // TOKENS, copies, body)
+        stream_tokens(0, n * length // TOKENS, copies, body)
         outs = [
             pltpu.make_async_copy(src, dst.at[l], edge.at[7 + i])
             for i, (src, dst) in enumerate(
@@ -767,45 +813,75 @@
 
     attention_layer(0, nothing)
     mlp_layer(0, steps((pass_on, "g", 1), (take_slices, "normed", 0)))
-    attention_layer(1, steps((pass_on, "mixed", 0), (take_across, "g", 1)))
-    mlp_layer(1, steps((pass_on, "normed_two", 0), (take_across, "mixed", 0)))
+    attention_layer(
+        1,
+        steps((pass_on, "mixed", 0), (take_across, "g", 1), (share_y, "g", 1, 0, 3)),
+    )
+    mlp_layer(
+        1,
+        steps((pass_on, "normed_two", 0), (take_across, "mixed", 0), (share_y, "g", 1, 1, 3)),
+    )
     going = [pltpu.make_async_copy(stream.at[2 * LAYERS], hidden_out, edge.at[2])]
     going[0].start()
     normed_low[...] = g_out[LAYERS - 1].astype(low)
-    mlp_back(1, steps((take_slices, "normed", 1), (take_across, "normed_two", 0)))
-    attention_layer_back(1, steps((pass_on, "mixed", 1), (share_y, "normed_two", 0, 0, 3)))
+    mlp_back(
+        1,
+        steps(
+            (take_slices, "normed", 1),
+            (take_across, "normed_two", 0),
+            (pass_on, "mixed", 1),
+            (share_y, "g", 1, 2, 3),
+        ),
+    )
+    attention_layer_back(1, steps((take_across, "mixed", 1), (share_y, "normed_two", 0, 0, 3)))
     send_own("g", 0)
     send_own("qkv", 1)
-    mlp_back(0, steps((take_across, "mixed", 1), (share_y, "normed_two", 0, 1, 3)))
-    attention_layer_back(0, steps((pass_on, "normed_two", 1), (share_y, "normed_two", 0, 2, 3)))
+    mlp_back(0, steps((pass_on, "normed_two", 1), (share_y, "normed_two", 0, 1, 3)))
+    attention_layer_back(
+        0,
+        steps(
+            (take_slices, "grad_att", 1),
+            (pass_on, "g", 0),
+            (take_across, "normed_two", 1),
+            (share_y, "normed_two", 0, 2, 3),
+        ),
+    )
     going.append(pltpu.make_async_copy(upstream, grad_input, edge.at[3]))
     going[1].start()
     cut(gains_out, 0, gain_rows)
     send_slices("gains", 0)
     for call, *what in (
-        (take_slices, "grad_att", 1),
-        (pass_on, "g", 0),
-        (take_across, "normed_two", 1),
-        (take_y, "normed_two", 0),
         (take_across, "g", 0),
         (share_y, "g", 0),
+        (take_slices, "grad_att", 0),
+        (take_y, "g", 1),
+        (take_slices_y, "normed", 0),
+        (take_slices_y, "normed", 1),
+        (take_slices_y, "grad_att", 1),
+        (take_y, "normed_two", 0),
         (complete, "normed_two", 1),
         (complete, "g", 1),
+        (mlp_gradients, 1, 0, 2),
         (pass_on, "qkv", 1),
-        (mlp_gradients, 1),
+        (mlp_gradients, 1, 1, 2),
         (take_y, "g", 0),
         (take_across, "qkv", 1),
         (complete, "normed_two", 0),
         (complete, "g", 0),
-        (mlp_gradients, 0),
-        (take_slices, "grad_att", 0),
-        (pass_on, "qkv", 0),
+        (mlp_gradients, 0, 0, 4),
+        (pass_part, "qkv", 0, 0, 3),
+        (mlp_gradients, 0, 1, 4),
+        (pass_part, "qkv", 0, 1, 3),
+        (mlp_gradients, 0, 2, 4),
+        (pass_part, "qkv", 0, 2, 3),
+        (mlp_gradients, 0, 3, 4),
         (complete, "qkv", 1),
         (complete, "mixed", 1),
         (complete, "normed", 1),
         (complete, "grad_att", 1),
         (attention_gradients, 1),
         (take_across, "qkv", 0),
+        (take_slices_y, "grad_att", 0),
         (take_slices, "gains", 0),
         (complete, "gains", 0),
         (complete, "qkv", 0),
@@ -845,8 +921,8 @@
         f32(LAYERS, n * length, qkv_width),
         f32(LAYERS, n * length, width),
         f32(LAYERS, n * length, width),
-        f32(LAYERS, n, length, piece),
-        f32(LAYERS, n, length, piece),
+        f32(LAYERS, n, piece, length),
+        f32(LAYERS, n, piece, length),
         f32(1, n, 8, piece),
     ]
     vmem = pl.BlockSpec(memory_space=pltpu.VMEM)
@@ -880,7 +956,7 @@
             keep(full, LAYERS, length, qkv_width),
             keep(full, LAYERS, length, width),
             keep(full, LAYERS, length, width),
-            keep(full, LAYERS, n, length, piece),
+            keep(full, LAYERS, width, length),
             keep(full, 1, n, 8, piece),
             keep(full, 8, width),
             keep(full, qkv_width, length),
@@ -899,8 +975,8 @@
             keep(full, window, hidden_units),
             keep(full, 2, TOKENS, qkv_width),
             keep(full, 2, TOKENS, q_width),
-            keep(full, 2, TOKENS // length, length, piece),
-            keep(full, 2, TOKENS // length, length, piece),
+            keep(full, 2, TOKENS // length, piece, length),
+            keep(full, 2, TOKENS // length, piece, length),
             keep(full, piece, q_width),
             keep(full, piece, kv_width),
             keep(full, piece, kv_width),
@@ -916,6 +992,10 @@
             dma((2 * LAYERS, n)),
             dma((3 * LAYERS, n)),
             dma((3 * LAYERS, n)),
+            dma((2 * LAYERS, n)),
+            dma((2 * LAYERS, n)),
+            dma((2 * LAYERS, n)),
+            dma((2 * LAYERS, n)),
             dma((2 * LAYERS, n)),
             dma((2 * LAYERS, n)),
             dma((2 * LAYERS, n)),

time: 347 us -> 322 us (0.928)
  Pallas kernels: 325 us -> 299 us
    pallas_call x1, Pallas kernels: 325 us -> 299 us  [layers(): pl.pallas_call(functools.partial(layers_kernel, n), out_shape=out_shape,...]
where the time goes in v4:
time: 322 us; the launch traced here: 316 us
  Pallas kernels  299 us (93%)
  local copies, waits for them, and re-layouts  11.8 us (4%)
  other arithmetic  3.83 us (1%)
    pallas_call x1, Pallas kernels, layers(): pl.pallas_call(functools.partial(layers_kernel, n), out_shape=out_shape,...  299 us
    unnamed x25, local copies, waits for them, and re-layouts  11.2 us

profile of v4, /device:TPU:0, one launch (start us, length us, event | category | flops | bytes accessed | tf_op | source)
XLA Modules:
  0.0 315.7 jit_solution(14708950909033942645)
XLA Ops:
  0.6 0.7 convert_bitcast_fusion
  1.3 0.8 multiply_sine_fusion
  2.1 1.4 fusion.1.refs_4_
  3.5 299.3 %layers.1 = (f32[128,1536]{1,0:T(8,128)}, f32[128,1536]{1,0:T(8,128)}, f32[2,192,384]{2,1,0:T(8,128)}, f32[2,192,192]{2,1,0:T(8,128)}, f32[2,192,192]{2,1,0:T(8,...) custom-call(f32[128,1536]{1,0:T(8,128)} %refs_0_.1, ...), custom_call_target="tpu_custom_call" | custom-call | tf_op jit(solution)/shard_map/layers/pallas_call | solution.py:935
  302.9 0.0 copy-start.3
  302.9 0.9 reduce_sum.9
  303.8 0.6 fusion.2
  304.4 0.0 copy-start.5
  304.4 2.1 copy.33
  306.5 0.0 copy-done.3
  306.5 0.0 copy-start.7
  306.5 0.0 copy-start.6
  306.5 0.9 copy.34
  307.4 0.0 copy-done.5
  307.4 0.0 copy-start.4
  307.4 0.8 copy.35
  308.2 0.0 copy-done.7
  308.2 0.0 copy-start.2
  308.2 0.7 copy.36
  309.0 0.0 copy-done.6
  309.0 0.7 copy.37
  309.7 0.0 copy-done.4
  309.7 0.8 copy.38
  310.6 0.0 copy-done.2
  310.6 0.0 copy-start.1
  310.6 1.1 copy.39
  311.7 0.8 copy-done.1
  312.5 0.0 copy-start
  312.5 1.1 copy.40
  313.7 0.8 copy-done
  314.5 1.1 copy.41
  (1 shorter events, 0.0 us)
Async XLA Ops:
  302.9 3.7 %copy-start.3 = (f32[128,1536]{1,0:T(8,128)S(1)}, f32[128,1536]{1,0:T(8,128)}, u32[]{:S(2)}) copy-start(f32[128,1536]{1,0:T(8,128)} %get-tuple-element.47) | copy-start | bytes 2359300
  304.4 3.0 copy-start.5
  306.5 1.7 copy-start.7
  306.5 2.5 copy-start.6
  307.4 2.3 copy-start.4
  308.2 2.3 copy-start.2
  310.6 2.0 copy-start.1
  312.5 2.0 copy-start

commit v5 on v4

--- a/solution.py
+++ b/solution.py
@@ -11,6 +11,7 @@
 HD = 96
 LAYERS = 2
 TILE = 256
+UNITS = 512
 ROWS = 16
 TOKENS = 256
 SHARED_Y = (("g", 1), ("normed_two", 0), ("g", 0))
@@ -84,7 +85,8 @@
         grad_u,
         grad_d,
         mixed_all,
-        qkv_all,
+        query_all,
+        keyval_all,
         normed_two_all,
         g_all,
         normed_all,
@@ -218,10 +220,12 @@
     ways = {}
     kinds = {
         "mixed": (0, mixed_out, mixed_all, False),
-        "qkv": (1, qkv_out, qkv_all, False),
+        "query": (1, qkv_out, query_all, False),
         "normed_two": (2, normed_two_out, normed_two_all, True),
         "g": (3, g_out, g_all, True),
+        "keyval": (4, qkv_out, keyval_all, False),
     }
+    spans = {"query": slice(0, heads * HD), "keyval": slice(heads * HD, qkv_out.shape[2])}
 
     quarter_width = width // 4
 
@@ -235,6 +239,10 @@
             return everywhere.at[l, rows, columns(core * side_width, side_width)]
         return everywhere.at[l, rows]
 
+    def own_of(kind, l):
+        own = kinds[kind][1]
+        return own.at[l, :, spans[kind]] if kind in spans else own.at[l]
+
     def send_own(kind, l):
         a, own, everywhere, shared = kinds[kind]
         slot = a * LAYERS + l
@@ -243,7 +251,7 @@
         elif shared:
             mine = own.at[l, :, columns(core * side_width, side_width)]
         else:
-            mine = own.at[l]
+            mine = own_of(kind, l)
         for k in range(groups):
             if k == 0:
                 c = remote(
@@ -258,7 +266,7 @@
             ways[kind, l, "own", k] = c
             unsent.append(c)
         rows = pl.ds(pl.multiple_of(dp * length, 8), length)
-        c = pltpu.make_async_copy(own.at[l], everywhere.at[l, rows], local.at[slot])
+        c = pltpu.make_async_copy(own_of(kind, l), everywhere.at[l, rows], local.at[slot])
         c.start()
         missing.setdefault((kind, l), []).append(c.wait)
 
@@ -377,7 +385,7 @@
             ways[kind, l, k] = c
             sent.append(c.wait_send)
         c = pltpu.make_async_copy(
-            sliced_own(kind, held_at, dp, True), everywhere.at[l, dp], local.at[4 * LAYERS + slot]
+            sliced_own(kind, held_at, dp, True), everywhere.at[l, dp], local.at[5 * LAYERS + slot]
         )
         c.start()
         missing[kind, l] = []
@@ -524,6 +532,13 @@
     def scores_t(l, h):
         raw = tn(head(key_t, l, h // share), head(query_t, l, h)) * scale
         return jnp.where(allowed[...] > 0.5, raw, masked_score)
+
+    def steps(*calls):
+        def run():
+            for call, *what in calls:
+                call(*what)
+
+        return run
 
     def attend(l):
         for i in range(3):
@@ -579,10 +594,17 @@
     step = hidden_units // 2
     nothing = lambda: None
 
+    def turn_normed(l):
+        turn_over(slices_out.at[l], normed_two_out.at[l])
+        send_slices("normed", l)
+
+    def turn_grad_att(l):
+        settle_slices("normed", LAYERS - 1 - l)
+        turn_over(slices_out.at[LAYERS - 1 - l], part_wide)
+        send_slices("grad_att", l)
+
     def attention_layer(l, meanwhile):
         normalize(stream.at[2 * l], attn_gain, l, normed_low, normed_two_out.at[l])
-        turn_over(slices_out.at[l], normed_two_out.at[l])
-        send_slices("normed", l)
         attend(l)
         send_own("mixed", l)
         loads[l, 3].wait()
@@ -591,7 +613,7 @@
             lambda at: nn(left_low[:, : heads * HD], v_output[l, :, at]),
             stream.at[2 * l],
             stream.at[2 * l + 1],
-            meanwhile,
+            steps((turn_normed, l), (meanwhile,)),
         )
 
     def mlp_layer(l, meanwhile):
@@ -647,16 +669,14 @@
             normed_low,
             part_wide,
         )
-        settle_slices("normed", LAYERS - 1 - l)
-        turn_over(slices_out.at[LAYERS - 1 - l], part_wide)
-        send_slices("grad_att", l)
 
     part_wide = grads.at[2]
 
     def attention_layer_back(l, meanwhile):
         attention_back(l)
+        send_own("query", l)
         if l == 0:
-            send_own("qkv", l)
+            send_own("keyval", l)
         j = 2 * LAYERS + 2 * (LAYERS - 1 - l) + 1
         q_end, k_end = heads * HD, (heads + kv_heads) * HD
         v_end = (heads + 2 * kv_heads) * HD
@@ -667,7 +687,7 @@
             + nn(left_low[:, k_end:v_end], v_value[l, :, at]),
             None,
             grads.at[j % 2],
-            meanwhile,
+            steps((turn_grad_att, l), (meanwhile,)),
         )
         last = l == 0
         norm_backward(
@@ -728,7 +748,7 @@
             cut_b[...] = jnp.transpose(token_b[slot, :, columns(start, window)]).astype(low)
 
             def units(i):
-                at = columns(i * TILE, TILE)
+                at = columns(i * UNITS, UNITS)
                 gate = nn(low_a[...], v_gate[l, :, at])
                 up = nn(low_a[...], v_up[l, :, at])
                 grad_act = nt(low_b[...], v_down[l, at, :])
@@ -737,7 +757,7 @@
                 sum_u[:, at] += nn(cut_a[...], right)
                 sum_d[:, at] += nn(cut_b[...], activated)
 
-            each(hidden_units // TILE, units)
+            each(hidden_units // UNITS, units)
 
         count = n * length // TOKENS // shares
         stream_tokens(share * count, count, copies, body)
@@ -757,18 +777,28 @@
 
         def copies(i, slot):
             rows = pl.ds(pl.multiple_of(i * TOKENS, 8), TOKENS)
-            several = pl.ds(i * blocks, blocks)
             return (
-                pltpu.make_async_copy(qkv_all.at[l, rows], state_qkv.at[slot], fetch.at[2, slot]),
+                pltpu.make_async_copy(
+                    query_all.at[l, rows],
+                    state_qkv.at[slot, :, spans["query"]],
+                    fetch.at[2, slot],
+                ),
+                pltpu.make_async_copy(
+                    keyval_all.at[l, rows],
+                    state_qkv.at[slot, :, spans["keyval"]],
+                    fetch.at[4 + 2 * blocks, slot],
+                ),
                 pltpu.make_async_copy(
                     mixed_all.at[l, rows], state_mixed.at[slot], fetch.at[3, slot]
                 ),
+            ) + tuple(
                 pltpu.make_async_copy(
-                    normed_all.at[l, several], state_a.at[slot], fetch.at[4, slot]
-                ),
-                pltpu.make_async_copy(
-                    grad_att_all.at[l, several], state_b.at[slot], fetch.at[5, slot]
-                ),
+                    src.at[l, i * blocks + b],
+                    dst.at[slot, :, pl.ds(b * length, length)],
+                    fetch.at[at + b, slot],
+                )
+                for src, dst, at in ((normed_all, state_a, 4), (grad_att_all, state_b, 4 + blocks))
+                for b in range(blocks)
             )
 
         for ref in (sum_q, sum_k, sum_v, sum_o):
@@ -776,15 +806,12 @@
         q_end, k_end = heads * HD, (heads + kv_heads) * HD
 
         def body(slot):
-            for b in range(blocks):
-                rows = slice(b * length, (b + 1) * length)
-                normed = state_a[slot, b].astype(low)
-                grad_att = state_b[slot, b].astype(low)
-                qkv = state_qkv[slot, rows, :].astype(low)
-                sum_q[...] += nn(normed, qkv[:, :q_end])
-                sum_k[...] += nn(normed, qkv[:, q_end:k_end])
-                sum_v[...] += nn(normed, qkv[:, k_end:])
-                sum_o[...] += nn(grad_att, state_mixed[slot, rows, :].astype(low))
+            normed = state_a[slot].astype(low)
+            qkv = state_qkv[slot].astype(low)
+            sum_q[...] += nn(normed, qkv[:, :q_end])
+            sum_k[...] += nn(normed, qkv[:, q_end:k_end])
+            sum_v[...] += nn(normed, qkv[:, k_end:])
+            sum_o[...] += nn(state_b[slot].astype(low), state_mixed[slot].astype(low))
 
         stream_tokens(0, n * length // TOKENS, copies, body)
         outs = [
@@ -797,13 +824,6 @@
             c.start()
         for c in outs:
             c.wait()
-
-    def steps(*calls):
-        def run():
-            for call, *what in calls:
-                call(*what)
-
-        return run
 
     for c in arriving:
         c.wait()
@@ -828,22 +848,40 @@
         1,
         steps(
             (take_slices, "normed", 1),
+            (pass_on, "mixed", 1),
             (take_across, "normed_two", 0),
-            (pass_on, "mixed", 1),
             (share_y, "g", 1, 2, 3),
         ),
     )
-    attention_layer_back(1, steps((take_across, "mixed", 1), (share_y, "normed_two", 0, 0, 3)))
+    attention_layer_back(
+        1,
+        steps(
+            (pass_on, "normed_two", 1),
+            (take_across, "mixed", 1),
+            (share_y, "normed_two", 0, 0, 3),
+        ),
+    )
     send_own("g", 0)
-    send_own("qkv", 1)
-    mlp_back(0, steps((pass_on, "normed_two", 1), (share_y, "normed_two", 0, 1, 3)))
+    send_own("keyval", 1)
+    mlp_back(
+        0,
+        steps(
+            (take_slices, "grad_att", 1),
+            (pass_on, "query", 1),
+            (share_y, "normed_two", 0, 1, 3),
+            (take_y, "g", 1),
+            (take_slices_y, "normed", 0),
+        ),
+    )
     attention_layer_back(
         0,
         steps(
-            (take_slices, "grad_att", 1),
             (pass_on, "g", 0),
             (take_across, "normed_two", 1),
             (share_y, "normed_two", 0, 2, 3),
+            (complete, "normed_two", 1),
+            (complete, "g", 1),
+            (mlp_gradients, 1, 0, 4),
         ),
     )
     going.append(pltpu.make_async_copy(upstream, grad_input, edge.at[3]))
@@ -851,40 +889,44 @@
     cut(gains_out, 0, gain_rows)
     send_slices("gains", 0)
     for call, *what in (
+        (pass_on, "keyval", 1),
         (take_across, "g", 0),
         (share_y, "g", 0),
-        (take_slices, "grad_att", 0),
-        (take_y, "g", 1),
-        (take_slices_y, "normed", 0),
         (take_slices_y, "normed", 1),
         (take_slices_y, "grad_att", 1),
         (take_y, "normed_two", 0),
-        (complete, "normed_two", 1),
-        (complete, "g", 1),
-        (mlp_gradients, 1, 0, 2),
-        (pass_on, "qkv", 1),
-        (mlp_gradients, 1, 1, 2),
+        (take_across, "query", 1),
+        (mlp_gradients, 1, 1, 4),
+        (take_slices, "grad_att", 0),
+        (pass_part, "query", 0, 0, 3),
+        (mlp_gradients, 1, 2, 4),
+        (pass_part, "query", 0, 1, 3),
+        (pass_part, "query", 0, 2, 3),
+        (mlp_gradients, 1, 3, 4),
+        (pass_part, "keyval", 0, 0, 3),
+        (take_across, "keyval", 1),
         (take_y, "g", 0),
-        (take_across, "qkv", 1),
+        (pass_part, "keyval", 0, 1, 3),
         (complete, "normed_two", 0),
         (complete, "g", 0),
         (mlp_gradients, 0, 0, 4),
-        (pass_part, "qkv", 0, 0, 3),
+        (pass_part, "keyval", 0, 2, 3),
+        (take_across, "query", 0),
         (mlp_gradients, 0, 1, 4),
-        (pass_part, "qkv", 0, 1, 3),
         (mlp_gradients, 0, 2, 4),
-        (pass_part, "qkv", 0, 2, 3),
         (mlp_gradients, 0, 3, 4),
-        (complete, "qkv", 1),
+        (complete, "query", 1),
+        (complete, "keyval", 1),
         (complete, "mixed", 1),
         (complete, "normed", 1),
         (complete, "grad_att", 1),
         (attention_gradients, 1),
-        (take_across, "qkv", 0),
+        (take_across, "keyval", 0),
         (take_slices_y, "grad_att", 0),
         (take_slices, "gains", 0),
         (complete, "gains", 0),
-        (complete, "qkv", 0),
+        (complete, "query", 0),
+        (complete, "keyval", 0),
         (complete, "mixed", 0),
         (complete, "normed", 0),
         (complete, "grad_att", 0),
@@ -918,7 +960,8 @@
         f32(LAYERS, piece, hidden_units),
         f32(LAYERS, piece, hidden_units),
         f32(LAYERS, n * length, q_width),
-        f32(LAYERS, n * length, qkv_width),
+        f32(LAYERS, n * length, q_width),
+        f32(LAYERS, n * length, 2 * kv_width),
         f32(LAYERS, n * length, width),
         f32(LAYERS, n * length, width),
         f32(LAYERS, n, piece, length),
@@ -936,7 +979,7 @@
         functools.partial(layers_kernel, n),
         out_shape=out_shape,
         in_specs=[anywhere] * 2 + [vmem] * 5 + [anywhere] * 7,
-        out_specs=[anywhere] * 16,
+        out_specs=[anywhere] * 17,
         scratch_shapes=[keep(low, *w.shape) for w in weights]
         + [
             keep(full, 2 * LAYERS + 1, length, width),
@@ -975,8 +1018,8 @@
             keep(full, window, hidden_units),
             keep(full, 2, TOKENS, qkv_width),
             keep(full, 2, TOKENS, q_width),
-            keep(full, 2, TOKENS // length, piece, length),
-            keep(full, 2, TOKENS // length, piece, length),
+            keep(full, 2, piece, TOKENS),
+            keep(full, 2, piece, TOKENS),
             keep(full, piece, q_width),
             keep(full, piece, kv_width),
             keep(full, piece, kv_width),
@@ -984,10 +1027,10 @@
             dma((LAYERS, 7)),
             dma((sums, 3, chunks)),
             dma((sums, 3, chunks)),
-            dma((4 * LAYERS, n // 2)),
-            dma((4 * LAYERS, n // 2)),
-            dma((4 * LAYERS, n // 2)),
-            dma((4 * LAYERS, n // 2)),
+            dma((5 * LAYERS, n // 2)),
+            dma((5 * LAYERS, n // 2)),
+            dma((5 * LAYERS, n // 2)),
+            dma((5 * LAYERS, n // 2)),
             dma((2 * LAYERS, n)),
             dma((2 * LAYERS, n)),
             dma((3 * LAYERS, n)),
@@ -1002,9 +1045,9 @@
             dma((2 * LAYERS, n)),
             dma((2 * LAYERS, n)),
             dma((2 * LAYERS, n)),
-            dma((7 * LAYERS,)),
+            dma((8 * LAYERS,)),
             dma((11,)),
-            dma((6, 2)),
+            dma((5 + 2 * (TOKENS // length), 2)),
         ],
         compiler_params=pltpu.CompilerParams(
             collective_id=0, has_side_effects=True, vmem_limit_bytes=66_000_000

time: 322 us -> 296 us (0.919); the launches traced: 316 us -> 295 us
  Pallas kernels: 299 us -> 278 us
    pallas_call x1, Pallas kernels: 299 us -> 278 us  [layers(): pl.pallas_call(functools.partial(layers_kernel, n), out_shape=out_shape,...]
    unnamed x25 -> x23, local copies, waits for them, and re-layouts: 11.2 us -> 11.7 us
where the time goes in v5:
time: 296 us; the launch traced here: 295 us
  Pallas kernels  278 us (94%)
  local copies, waits for them, and re-layouts  12.2 us (4%)
  other arithmetic  3.84 us (1%)
    pallas_call x1, Pallas kernels, layers(): pl.pallas_call(functools.partial(layers_kernel, n), out_shape=out_shape,...  278 us
    unnamed x23, local copies, waits for them, and re-layouts  11.7 us

profile of v5, /device:TPU:0, one launch (start us, length us, event | category | flops | bytes accessed | tf_op | source)
XLA Modules:
  0.0 294.9 jit_solution(9591363657837116786)
XLA Ops:
  0.6 0.7 convert_bitcast_fusion
  1.3 0.8 multiply_sine_fusion
  2.1 1.4 fusion.1.refs_4_
  3.5 278.2 %layers.1 = (f32[128,1536]{1,0:T(8,128)}, f32[128,1536]{1,0:T(8,128)}, f32[2,192,384]{2,1,0:T(8,128)}, f32[2,192,192]{2,1,0:T(8,128)}, f32[2,192,192]{2,1,0:T(8,...) custom-call(f32[128,1536]{1,0:T(8,128)} %refs_0_.1, ...), custom_call_target="tpu_custom_call" | custom-call | tf_op jit(solution)/shard_map/layers/pallas_call | solution.py:978
  281.7 0.0 copy-start.4
  281.7 0.0 copy-start.6
  281.8 0.9 reduce_sum.9
  282.7 0.6 fusion.2
  283.3 0.0 copy-start.5
  283.3 2.1 copy.33
  285.4 0.0 copy-start.3
  285.4 2.1 copy.34
  287.5 0.0 copy-done.4
  287.5 0.0 copy-start.2
  287.5 0.8 copy.35
  288.4 0.0 copy-done.6
  288.4 0.7 copy.36
  289.1 0.0 copy-done.5
  289.1 0.7 copy.37
  289.9 0.0 copy-done.3
  289.9 0.0 copy-start.1
  289.9 0.8 copy.38
  290.7 0.0 copy-done.2
  290.7 1.1 copy.39
  291.8 0.0 copy-done.1
  291.8 0.0 copy-start
  291.8 1.1 copy.40
  293.0 0.8 copy-done
  293.8 1.1 copy.41
  (1 shorter events, 0.0 us)
Async XLA Ops:
  281.7 5.8 %copy-start.4 = (f32[2,192,384]{2,1,0:T(8,128)S(1)}, f32[2,192,384]{2,1,0:T(8,128)}, u32[]{:S(2)}) copy-start(f32[2,192,384]{2,1,0:T(8,128)} %get-tuple-element.48) | copy-start | bytes 1769476
  281.7 6.6 %copy-start.6 = (f32[2,192,192]{2,1,0:T(8,128)S(1)}, f32[2,192,192]{2,1,0:T(8,128)}, u32[]{:S(2)}) copy-start(f32[2,192,192]{2,1,0:T(8,128)} %get-tuple-element.49) | copy-start | bytes 884740
  283.3 5.8 %copy-start.5 = (f32[2,192,192]{2,1,0:T(8,128)S(1)}, f32[2,192,192]{2,1,0:T(8,128)}, u32[]{:S(2)}) copy-start(f32[2,192,192]{2,1,0:T(8,128)} %get-tuple-element.50) | copy-start | bytes 884740
  285.4 4.5 %copy-start.3 = (f32[2,192,384]{2,1,0:T(8,128)S(1)}, f32[2,192,384]{2,1,0:T(8,128)}, u32[]{:S(2)}) copy-start(f32[2,192,384]{2,1,0:T(8,128)} %get-tuple-element.26) | copy-start | bytes 1769476
  287.5 3.1 %copy-start.2 = (f32[2,192,1024]{2,1,0:T(8,128)S(1)}, f32[2,192,1024]{2,1,0:T(8,128)}, u32[]{:S(2)}) copy-start(f32[2,192,1024]{2,1,0:T(8,128)} %get-tuple-element.52) | copy-start | bytes 4718596
  289.9 2.0 copy-start.1
  291.8 2.0 copy-start

commit v6 on v5

--- a/solution.py
+++ b/solution.py
@@ -12,6 +12,18 @@
 LAYERS = 2
 TILE = 256
 UNITS = 512
+RELAYED = (
+    ("g", 1),
+    ("mixed", 0),
+    ("normed_two", 0),
+    ("mixed", 1),
+    ("normed_two", 1),
+    ("query", 1),
+    ("g", 0),
+    ("keyval", 1),
+    ("query", 0),
+    ("keyval", 0),
+)
 ROWS = 16
 TOKENS = 256
 SHARED_Y = (("g", 1), ("normed_two", 0), ("g", 0))
@@ -145,6 +157,7 @@
         sum_send,
         sum_recv,
         z_send,
+        z_down,
         z_recv,
         x_send,
         x_recv,
@@ -215,6 +228,7 @@
 
     unsent = []
     missing = {}
+    conditional = []
     leaving = {}
 
     ways = {}
@@ -252,7 +266,29 @@
             mine = own.at[l, :, columns(core * side_width, side_width)]
         else:
             mine = own_of(kind, l)
-        for k in range(groups):
+        relayed = (kind, l) in RELAYED
+        if relayed:
+            send_if(
+                group < groups - 1,
+                lambda: remote(
+                    mine,
+                    block(kind, l, dp),
+                    z_send.at[slot, 0],
+                    z_recv.at[slot, 1],
+                    ((group + 1) * 2 + side, tensor),
+                ),
+            )
+            send_if(
+                group > 0,
+                lambda: remote(
+                    mine,
+                    block(kind, l, dp),
+                    z_down.at[slot],
+                    z_recv.at[slot, groups - 1],
+                    ((group - 1) * 2 + side, tensor),
+                ),
+            )
+        for k in range(1 if relayed else groups):
             if k == 0:
                 c = remote(
                     mine, block(kind, l, dp), x_send.at[slot, 0], x_recv.at[slot, 0], x_peer
@@ -270,16 +306,39 @@
         c.start()
         missing.setdefault((kind, l), []).append(c.wait)
 
-    def source_of(i):
-        if i < groups - 1:
-            return lax.rem(group + groups - 1 - i, groups) * 2 + side
-        return lax.rem(group + 2 * groups - 1 - i, groups) * 2 + 1 - side
+    def send_if(condition, make):
+        @pl.when(condition)
+        def _():
+            make().start()
+
+        conditional.append((condition, make))
+
+    both = jnp.minimum(group, groups - 1 - group)
+    longer_below = (group > groups - 1 - group).astype(jnp.int32)
+
+    def ranked(j):
+        single = (j >= 2 * both).astype(jnp.int32)
+        below = single * longer_below + (1 - single) * (1 - j % 2)
+        distance = single * (j - both + 1) + (1 - single) * (j // 2 + 1)
+        return below, distance
+
+    def behind(kind, l, j):
+        if (kind, l) in RELAYED:
+            below, distance = ranked(j)
+            return below * distance + (1 - below) * (groups - distance)
+        return j + 1
+
+    def source_of(kind, l, i):
+        across = i >= groups - 1
+        j = i - groups if across else i
+        steps_back = 0 if j < 0 else behind(kind, l, j)
+        return lax.rem(group + groups - steps_back, groups) * 2 + (1 - side if across else side)
 
     def to_core(kind, l, i):
         a = kinds[kind][0]
         if kinds[kind][3]:
             slot = (a - 2) * LAYERS + l
-            here = block(kind, l, source_of(i))
+            here = block(kind, l, source_of(kind, l, i))
             c = remote(here, here, c_send.at[slot, i], c_recv.at[slot, i], core_peer)
             c.start()
             unsent.append(c)
@@ -287,8 +346,35 @@
 
     def pass_one(kind, l, k):
         slot = kinds[kind][0] * LAYERS + l
-        ways[kind, l, "own", k].wait_recv()
-        here = block(kind, l, source_of(k - 1))
+        here = block(kind, l, source_of(kind, l, k - 1))
+        if (kind, l) in RELAYED:
+            below, _ = ranked(k - 1)
+            steps_back = behind(kind, l, k - 1)
+            remote(
+                here, here, z_send.at[slot, k], z_recv.at[slot, steps_back], x_peer
+            ).wait_recv()
+            send_if(
+                jnp.logical_and(below == 1, group < groups - 1),
+                lambda: remote(
+                    here,
+                    here,
+                    z_send.at[slot, k],
+                    z_recv.at[slot, steps_back + 1],
+                    ((group + 1) * 2 + side, tensor),
+                ),
+            )
+            send_if(
+                jnp.logical_and(below == 0, group > 0),
+                lambda: remote(
+                    here,
+                    here,
+                    z_send.at[slot, k],
+                    z_recv.at[slot, steps_back - 1],
+                    ((group - 1) * 2 + side, tensor),
+                ),
+            )
+        else:
+            ways[kind, l, "own", k].wait_recv()
         c = remote(here, here, x_send.at[slot, k], x_recv.at[slot, k], x_peer)
         c.start()
         ways[kind, l, "x", k] = c
@@ -312,7 +398,7 @@
 
     def share_one(kind, l, i):
         slot = (kinds[kind][0] - 2) * LAYERS + l
-        here = block(kind, l, source_of(i))
+        here = block(kind, l, source_of(kind, l, i))
         c = remote(here, here, y_send.at[slot, i], y_recv.at[slot, i], y_peer)
         c.start()
         ways[kind, l, "y", i] = c
@@ -321,6 +407,16 @@
     def share_y(kind, l, part=0, parts=1):
         if (kind, l) in SHARED_Y:
             for i in range(part * (n - 1) // parts, (part + 1) * (n - 1) // parts):
+                share_one(kind, l, i)
+
+    def share_own(kind, l):
+        if (kind, l) in SHARED_Y:
+            for i in range(groups - 1):
+                share_one(kind, l, i)
+
+    def share_across(kind, l):
+        if (kind, l) in SHARED_Y:
+            for i in range(groups - 1, n - 1):
                 share_one(kind, l, i)
 
     def take_y(kind, l):
@@ -328,7 +424,7 @@
             slot = (kinds[kind][0] - 2) * LAYERS + l
             for i in range(n - 1):
                 ways[kind, l, "y", i].wait_recv()
-                here = block(kind, l, source_of(i), lax.rem(tensor + 2, 4))
+                here = block(kind, l, source_of(kind, l, i), lax.rem(tensor + 2, 4))
                 c = remote(here, here, d_send.at[slot, i], d_recv.at[slot, i], core_peer)
                 c.start()
                 unsent.append(c)
@@ -832,14 +928,28 @@
     gain_rows[...] = jnp.zeros_like(gain_rows)
 
     attention_layer(0, nothing)
-    mlp_layer(0, steps((pass_on, "g", 1), (take_slices, "normed", 0)))
+    mlp_layer(
+        0,
+        steps(
+            (pass_on, "g", 1),
+            (take_slices, "normed", 0),
+        ),
+    )
     attention_layer(
         1,
-        steps((pass_on, "mixed", 0), (take_across, "g", 1), (share_y, "g", 1, 0, 3)),
+        steps(
+            (pass_on, "mixed", 0),
+            (take_across, "g", 1),
+            (share_y, "g", 1, 0, 3),
+        ),
     )
     mlp_layer(
         1,
-        steps((pass_on, "normed_two", 0), (take_across, "mixed", 0), (share_y, "g", 1, 1, 3)),
+        steps(
+            (pass_on, "normed_two", 0),
+            (take_across, "mixed", 0),
+            (share_y, "g", 1, 1, 3),
+        ),
     )
     going = [pltpu.make_async_copy(stream.at[2 * LAYERS], hidden_out, edge.at[2])]
     going[0].start()
@@ -877,6 +987,7 @@
         0,
         steps(
             (pass_on, "g", 0),
+            (share_own, "g", 0),
             (take_across, "normed_two", 1),
             (share_y, "normed_two", 0, 2, 3),
             (complete, "normed_two", 1),
@@ -891,7 +1002,7 @@
     for call, *what in (
         (pass_on, "keyval", 1),
         (take_across, "g", 0),
-        (share_y, "g", 0),
+        (share_across, "g", 0),
         (take_slices_y, "normed", 1),
         (take_slices_y, "grad_att", 1),
         (take_y, "normed_two", 0),
@@ -936,6 +1047,12 @@
     assert not missing
     for c in unsent:
         c.wait_send()
+    for condition, make in conditional:
+
+        @pl.when(condition)
+        def _():
+            make().wait_send()
+
     for key in list(leaving):
         settle_slices(*key)
     for c in going:
@@ -1028,6 +1145,7 @@
             dma((sums, 3, chunks)),
             dma((sums, 3, chunks)),
             dma((5 * LAYERS, n // 2)),
+            dma((5 * LAYERS,)),
             dma((5 * LAYERS, n // 2)),
             dma((5 * LAYERS, n // 2)),
             dma((5 * LAYERS, n // 2)),

time: 296 us -> 287 us (0.970)
  Pallas kernels: 278 us -> 270 us
    pallas_call x1, Pallas kernels: 278 us -> 270 us  [layers(): pl.pallas_call(functools.partial(layers_kernel, n), out_shape=out_shape,...]
where the time goes in v6:
time: 287 us; the launch traced here: 286 us
  Pallas kernels  270 us (94%)
  local copies, waits for them, and re-layouts  12.2 us (4%)
  other arithmetic  3.84 us (1%)
    pallas_call x1, Pallas kernels, layers(): pl.pallas_call(functools.partial(layers_kernel, n), out_shape=out_shape,...  270 us
    unnamed x23, local copies, waits for them, and re-layouts  11.7 us

profile of v6, /device:TPU:0, one launch (start us, length us, event | category | flops | bytes accessed | tf_op | source)
XLA Modules:
  0.0 286.3 jit_solution(10110590034863373796)
XLA Ops:
  0.6 0.7 convert_bitcast_fusion
  1.3 0.8 multiply_sine_fusion
  2.1 1.4 fusion.1.refs_4_
  3.5 269.6 %layers.1 = (f32[128,1536]{1,0:T(8,128)}, f32[128,1536]{1,0:T(8,128)}, f32[2,192,384]{2,1,0:T(8,128)}, f32[2,192,192]{2,1,0:T(8,128)}, f32[2,192,192]{2,1,0:T(8,...) custom-call(f32[128,1536]{1,0:T(8,128)} %refs_0_.1, ...), custom_call_target="tpu_custom_call" | custom-call | tf_op jit(solution)/shard_map/layers/pallas_call | solution.py:1095
  273.1 0.0 copy-start.4
  273.1 0.0 copy-start.6
  273.2 0.9 reduce_sum.9
  274.1 0.6 fusion.2
  274.7 0.0 copy-start.5
  274.7 2.1 copy.33
  276.8 0.0 copy-start.3
  276.8 2.1 copy.34
  278.9 0.0 copy-done.4
  278.9 0.0 copy-start.2
  278.9 0.8 copy.35
  279.8 0.0 copy-done.6
  279.8 0.7 copy.36
  280.5 0.0 copy-done.5
  280.5 0.7 copy.37
  281.2 0.0 copy-done.3
  281.3 0.0 copy-start.1
  281.3 0.8 copy.38
  282.1 0.0 copy-done.2
  282.1 1.1 copy.39
  283.2 0.0 copy-done.1
  283.2 0.0 copy-start
  283.2 1.1 copy.40
  284.4 0.8 copy-done
  285.2 1.1 copy.41
  (1 shorter events, 0.0 us)
Async XLA Ops:
  273.1 5.8 %copy-start.4 = (f32[2,192,384]{2,1,0:T(8,128)S(1)}, f32[2,192,384]{2,1,0:T(8,128)}, u32[]{:S(2)}) copy-start(f32[2,192,384]{2,1,0:T(8,128)} %get-tuple-element.48) | copy-start | bytes 1769476
  273.1 6.6 %copy-start.6 = (f32[2,192,192]{2,1,0:T(8,128)S(1)}, f32[2,192,192]{2,1,0:T(8,128)}, u32[]{:S(2)}) copy-start(f32[2,192,192]{2,1,0:T(8,128)} %get-tuple-element.49) | copy-start | bytes 884740
  274.7 5.8 %copy-start.5 = (f32[2,192,192]{2,1,0:T(8,128)S(1)}, f32[2,192,192]{2,1,0:T(8,128)}, u32[]{:S(2)}) copy-start(f32[2,192,192]{2,1,0:T(8,128)} %get-tuple-element.50) | copy-start | bytes 884740
  276.8 4.5 %copy-start.3 = (f32[2,192,384]{2,1,0:T(8,128)S(1)}, f32[2,192,384]{2,1,0:T(8,128)}, u32[]{:S(2)}) copy-start(f32[2,192,384]{2,1,0:T(8,128)} %get-tuple-element.26) | copy-start | bytes 1769476
  278.9 3.1 %copy-start.2 = (f32[2,192,1024]{2,1,0:T(8,128)S(1)}, f32[2,192,1024]{2,1,0:T(8,128)}, u32[]{:S(2)}) copy-start(f32[2,192,1024]{2,1,0:T(8,128)} %get-tuple-element.52) | copy-start | bytes 4718596
  281.3 2.0 copy-start.1
  283.2 2.0 copy-start

commit v7 on v6

--- a/solution.py
+++ b/solution.py
@@ -927,28 +927,41 @@
     send_own("g", LAYERS - 1)
     gain_rows[...] = jnp.zeros_like(gain_rows)
 
-    attention_layer(0, nothing)
+    attention_layer(
+        0,
+        steps(
+            (pass_part, "g", 1, 0, 3),
+            (pass_part, "g", 1, 1, 3),
+        ),
+    )
     mlp_layer(
         0,
         steps(
-            (pass_on, "g", 1),
+            (pass_part, "g", 1, 2, 3),
+            (pass_part, "mixed", 0, 0, 3),
+            (pass_part, "mixed", 0, 1, 3),
             (take_slices, "normed", 0),
         ),
     )
     attention_layer(
         1,
         steps(
-            (pass_on, "mixed", 0),
+            (pass_part, "mixed", 0, 2, 3),
             (take_across, "g", 1),
             (share_y, "g", 1, 0, 3),
+            (pass_part, "normed_two", 0, 0, 3),
+            (pass_part, "normed_two", 0, 1, 3),
         ),
     )
     mlp_layer(
         1,
         steps(
-            (pass_on, "normed_two", 0),
+            (pass_part, "normed_two", 0, 2, 3),
             (take_across, "mixed", 0),
             (share_y, "g", 1, 1, 3),
+            (take_slices, "normed", 1),
+            (pass_part, "mixed", 1, 0, 3),
+            (pass_part, "mixed", 1, 1, 3),
         ),
     )
     going = [pltpu.make_async_copy(stream.at[2 * LAYERS], hidden_out, edge.at[2])]
@@ -957,18 +970,21 @@
     mlp_back(
         1,
         steps(
-            (take_slices, "normed", 1),
-            (pass_on, "mixed", 1),
+            (pass_part, "mixed", 1, 2, 3),
             (take_across, "normed_two", 0),
             (share_y, "g", 1, 2, 3),
+            (pass_part, "normed_two", 1, 0, 3),
+            (pass_part, "normed_two", 1, 1, 3),
         ),
     )
     attention_layer_back(
         1,
         steps(
-            (pass_on, "normed_two", 1),
+            (pass_part, "normed_two", 1, 2, 3),
             (take_across, "mixed", 1),
             (share_y, "normed_two", 0, 0, 3),
+            (take_y, "g", 1),
+            (take_slices_y, "normed", 0),
         ),
     )
     send_own("g", 0)
@@ -977,18 +993,18 @@
         0,
         steps(
             (take_slices, "grad_att", 1),
-            (pass_on, "query", 1),
+            (pass_part, "query", 1, 0, 3),
+            (pass_part, "query", 1, 1, 3),
+            (take_across, "normed_two", 1),
             (share_y, "normed_two", 0, 1, 3),
-            (take_y, "g", 1),
-            (take_slices_y, "normed", 0),
         ),
     )
     attention_layer_back(
         0,
         steps(
+            (pass_part, "query", 1, 2, 3),
             (pass_on, "g", 0),
             (share_own, "g", 0),
-            (take_across, "normed_two", 1),
             (share_y, "normed_two", 0, 2, 3),
             (complete, "normed_two", 1),
             (complete, "g", 1),

time: 287 us -> 278 us (0.969)
  Pallas kernels: 270 us -> 260 us
    pallas_call x1, Pallas kernels: 270 us -> 260 us  [layers(): pl.pallas_call(functools.partial(layers_kernel, n), out_shape=out_shape,...]
where the time goes in v7:
time: 278 us; the launch traced here: 277 us
  Pallas kernels  260 us (94%)
  local copies, waits for them, and re-layouts  12.2 us (4%)
  other arithmetic  3.84 us (1%)
    pallas_call x1, Pallas kernels, layers(): pl.pallas_call(functools.partial(layers_kernel, n), out_shape=out_shape,...  260 us
    unnamed x23, local copies, waits for them, and re-layouts  11.7 us

profile of v7, /device:TPU:0, one launch (start us, length us, event | category | flops | bytes accessed | tf_op | source)
XLA Modules:
  0.0 276.9 jit_solution(15539600811267069237)
XLA Ops:
  0.6 0.7 convert_bitcast_fusion
  1.3 0.8 multiply_sine_fusion
  2.1 1.4 fusion.1.refs_4_
  3.5 260.2 %layers.1 = (f32[128,1536]{1,0:T(8,128)}, f32[128,1536]{1,0:T(8,128)}, f32[2,192,384]{2,1,0:T(8,128)}, f32[2,192,192]{2,1,0:T(8,128)}, f32[2,192,192]{2,1,0:T(8,...) custom-call(f32[128,1536]{1,0:T(8,128)} %refs_0_.1, ...), custom_call_target="tpu_custom_call" | custom-call | tf_op jit(solution)/shard_map/layers/pallas_call | solution.py:1111
  263.7 0.0 copy-start.4
  263.8 0.0 copy-start.6
  263.8 0.9 reduce_sum.9
  264.7 0.6 fusion.2
  265.3 0.0 copy-start.5
  265.3 2.1 copy.33
  267.4 0.0 copy-start.3
  267.4 2.1 copy.34
  269.5 0.0 copy-done.4
  269.5 0.0 copy-start.2
  269.5 0.8 copy.35
  270.4 0.0 copy-done.6
  270.4 0.7 copy.36
  271.1 0.0 copy-done.5
  271.1 0.7 copy.37
  271.9 0.0 copy-done.3
  271.9 0.0 copy-start.1
  271.9 0.8 copy.38
  272.7 0.0 copy-done.2
  272.7 1.1 copy.39
  273.8 0.0 copy-done.1
  273.8 0.0 copy-start
  273.8 1.1 copy.40
  275.0 0.8 copy-done
  275.8 1.1 copy.41
  (1 shorter events, 0.0 us)
Async XLA Ops:
  263.7 5.8 %copy-start.4 = (f32[2,192,384]{2,1,0:T(8,128)S(1)}, f32[2,192,384]{2,1,0:T(8,128)}, u32[]{:S(2)}) copy-start(f32[2,192,384]{2,1,0:T(8,128)} %get-tuple-element.48) | copy-start | bytes 1769476
  263.8 6.6 %copy-start.6 = (f32[2,192,192]{2,1,0:T(8,128)S(1)}, f32[2,192,192]{2,1,0:T(8,128)}, u32[]{:S(2)}) copy-start(f32[2,192,192]{2,1,0:T(8,128)} %get-tuple-element.49) | copy-start | bytes 884740
  265.3 5.8 %copy-start.5 = (f32[2,192,192]{2,1,0:T(8,128)S(1)}, f32[2,192,192]{2,1,0:T(8,128)}, u32[]{:S(2)}) copy-start(f32[2,192,192]{2,1,0:T(8,128)} %get-tuple-element.50) | copy-start | bytes 884740
  267.4 4.5 %copy-start.3 = (f32[2,192,384]{2,1,0:T(8,128)S(1)}, f32[2,192,384]{2,1,0:T(8,128)}, u32[]{:S(2)}) copy-start(f32[2,192,384]{2,1,0:T(8,128)} %get-tuple-element.26) | copy-start | bytes 1769476
  269.5 3.1 %copy-start.2 = (f32[2,192,1024]{2,1,0:T(8,128)S(1)}, f32[2,192,1024]{2,1,0:T(8,128)}, u32[]{:S(2)}) copy-start(f32[2,192,1024]{2,1,0:T(8,128)} %get-tuple-element.52) | copy-start | bytes 4718596
  271.9 2.0 copy-start.1
  273.8 2.0 copy-start
